TPU v7x, 32 devices: a whole 2x2x4 slice. The times are simulated.
32 devices in a mesh: pipe: 2 (over core), dp: 4 (over y, x), tensor: 4 (over z).
Axes of the slice: x: 2, y: 2, z: 4, core: 2. Of those that a mesh axis runs over, the one named last changes fastest.
Arguments:
- images: bfloat16 [4, 32, 196, 512], P(None, ('dp', 'tensor')), may hold values from -6 to 6
- cotangent: bfloat16 [4, 32, 196, 512], P(None, ('dp', 'tensor')), may hold values from -6 to 6
- counts: int32 [4, 4], P(None, 'dp'), may hold values from 4 to 8, as said below
- rel_index: int32 [49, 49], replicated, may hold values from 0 to 168, as said below
- pre_attn_gain: bfloat16 [2, 512], P('pipe', 'tensor'), may hold values from 0.25 to 1.75
- pre_attn_bias: bfloat16 [2, 512], P('pipe', 'tensor'), may hold values from -3 to 3
- qkv_weight: bfloat16 [2, 512, 1536], P('pipe', None, 'tensor'), may hold values from -0.25 to 0.25
- qv_bias: bfloat16 [2, 1024], P('pipe', 'tensor'), may hold values from -3 to 3
- bias_table: bfloat16 [2, 16, 169], P('pipe', 'tensor'), may hold values from -3 to 256
- proj_weight: bfloat16 [2, 512, 512], P('pipe', 'tensor'), may hold values from -0.75 to 0.75
- proj_bias: bfloat16 [2, 512], P('pipe', 'tensor'), may hold values from -3 to 3
- pre_mlp_gain: bfloat16 [2, 512], P('pipe', 'tensor'), may hold values from 0.25 to 1.75
- pre_mlp_bias: bfloat16 [2, 512], P('pipe', 'tensor'), may hold values from -3 to 3
- hidden_weight: bfloat16 [2, 512, 2048], P('pipe', None, 'tensor'), may hold values from -0.25 to 0.25
- hidden_bias: bfloat16 [2, 2048], P('pipe', 'tensor'), may hold values from -3 to 3
- out_weight: bfloat16 [2, 2048, 512], P('pipe', 'tensor'), may hold values from -0.125 to 0.125
- out_bias: bfloat16 [2, 512], P('pipe', 'tensor'), may hold values from -3 to 3
Outputs:
- block_out: bfloat16 [2, 4, 32, 196, 512], P('pipe', None, ('dp', 'tensor'))
- input_grad: bfloat16 [2, 4, 32, 196, 512], P('pipe', None, ('dp', 'tensor'))
- pre_attn_gain_grad: float32 [2, 512], P('pipe', 'tensor')
- pre_attn_bias_grad: float32 [2, 512], P('pipe', 'tensor')
- qkv_weight_grad: float32 [2, 512, 1536], P('pipe', None, 'tensor')
- qv_bias_grad: float32 [2, 1024], P('pipe', 'tensor')
- bias_table_grad: float32 [2, 16, 169], P('pipe', 'tensor')
- proj_weight_grad: float32 [2, 512, 512], P('pipe', 'tensor')
- proj_bias_grad: float32 [2, 512], P('pipe', 'tensor')
- pre_mlp_gain_grad: float32 [2, 512], P('pipe', 'tensor')
- pre_mlp_bias_grad: float32 [2, 512], P('pipe', 'tensor')
- hidden_weight_grad: float32 [2, 512, 2048], P('pipe', None, 'tensor')
- hidden_bias_grad: float32 [2, 2048], P('pipe', 'tensor')
- out_weight_grad: float32 [2, 2048, 512], P('pipe', 'tensor')
- out_bias_grad: float32 [2, 512], P('pipe', 'tensor')
Inputs may be any that keep to these rules, and one draw needn't show every extreme that they name: Slots 0 to counts - 1 of a data shard's 8 slots hold images; both ends are reached in every draw. rel_index[a, b] depends only on the offset between positions a and b of a window; distinct offsets have distinct entries.
All inputs are finite; a program needn't handle non-finite values.
Results may differ from a plain program's by a relative error of at most 0.023.
Values may be sent and summed in bfloat16 or wider, within the bound.
A program may use at most 320 MiB of HBM per device.

v0:
```python
import math

import jax
import jax.numpy as jnp
from jax import lax
from jax.sharding import PartitionSpec as P

D = 512
H = 16
HD = 32
WIN = 7
GRID = 14
SHIFT = 3
TOK = 196
RELS = 169


EPSILON = 1e-05
MASK_VALUE = -100.0


def from_behind(block, axis, distance):
    devices = range(lax.axis_size(axis))
    route = [(i - distance, i) for i in devices if i - distance in devices]
    return lax.ppermute(block, axis, route)


def cyclic(tensor, offset, which_dim):
    length = tensor.shape[which_dim]
    doubled = jnp.concatenate([tensor, tensor], which_dim)
    return lax.dynamic_slice_in_dim(doubled, offset, length, which_dim)


def to_windows(tensor, offset):
    count_img = tensor.shape[0]
    channels = tensor.shape[-1]
    per_side = GRID // WIN
    grid_view = tensor.reshape(count_img, GRID, GRID, channels)
    grid_view = cyclic(cyclic(grid_view, offset, 1), offset, 2)
    grid_view = grid_view.reshape(count_img, per_side, WIN, per_side, WIN, channels).transpose(
        0, 1, 3, 2, 4, 5
    )
    return grid_view.reshape(count_img * per_side * per_side, WIN * WIN, channels)


def from_windows(windows, offset, count_img):
    channels = windows.shape[-1]
    per_side = GRID // WIN
    grid_view = windows.reshape(count_img, per_side, per_side, WIN, WIN, channels).transpose(
        0, 1, 3, 2, 4, 5
    )
    grid_view = grid_view.reshape(count_img, GRID, GRID, channels)
    grid_view = cyclic(cyclic(grid_view, GRID - offset, 1), GRID - offset, 2)
    return grid_view.reshape(count_img, GRID * GRID, channels)


def region_labels():
    span = jnp.arange(TOK, dtype=jnp.int32)
    row_band = (span // GRID >= GRID - WIN).astype(jnp.int32) + (
        span // GRID >= GRID - SHIFT
    ).astype(jnp.int32)
    col_band = (span % GRID >= GRID - WIN).astype(jnp.int32) + (span % GRID >= GRID - SHIFT).astype(
        jnp.int32
    )
    return row_band * 3 + col_band


def bias_and_mask(table, onehot, mask_on):
    flat_bias = jnp.dot(table.astype(jnp.float32), onehot.T, precision=lax.Precision.HIGHEST)
    position = flat_bias.reshape(H, WIN * WIN, WIN * WIN)
    labels = to_windows(region_labels().reshape(1, TOK, 1), 0)[:, :, 0]
    differ = (labels[:, :, None] != labels[:, None, :]).astype(jnp.float32)
    return position[None, :, :, :] + MASK_VALUE * mask_on * differ[:, None, :, :]


def norm_rows(resid, gain, shift_term):
    center = resid - jnp.mean(resid, -1, keepdims=True)
    inverse = lax.rsqrt(jnp.mean(center * center, -1, keepdims=True) + EPSILON)
    normed = center * inverse
    return (normed * gain.astype(jnp.float32) + shift_term.astype(jnp.float32), normed, inverse)


def norm_back(grad_out, normed, inverse, gain):
    scaled = grad_out * gain.astype(jnp.float32)
    grad_in = inverse * (
        scaled
        - jnp.mean(scaled, -1, keepdims=True)
        - normed * jnp.mean(scaled * normed, -1, keepdims=True)
    )
    return (grad_in, jnp.sum(grad_out * normed, (0, 1)), jnp.sum(grad_out, (0, 1)))


def gelu_slope(inputs):
    cdf_part = 0.5 * (1.0 + lax.erf(inputs * 0.5**0.5))
    pdf_part = jnp.exp(-0.5 * inputs * inputs) * (2.0 * math.pi) ** (-0.5)
    return cdf_part + inputs * pdf_part


def batched(spec, left, right):
    return jnp.einsum(spec, left, right, preferred_element_type=jnp.float32)


def matmul(left, right):
    return jnp.dot(left, right, preferred_element_type=jnp.float32)


def layer_parts(params, layer_in, alive, offset, bias_mask):
    (
        attn_gain,
        attn_shift,
        qkv_w,
        qv_terms_in,
        table_unused,
        proj_w,
        proj_b,
        mlp_gain,
        mlp_shift,
        hidden_w,
        hidden_b,
        out_w,
        out_b,
    ) = params
    count_img = layer_in.shape[0]
    query_scale = HD ** (-0.5)
    resid = layer_in.astype(jnp.float32)
    first_in, normed_a, inverse_a = norm_rows(resid, attn_gain, attn_shift)
    windows = to_windows(first_in.astype(jnp.bfloat16), offset)
    count_win = windows.shape[0]
    projected = matmul(windows.reshape(-1, D), qkv_w).reshape(count_win, WIN * WIN, H, 3, HD)
    qv_terms = qv_terms_in.astype(jnp.float32).reshape(H, 2, HD)
    queries = ((projected[:, :, :, 0] + qv_terms[:, 0]) * query_scale).astype(jnp.bfloat16)
    keys_w = projected[:, :, :, 1].astype(jnp.bfloat16)
    values = (projected[:, :, :, 2] + qv_terms[:, 1]).astype(jnp.bfloat16)
    scores = batched("bqhe,bkhe->bhqk", queries, keys_w)
    scores = scores.reshape(count_img, -1, H, WIN * WIN, WIN * WIN) + bias_mask[None]
    scores = scores.reshape(count_win, H, WIN * WIN, WIN * WIN)
    top_score = jnp.max(scores, -1, keepdims=True)
    exp_scores = jnp.exp(scores - top_score)
    attn_probs = exp_scores / jnp.sum(exp_scores, -1, keepdims=True)
    probs_bf = attn_probs.astype(jnp.bfloat16)
    mixed_heads = batched("bhqk,bkhe->bqhe", probs_bf, values).astype(jnp.bfloat16)
    heads_out = from_windows(mixed_heads.reshape(count_win, WIN * WIN, D), offset, count_img)
    attended = matmul(heads_out.reshape(-1, D), proj_w).reshape(resid.shape) + proj_b.astype(
        jnp.float32
    )
    middle = resid + attended
    second_in, normed_m, inverse_m = norm_rows(middle, mlp_gain, mlp_shift)
    second_bf = second_in.astype(jnp.bfloat16).reshape(-1, D)
    hidden_pre = matmul(second_bf, hidden_w) + hidden_b.astype(jnp.float32)
    activ_bf = jax.nn.gelu(hidden_pre, approximate=False).astype(jnp.bfloat16)
    mlp_out = matmul(activ_bf, out_w).reshape(resid.shape) + out_b.astype(jnp.float32)
    result = ((middle + mlp_out) * alive).astype(jnp.bfloat16)
    kept_state = (
        normed_a,
        inverse_a,
        windows,
        queries,
        keys_w,
        values,
        attn_probs,
        probs_bf,
        heads_out,
        normed_m,
        inverse_m,
        second_bf,
        hidden_pre,
        activ_bf,
    )
    return (result, kept_state)


def layer_back(params, kept_state, cotan, alive, offset, onehot):
    (
        attn_gain,
        attn_shift,
        qkv_w,
        qv_terms_in,
        table_unused,
        proj_w,
        proj_b,
        mlp_gain,
        mlp_shift,
        hidden_w,
        hidden_b,
        out_w,
        out_b,
    ) = params
    (
        normed_a,
        inverse_a,
        windows,
        queries,
        keys_w,
        values,
        attn_probs,
        probs_bf,
        heads_out,
        normed_m,
        inverse_m,
        second_bf,
        hidden_pre,
        activ_bf,
    ) = kept_state
    count_img = cotan.shape[0]
    count_win = windows.shape[0]
    query_scale = HD ** (-0.5)
    grad_rows = (cotan.astype(jnp.float32) * alive).reshape(-1, D)
    grad_rows_bf = grad_rows.astype(jnp.bfloat16)
    out_w_grad = matmul(activ_bf.T, grad_rows_bf)
    out_b_grad = jnp.sum(grad_rows, 0)
    grad_pre = matmul(grad_rows_bf, out_w.T) * gelu_slope(hidden_pre)
    grad_pre_bf = grad_pre.astype(jnp.bfloat16)
    hidden_w_grad = matmul(second_bf.T, grad_pre_bf)
    hidden_b_grad = jnp.sum(grad_pre, 0)
    grad_second = matmul(grad_pre_bf, hidden_w.T).reshape(count_img, TOK, D)
    grad_norm_m, mlp_gain_grad, mlp_shift_grad = norm_back(
        grad_second, normed_m, inverse_m, mlp_gain
    )
    grad_middle = grad_rows.reshape(count_img, TOK, D) + grad_norm_m
    middle_rows = grad_middle.reshape(-1, D)
    middle_bf = middle_rows.astype(jnp.bfloat16)
    proj_w_grad = matmul(heads_out.reshape(-1, D).T, middle_bf)
    proj_b_grad = jnp.sum(middle_rows, 0)
    grad_heads = matmul(middle_bf, proj_w.T).astype(jnp.bfloat16).reshape(count_img, TOK, D)
    grad_win = to_windows(grad_heads, offset).reshape(count_win, WIN * WIN, H, HD)
    grad_probs = batched("bqhe,bkhe->bhqk", grad_win, values)
    grad_values = batched("bhqk,bqhe->bkhe", probs_bf, grad_win)
    grad_scores = attn_probs * (grad_probs - jnp.sum(grad_probs * attn_probs, -1, keepdims=True))
    table_grad = jnp.dot(
        jnp.sum(grad_scores, 0).reshape(H, -1), onehot, precision=lax.Precision.HIGHEST
    )
    scores_bf = grad_scores.astype(jnp.bfloat16)
    grad_queries = batched("bhqk,bkhe->bqhe", scores_bf, keys_w) * query_scale
    grad_keys = batched("bhqk,bqhe->bkhe", scores_bf, queries)
    qv_grad = jnp.stack([jnp.sum(grad_queries, (0, 1)), jnp.sum(grad_values, (0, 1))], 1).reshape(
        -1
    )
    grad_proj = (
        jnp.stack([grad_queries, grad_keys, grad_values], 3).astype(jnp.bfloat16).reshape(-1, 3 * D)
    )
    qkv_w_grad = matmul(windows.reshape(-1, D).T, grad_proj)
    grad_first = from_windows(
        matmul(grad_proj, qkv_w.T).reshape(count_win, WIN * WIN, D), offset, count_img
    )
    grad_norm_a, attn_gain_grad, attn_shift_grad = norm_back(
        grad_first, normed_a, inverse_a, attn_gain
    )
    grad_in = (grad_middle + grad_norm_a).astype(jnp.bfloat16)
    return (
        grad_in,
        (
            attn_gain_grad,
            attn_shift_grad,
            qkv_w_grad,
            qv_grad,
            table_grad,
            proj_w_grad,
            proj_b_grad,
            mlp_gain_grad,
            mlp_shift_grad,
            hidden_w_grad,
            hidden_b_grad,
            out_w_grad,
            out_b_grad,
        ),
    )


def local(
    images,
    cotangent,
    counts,
    rel_index,
    pre_attn_gain,
    pre_attn_bias,
    qkv_weight,
    qv_bias,
    bias_table,
    proj_weight,
    proj_bias,
    pre_mlp_gain,
    pre_mlp_bias,
    hidden_weight,
    hidden_bias,
    out_weight,
    out_bias,
):
    section_idx = lax.axis_index("pipe")
    mask_on = (section_idx == 1).astype(jnp.float32)
    offset = section_idx * SHIFT
    params = (
        lax.all_gather(pre_attn_gain[0], "tensor", axis=0, tiled=True),
        lax.all_gather(pre_attn_bias[0], "tensor", axis=0, tiled=True),
        lax.all_gather(qkv_weight[0], "tensor", axis=1, tiled=True),
        lax.all_gather(qv_bias[0], "tensor", axis=0, tiled=True),
        lax.all_gather(bias_table[0], "tensor", axis=0, tiled=True),
        lax.all_gather(proj_weight[0], "tensor", axis=0, tiled=True),
        lax.all_gather(proj_bias[0], "tensor", axis=0, tiled=True),
        lax.all_gather(pre_mlp_gain[0], "tensor", axis=0, tiled=True),
        lax.all_gather(pre_mlp_bias[0], "tensor", axis=0, tiled=True),
        lax.all_gather(hidden_weight[0], "tensor", axis=1, tiled=True),
        lax.all_gather(hidden_bias[0], "tensor", axis=0, tiled=True),
        lax.all_gather(out_weight[0], "tensor", axis=0, tiled=True),
        lax.all_gather(out_bias[0], "tensor", axis=0, tiled=True),
    )
    onehot = (rel_index.reshape(-1)[:, None] == jnp.arange(RELS, dtype=jnp.int32)[None, :]).astype(
        jnp.float32
    )
    bias_mask = bias_and_mask(params[4], onehot, mask_on)
    batches = images.shape[0]
    per_device = images.shape[1]
    slot_ids = lax.axis_index("tensor") * per_device + jnp.arange(per_device, dtype=jnp.int32)
    alive_all = (slot_ids[None, :] < counts).astype(jnp.float32)
    incoming = jnp.zeros(images.shape[1:], jnp.bfloat16)
    saved_inputs = []
    saved_alive = []
    tick_outputs = []
    for tick_num in range(batches + 1):
        own_input = images[min(tick_num, batches - 1)]
        layer_in = jnp.where(section_idx == 0, own_input, incoming)
        alive_here = jnp.where(
            section_idx == 0, alive_all[min(tick_num, batches - 1)], alive_all[max(tick_num - 1, 0)]
        )[:, None, None]
        result, unused_state = layer_parts(params, layer_in, alive_here, offset, bias_mask)
        saved_inputs.append(layer_in)
        saved_alive.append(alive_here)
        tick_outputs.append(result)
        if tick_num < batches:
            incoming = from_behind(result, "pipe", 1)
    totals = tuple(
        (
            jnp.zeros(member.shape[1:], jnp.float32)
            for member in (
                pre_attn_gain,
                pre_attn_bias,
                qkv_weight,
                qv_bias,
                bias_table,
                proj_weight,
                proj_bias,
                pre_mlp_gain,
                pre_mlp_bias,
                hidden_weight,
                hidden_bias,
                out_weight,
                out_bias,
            )
        )
    )
    incoming = jnp.zeros(images.shape[1:], jnp.bfloat16)
    tick_grads = []
    for step_num in range(batches + 1):
        forward_tick = batches - step_num
        own_cot = (
            cotangent[batches - 1 - step_num] if step_num < batches else jnp.zeros_like(incoming)
        )
        layer_cot = jnp.where(section_idx == 1, own_cot, incoming)
        result, kept_state = layer_parts(
            params, saved_inputs[forward_tick], saved_alive[forward_tick], offset, bias_mask
        )
        grad_in, terms = layer_back(
            params, kept_state, layer_cot, saved_alive[forward_tick], offset, onehot
        )
        terms = (
            lax.psum_scatter(
                terms[0].astype(jnp.bfloat16), "tensor", scatter_dimension=0, tiled=True
            ).astype(jnp.float32),
            lax.psum_scatter(
                terms[1].astype(jnp.bfloat16), "tensor", scatter_dimension=0, tiled=True
            ).astype(jnp.float32),
            lax.psum_scatter(
                terms[2].astype(jnp.bfloat16), "tensor", scatter_dimension=1, tiled=True
            ).astype(jnp.float32),
            lax.psum_scatter(
                terms[3].astype(jnp.bfloat16), "tensor", scatter_dimension=0, tiled=True
            ).astype(jnp.float32),
            lax.psum_scatter(
                terms[4].astype(jnp.bfloat16), "tensor", scatter_dimension=0, tiled=True
            ).astype(jnp.float32),
            lax.psum_scatter(
                terms[5].astype(jnp.bfloat16), "tensor", scatter_dimension=0, tiled=True
            ).astype(jnp.float32),
            lax.psum_scatter(
                terms[6].astype(jnp.bfloat16), "tensor", scatter_dimension=0, tiled=True
            ).astype(jnp.float32),
            lax.psum_scatter(
                terms[7].astype(jnp.bfloat16), "tensor", scatter_dimension=0, tiled=True
            ).astype(jnp.float32),
            lax.psum_scatter(
                terms[8].astype(jnp.bfloat16), "tensor", scatter_dimension=0, tiled=True
            ).astype(jnp.float32),
            lax.psum_scatter(
                terms[9].astype(jnp.bfloat16), "tensor", scatter_dimension=1, tiled=True
            ).astype(jnp.float32),
            lax.psum_scatter(
                terms[10].astype(jnp.bfloat16), "tensor", scatter_dimension=0, tiled=True
            ).astype(jnp.float32),
            lax.psum_scatter(
                terms[11].astype(jnp.bfloat16), "tensor", scatter_dimension=0, tiled=True
            ).astype(jnp.float32),
            lax.psum_scatter(
                terms[12].astype(jnp.bfloat16), "tensor", scatter_dimension=0, tiled=True
            ).astype(jnp.float32),
        )
        totals = tuple((total + term for total, term in zip(totals, terms)))
        tick_grads.append(grad_in)
        if step_num < batches:
            incoming = from_behind(grad_in, "pipe", -1)
    summed = (
        lax.psum(totals[0].astype(jnp.bfloat16), "dp").astype(jnp.float32),
        lax.psum(totals[1].astype(jnp.bfloat16), "dp").astype(jnp.float32),
        lax.psum(totals[2].astype(jnp.bfloat16), "dp").astype(jnp.float32),
        lax.psum(totals[3].astype(jnp.bfloat16), "dp").astype(jnp.float32),
        lax.psum(totals[4].astype(jnp.bfloat16), "dp").astype(jnp.float32),
        lax.psum(totals[5].astype(jnp.bfloat16), "dp").astype(jnp.float32),
        lax.psum(totals[6].astype(jnp.bfloat16), "dp").astype(jnp.float32),
        lax.psum(totals[7].astype(jnp.bfloat16), "dp").astype(jnp.float32),
        lax.psum(totals[8].astype(jnp.bfloat16), "dp").astype(jnp.float32),
        lax.psum(totals[9].astype(jnp.bfloat16), "dp").astype(jnp.float32),
        lax.psum(totals[10].astype(jnp.bfloat16), "dp").astype(jnp.float32),
        lax.psum(totals[11].astype(jnp.bfloat16), "dp").astype(jnp.float32),
        lax.psum(totals[12].astype(jnp.bfloat16), "dp").astype(jnp.float32),
    )
    block_out = jnp.stack(
        [
            jnp.where(section_idx == 0, tick_outputs[batch_idx], tick_outputs[batch_idx + 1])
            for batch_idx in range(batches)
        ]
    )[None]
    input_grad = jnp.stack(
        [
            jnp.where(
                section_idx == 0,
                tick_grads[batches - batch_idx],
                tick_grads[batches - 1 - batch_idx],
            )
            for batch_idx in range(batches)
        ]
    )[None]
    return (
        block_out,
        input_grad,
        summed[0][None],
        summed[1][None],
        summed[2][None],
        summed[3][None],
        summed[4][None],
        summed[5][None],
        summed[6][None],
        summed[7][None],
        summed[8][None],
        summed[9][None],
        summed[10][None],
        summed[11][None],
        summed[12][None],
    )


def solution(mesh):
    return jax.shard_map(
        local,
        mesh=mesh,
        in_specs=(
            P(None, ("dp", "tensor"), None, None),
            P(None, ("dp", "tensor"), None, None),
            P(None, "dp"),
            P(),
            P("pipe", "tensor"),
            P("pipe", "tensor"),
            P("pipe", None, "tensor"),
            P("pipe", "tensor"),
            P("pipe", "tensor", None),
            P("pipe", "tensor", None),
            P("pipe", "tensor"),
            P("pipe", "tensor"),
            P("pipe", "tensor"),
            P("pipe", None, "tensor"),
            P("pipe", "tensor"),
            P("pipe", "tensor", None),
            P("pipe", "tensor"),
        ),
        out_specs=(
            P("pipe", None, ("dp", "tensor"), None, None),
            P("pipe", None, ("dp", "tensor"), None, None),
            P("pipe", "tensor"),
            P("pipe", "tensor"),
            P("pipe", None, "tensor"),
            P("pipe", "tensor"),
            P("pipe", "tensor", None),
            P("pipe", "tensor", None),
            P("pipe", "tensor"),
            P("pipe", "tensor"),
            P("pipe", "tensor"),
            P("pipe", None, "tensor"),
            P("pipe", "tensor"),
            P("pipe", "tensor", None),
            P("pipe", "tensor"),
        ),
        check_vma=False,
    )
```

profile of v0, /device:TPU:0, one launch (start us, length us, event | category | flops | bytes accessed | tf_op | source)
XLA Modules:
  0.0 1510.7 jit_solution(10497966131542343977)
XLA Ops:
  14.3 12.8 all-gather
  27.1 7.9 all-gather.1
  35.0 10.0 all-gather.6
  45.6 7.6 all-gather.7
  53.2 9.7 all-gather.8
  62.9 8.0 all-gather.12
  70.8 11.1 all-gather.3
  82.0 12.6 all-gather.10
  95.3 13.3 all-gather.4
  110.5 18.6 %all-gather.5 = bf16[1,512,512]{2,1,0:T(8,128)(2,1)S(1)} all-gather(bf16[1,128,512]{2,1,0:T(8,128)(2,1)S(1)} %copy-done.115), channel_id=7, replica_groups=mesh['pipe'=2,'dp'=4,'tensor'=4] {'tensor'}, dimensions={1}, use_global_device_ids=true | all-gather | bytes 655360 | tf_op jit(solution)/shard_map/all_gather | solution.py:297
  165.1 10.6 fusion.7
  219.0 10.1 fusion.10
  273.5 10.1 fusion.13
  328.4 10.1 fusion.16
  371.8 6.0 fusion.159
  390.5 9.9 fusion.19
  420.0 6.3 bitcast_reduce_fusion.8
  441.2 10.8 copy.832
  452.0 11.3 reshape.968
  520.9 10.8 copy.833
  531.7 11.1 reshape.969
  556.9 5.5 fusion.519
  596.2 10.8 copy.834
  606.9 10.0 reshape.970
  669.3 10.8 copy.835
  680.1 10.1 reshape.971
  717.7 7.2 copy.775
  734.9 7.2 copy.777
  752.1 7.2 copy.779
  770.3 7.2 copy.781
  777.5 5.5 convert_element_type.1213
  792.4 6.0 bitcast_reduce_fusion
  813.2 5.7 convert_element_type.1216
  901.1 8.6 copy.836
  911.8 9.9 reshape.972
  938.7 35.8 %reduce-scatter.51.cloned.1.call-done = bf16[512,512]{1,0:T(8,128)(2,1)} async-done(((bf16[2048,512]{1,0:T(8,128)(2,1)}), bf16[512,512]{1,0:T(8,128)(2,1)}) %reduce-scatter.51.cloned.1.call-update) | async-done | bytes 524304 | tf_op jit(solution)/shard_map/reduce_scatter | solution.py:398
  974.5 45.0 %reduce-scatter.53.cloned.1.call-done = bf16[512,512]{1,0:T(8,128)(2,1)} async-done(((bf16[2048,512]{1,0:T(8,128)(2,1)}), bf16[512,512]{1,0:T(8,128)(2,1)}) %reduce-scatter.53.cloned.1.call-update) | async-done | bytes 524304 | tf_op jit(solution)/shard_map/reduce_scatter | solution.py:398
  1019.5 45.0 %reduce-scatter.55.cloned.1.call-done = bf16[512,512]{1,0:T(8,128)(2,1)} async-done(((bf16[2048,512]{1,0:T(8,128)(2,1)}), bf16[512,512]{1,0:T(8,128)(2,1)}) %reduce-scatter.55.cloned.1.call-update) | async-done | bytes 524304 | tf_op jit(solution)/shard_map/reduce_scatter | solution.py:398
  1064.5 45.0 %reduce-scatter.57.cloned.1.call-done = bf16[512,512]{1,0:T(8,128)(2,1)} async-done(((bf16[2048,512]{1,0:T(8,128)(2,1)}), bf16[512,512]{1,0:T(8,128)(2,1)}) %reduce-scatter.57.cloned.1.call-update) | async-done | bytes 524304 | tf_op jit(solution)/shard_map/reduce_scatter | solution.py:398
  1109.5 45.0 %reduce-scatter.59.cloned.1.call-done = bf16[512,512]{1,0:T(8,128)(2,1)} async-done(((bf16[2048,512]{1,0:T(8,128)(2,1)}), bf16[512,512]{1,0:T(8,128)(2,1)}) %reduce-scatter.59.cloned.1.call-update) | async-done | bytes 524304 | tf_op jit(solution)/shard_map/reduce_scatter | solution.py:398
  1157.3 42.3 %reduce-scatter.41.cloned.1.call-done = bf16[512,512]{1,0:T(8,128)(2,1)} async-done(((bf16[512,2048]{1,0:T(8,128)(2,1)}), bf16[512,512]{1,0:T(8,128)(2,1)}) %reduce-scatter.41.cloned.1.call-update) | async-done | bytes 524304 | tf_op jit(solution)/shard_map/reduce_scatter | solution.py:392
  1199.6 45.0 %reduce-scatter.43.cloned.1.call-done = bf16[512,512]{1,0:T(8,128)(2,1)} async-done(((bf16[512,2048]{1,0:T(8,128)(2,1)}), bf16[512,512]{1,0:T(8,128)(2,1)}) %reduce-scatter.43.cloned.1.call-update) | async-done | bytes 524304 | tf_op jit(solution)/shard_map/reduce_scatter | solution.py:392
  1244.6 45.2 %reduce-scatter.45.cloned.1.call-done = bf16[512,512]{1,0:T(8,128)(2,1)} async-done(((bf16[512,2048]{1,0:T(8,128)(2,1)}), bf16[512,512]{1,0:T(8,128)(2,1)}) %reduce-scatter.45.cloned.1.call-update) | async-done | bytes 524304 | tf_op jit(solution)/shard_map/reduce_scatter | solution.py:392
  1289.8 45.1 %reduce-scatter.47.cloned.1.call-done = bf16[512,512]{1,0:T(8,128)(2,1)} async-done(((bf16[512,2048]{1,0:T(8,128)(2,1)}), bf16[512,512]{1,0:T(8,128)(2,1)}) %reduce-scatter.47.cloned.1.call-update) | async-done | bytes 524304 | tf_op jit(solution)/shard_map/reduce_scatter | solution.py:392
  1334.9 45.2 %reduce-scatter.49.cloned.1.call-done = bf16[512,512]{1,0:T(8,128)(2,1)} async-done(((bf16[512,2048]{1,0:T(8,128)(2,1)}), bf16[512,512]{1,0:T(8,128)(2,1)}) %reduce-scatter.49.cloned.1.call-update) | async-done | bytes 524304 | tf_op jit(solution)/shard_map/reduce_scatter | solution.py:392
  1391.8 39.5 %all-reduce.51.cloned.1.call-done = (bf16[512]{0:T(512)(128)(2,1)}, bf16[512]{0:T(512)(128)(2,1)}, bf16[512]{0:T(512)(128)(2,1)}, bf16[512]{0:T(512)(128)(2,1)},...) async-done(((bf16[512]{0:T(512)(128)(2,1)}, ...) | async-done | bytes 88496
  1436.0 10.2 all-reduce.46
  1451.1 45.7 %all-reduce.53.cloned.1.call-done = (bf16[1,512,384]{2,1,0:T(8,128)(2,1)}, bf16[1,128,512]{2,1,0:T(8,128)(2,1)}, bf16[1,512,512]{2,1,0:T(8,128)(2,1)}, bf16[1,512,512]{2,1,0:T(8,128)(2,1)}) async-done(((bf16[1,512,384]{2,1,0:T(8,128)(2,1)}, bf16[1,128,512]{2,1,0:T(8,128)(2,1)}, bf16[1,512,512]{2,1,0:T(8,128)(2,1)}, bf16[1,512,512]{2,1,0:T(8,128)(2,1)}), (bf16[1,512,384]{2,1,0:T(8,128)(2,1)}, ...) | async-done | bytes 1572880 | tf_op jit(solution)/shard_map/psum | solution.py:412
  (968 shorter events, 625.5 us)
Async XLA Ops:
  7.2 126.8 %all-gather.17.cloned.1.call-start = ((), (), s32[]{:S(2)}) async-start(), calls=%async_computation.35 | async-start | bytes 1966080 | tf_op jit(solution)/shard_map/all_gather | solution.py:294
  8.0 87.1 %copy-start.146 = (s32[49,49]{1,0:T(8,128)S(1)}, s32[49,49]{1,0:T(8,128)}, u32[]{:S(2)}) copy-start(s32[49,49]{1,0:T(8,128)} %param.20) | copy-start | bytes 28816
  8.0 157.0 %all-gather.19.cloned.1.call-start = ((), (), s32[]{:S(2)}) async-start(), calls=%async_computation.36 | async-start | bytes 2621440 | tf_op jit(solution)/shard_map/all_gather | solution.py:301
  8.8 166.9 %all-gather.21.cloned.1.call-start = ((), (), s32[]{:S(2)}) async-start(), calls=%async_computation.37 | async-start | bytes 2621440 | tf_op jit(solution)/shard_map/all_gather | solution.py:303
  9.5 919.9 %reduce-scatter.31.cloned.1.call-start = ((), (), s32[]{:S(2)}) async-start(), calls=%async_computation.20 | async-start | bytes 655360 | tf_op jit(solution)/shard_map/reduce_scatter | solution.py:380
  9.6 100.9 %copy-start.115 = (bf16[1,128,512]{2,1,0:T(8,128)(2,1)S(1)}, bf16[1,128,512]{2,1,0:T(8,128)(2,1)}, u32[]{:S(2)}) copy-start(bf16[1,128,512]{2,1,0:T(8,128)(2,1)} %param.26) | copy-start | bytes 393220
  13.0 97.2 %copy-start.32 = (bf16[1,2,196,512]{3,1,2,0:T(2,128)(2,1)}, bf16[1,2,196,512]{3,1,2,0:T(2,128)(2,1)S(1)}, u32[]{:S(2)}) copy-start(bf16[1,2,196,512]{3,1,2,0:T(2,128)(2,1)S(1)} %get-tuple-element.255) | copy-start | bytes 1204228
  13.2 117.0 %copy-start.142 = (f32[2,196]{1,0:T(2,128)}, f32[2,196]{1,0:T(2,128)S(1)}, u32[]{:S(2)}) copy-start(f32[2,196]{1,0:T(2,128)S(1)} %broadcast_multiply_fusion.29) | copy-start | bytes 4708
  13.7 95.7 %copy-start.153 = (f32[4,2]{1,0:T(4,128)}, f32[4,2]{1,0:T(4,128)S(1)}, u32[]{:S(2)}) copy-start(f32[4,2]{1,0:T(4,128)S(1)} %compare_convert_fusion) | copy-start | bytes 100
  62.9 262.7 %copy-start.116 = (f32[1,512]{1,0:T(1,128)}, f32[1,512]{1,0:T(1,128)S(1)}, u32[]{:S(2)}) copy-start(f32[1,512]{1,0:T(1,128)S(1)} %convert_element_type.1338) | copy-start | bytes 6148
  70.8 272.8 %copy-start.118 = (f32[1,512]{1,0:T(1,128)}, f32[1,512]{1,0:T(1,128)S(1)}, u32[]{:S(2)}) copy-start(f32[1,512]{1,0:T(1,128)S(1)} %convert_element_type.1340) | copy-start | bytes 6148
  183.2 2.7 collective-permute-start
  184.5 104.2 %copy-start.162 = (f32[2]{0:T(128)}, f32[2]{0:T(128)S(1)}, u32[]{:S(2)}) copy-start(f32[2]{0:T(128)S(1)} %get-tuple-element.268) | copy-start | bytes 28
  184.5 159.1 %copy-start.164 = (f32[2]{0:T(128)}, f32[2]{0:T(128)S(1)}, u32[]{:S(2)}) copy-start(f32[2]{0:T(128)S(1)} %get-tuple-element.267) | copy-start | bytes 28
  236.6 3.5 collective-permute-start.1
  291.3 3.7 collective-permute-start.2
  346.3 9.2 collective-permute-start.3
  473.4 3.9 collective-permute-start.4
  477.2 452.2 %reduce-scatter.33.cloned.1.call-start = ((), (), s32[]{:S(2)}) async-start(), calls=%async_computation.21 | async-start | bytes 655360 | tf_op jit(solution)/shard_map/reduce_scatter | solution.py:380
  551.1 4.8 collective-permute-start.5
  554.9 374.5 %reduce-scatter.35.cloned.1.call-start = ((), (), s32[]{:S(2)}) async-start(), calls=%async_computation.22 | async-start | bytes 655360 | tf_op jit(solution)/shard_map/reduce_scatter | solution.py:380
  625.4 4.0 collective-permute-start.6
  629.3 300.1 %reduce-scatter.37.cloned.1.call-start = ((), (), s32[]{:S(2)}) async-start(), calls=%async_computation.23 | async-start | bytes 655360 | tf_op jit(solution)/shard_map/reduce_scatter | solution.py:380
  698.5 4.9 collective-permute-start.7
  703.4 226.1 %reduce-scatter.39.cloned.1.call-start = ((), (), s32[]{:S(2)}) async-start(), calls=%async_computation.24 | async-start | bytes 655360 | tf_op jit(solution)/shard_map/reduce_scatter | solution.py:380
  717.0 214.4 %reduce-scatter.61.cloned.1.call-start = ((), (), s32[]{:S(2)}) async-start(), calls=%async_computation.38 | async-start | bytes 1966080
  734.6 198.1 %reduce-scatter.63.cloned.1.call-start = ((), (), s32[]{:S(2)}) async-start(), calls=%async_computation.39 | async-start | bytes 1966080
  751.7 182.2 %reduce-scatter.65.cloned.1.call-start = ((), (), s32[]{:S(2)}) async-start(), calls=%async_computation.40 | async-start | bytes 1966080
  768.9 166.2 %reduce-scatter.67.cloned.1.call-start = ((), (), s32[]{:S(2)}) async-start(), calls=%async_computation.41 | async-start | bytes 1966080
  787.1 149.2 %reduce-scatter.69.cloned.1.call-start = ((), (), s32[]{:S(2)}) async-start(), calls=%async_computation.42 | async-start | bytes 1966080
  825.1 149.4 %reduce-scatter.51.cloned.1.call-start = ((), (), s32[]{:S(2)}) async-start(), calls=%async_computation.30 | async-start | bytes 2621440 | tf_op jit(solution)/shard_map/reduce_scatter | solution.py:398
  829.7 189.8 %reduce-scatter.53.cloned.1.call-start = ((), (), s32[]{:S(2)}) async-start(), calls=%async_computation.31 | async-start | bytes 2621440 | tf_op jit(solution)/shard_map/reduce_scatter | solution.py:398
  833.8 230.6 %reduce-scatter.55.cloned.1.call-start = ((), (), s32[]{:S(2)}) async-start(), calls=%async_computation.32 | async-start | bytes 2621440 | tf_op jit(solution)/shard_map/reduce_scatter | solution.py:398
  838.1 271.4 %reduce-scatter.57.cloned.1.call-start = ((), (), s32[]{:S(2)}) async-start(), calls=%async_computation.33 | async-start | bytes 2621440 | tf_op jit(solution)/shard_map/reduce_scatter | solution.py:398
  842.2 312.3 %reduce-scatter.59.cloned.1.call-start = ((), (), s32[]{:S(2)}) async-start(), calls=%async_computation.34 | async-start | bytes 2621440 | tf_op jit(solution)/shard_map/reduce_scatter | solution.py:398
  846.4 353.3 %reduce-scatter.41.cloned.1.call-start = ((), (), s32[]{:S(2)}) async-start(), calls=%async_computation.25 | async-start | bytes 2621440 | tf_op jit(solution)/shard_map/reduce_scatter | solution.py:392
  850.7 394.0 %reduce-scatter.43.cloned.1.call-start = ((), (), s32[]{:S(2)}) async-start(), calls=%async_computation.26 | async-start | bytes 2621440 | tf_op jit(solution)/shard_map/reduce_scatter | solution.py:392
  854.8 435.0 %reduce-scatter.45.cloned.1.call-start = ((), (), s32[]{:S(2)}) async-start(), calls=%async_computation.27 | async-start | bytes 2621440 | tf_op jit(solution)/shard_map/reduce_scatter | solution.py:392
  859.1 475.8 %reduce-scatter.47.cloned.1.call-start = ((), (), s32[]{:S(2)}) async-start(), calls=%async_computation.28 | async-start | bytes 2621440 | tf_op jit(solution)/shard_map/reduce_scatter | solution.py:392
  863.5 516.6 %reduce-scatter.49.cloned.1.call-start = ((), (), s32[]{:S(2)}) async-start(), calls=%async_computation.29 | async-start | bytes 2621440 | tf_op jit(solution)/shard_map/reduce_scatter | solution.py:392
  867.8 563.5 %all-reduce.51.cloned.1.call-start = ((), (), s32[]{:S(2)}) async-start(), calls=%async_computation.43 | async-start | bytes 204800
  929.1 567.8 %all-reduce.53.cloned.1.call-start = ((), (), s32[]{:S(2)}) async-start(), calls=%async_computation.44 | async-start | bytes 3145728 | tf_op jit(solution)/shard_map/psum | solution.py:412
  938.7 444.2 %copy-start.5 = (f32[2,196,512]{2,1,0:T(8,128)S(1)}, f32[2,196,512]{2,1,0:T(8,128)}, u32[]{:S(2)}) copy-start(f32[2,196,512]{2,1,0:T(8,128)} %copy-done.4) | copy-start | bytes 2408452
  938.7 444.2 %copy-start.64 = (f32[2,196,512]{2,1,0:T(8,128)S(1)}, f32[2,196,512]{2,1,0:T(8,128)}, u32[]{:S(2)}) copy-start(f32[2,196,512]{2,1,0:T(8,128)} %reshape.896) | copy-start | bytes 2408452
  938.7 444.3 %copy-start.119 = (f32[1,512]{1,0:T(1,128)S(1)}, f32[1,512]{1,0:T(1,128)}, u32[]{:S(2)}) copy-start(f32[1,512]{1,0:T(1,128)} %copy-done.118) | copy-start | bytes 6148
  938.7 444.3 %copy-start.157 = (f32[2]{0:T(128)S(1)}, f32[2]{0:T(128)}, u32[]{:S(2)}) copy-start(f32[2]{0:T(128)} %get-tuple-element.265) | copy-start | bytes 28
  1157.3 227.0 %copy-start.65 = (bf16[1,2,196,512]{3,2,1,0:T(8,128)(2,1)S(1)}, bf16[1,2,196,512]{3,2,1,0:T(8,128)(2,1)}, u32[]{:S(2)}) copy-start(bf16[1,2,196,512]{3,2,1,0:T(8,128)(2,1)} %get-tuple-element.224) | copy-start | bytes 1204228
  1157.3 227.0 %copy-start.66 = (bf16[1,2,196,512]{3,2,1,0:T(8,128)(2,1)S(1)}, bf16[1,2,196,512]{3,2,1,0:T(8,128)(2,1)}, u32[]{:S(2)}) copy-start(bf16[1,2,196,512]{3,2,1,0:T(8,128)(2,1)} %get-tuple-element.226) | copy-start | bytes 1204228
  (197 other events, 1480.8 us)
Sparse Core Ops, SparseCore 0:
  9.6 39.4 all-gather.16
  50.6 45.8 all-gather.18
  98.0 48.2 all-gather.20
  477.3 21.0 reduce-scatter.30
  555.0 21.9 reduce-scatter.32
  629.4 21.0 reduce-scatter.34
  703.5 20.9 reduce-scatter.36
  727.4 20.1 reduce-scatter.38
  749.9 33.7 reduce-scatter.60
  785.8 34.2 reduce-scatter.62
  822.4 34.2 reduce-scatter.64
  858.9 34.2 reduce-scatter.66
  895.5 34.2 reduce-scatter.68
  932.0 42.4 reduce-scatter.50
  976.6 42.8 reduce-scatter.52
  1021.6 42.8 reduce-scatter.54
  1066.6 42.8 reduce-scatter.56
  1111.6 42.8 reduce-scatter.58
  1156.8 42.8 reduce-scatter.40
  1201.8 42.8 reduce-scatter.42
  1246.9 42.8 reduce-scatter.44
  1292.1 42.8 reduce-scatter.46
  1337.2 42.8 reduce-scatter.48
  1387.2 44.0 all-reduce.50
  1435.2 61.5 all-reduce.52
where the time goes:
time: 1520 us; the launch traced here: 1510 us
  waiting for transfers between devices  531 us (35%)
  local copies, waits for them, and re-layouts  346 us (23%)
  matrix products  318 us (21%)
  other arithmetic  156 us (10%)
  blocking collectives  122 us (8%)
  between operations  20.9 us (1%)
  starting transfers between devices  17.3 us (1%)
    reduce_scatter x5, waiting for transfers between devices, local(): lax.psum_scatter(terms[9].astype(jnp.bfloat16), 'tensor', scatter_dimensi...  223 us
    reduce_scatter x5, waiting for transfers between devices, local(): lax.psum_scatter(terms[11].astype(jnp.bfloat16), 'tensor', scatter_dimens...  216 us
    dot_general x60, matrix products, matmul(): return jnp.dot(left, right, preferred_element_type=jnp.float32)  202 us
    convert_element_type x20, local copies, waits for them, and re-layouts, layer_back(): jnp.stack([grad_queries, grad_keys, grad_values], 3).astype(jnp.bfloat16)  166 us
    dot_general x30, matrix products, batched(): return jnp.einsum(spec, left, right, preferred_element_type=jnp.float32)  109 us
    psum x1, waiting for transfers between devices, local(): lax.psum(totals[2].astype(jnp.bfloat16), 'dp').astype(jnp.float32)  45.7 us
    unnamed x438, local copies, waits for them, and re-layouts  43.6 us
    unnamed x31, waiting for transfers between devices  42 us
  transfers between devices with their start and end apart: 33, of which 17 were waited for; matrix products, arithmetic and copies ran while one was open for 35% of the time, Pallas kernels for 0%

commit v1 on v0

v1 whole, which is shorter than its diff:
```python
import functools
import math

import jax
import jax.numpy as jnp
from jax import lax
from jax.experimental import pallas as pl
from jax.experimental.pallas import tpu as pltpu
from jax.sharding import PartitionSpec as P

D = 512
H = 16
HD = 32
WIN = 7
GRID = 14
SHIFT = 3
TOK = 196
RELS = 169
POS = WIN * WIN
NW = 4
WP = 64
TP = 208
ROWS = NW * WP
GH = 4
GL = GH * HD
EPSILON = 1e-05
MASK_VALUE = -100.0
F32 = jnp.float32
BF = jnp.bfloat16


def dot_nn(a, b):
    return lax.dot_general(a, b, (((1,), (0,)), ((), ())), preferred_element_type=F32)


def dot_nt(a, b):
    return lax.dot_general(a, b, (((1,), (1,)), ((), ())), preferred_element_type=F32)


def dot_tn(a, b):
    return lax.dot_general(a, b, (((0,), (0,)), ((), ())), preferred_element_type=F32)


def normalize(rows):
    center = rows - jnp.mean(rows, -1, keepdims=True)
    inverse = lax.rsqrt(jnp.mean(center * center, -1, keepdims=True) + EPSILON)
    return center * inverse, inverse


def norm_back(grad_out, normed, inverse, gain):
    scaled = grad_out * gain
    return inverse * (
        scaled
        - jnp.mean(scaled, -1, keepdims=True)
        - normed * jnp.mean(scaled * normed, -1, keepdims=True)
    )


def block_diagonal(rows, head_mask):
    return jnp.concatenate([rows] * GH, axis=0) * head_mask


def pick_diagonal(full):
    head = lax.broadcasted_iota(jnp.int32, (WP, GL), 1) // HD
    out = full[0:WP]
    for h in range(1, GH):
        out = jnp.where(head == h, full[h * WP : (h + 1) * WP], out)
    return out


def attn_fwd_body(
    x_ref, gain_ref, shift_ref, spread_ref, gather_ref, head_mask_ref, wqkv_ref, qkv_scale_ref, qkv_shift_ref,
    bias_ref, wproj_ref, bproj_ref, fw_ref, qkv_ref, p_ref, ho_ref, mid_ref, how_ref,
):
    x = x_ref[0].astype(F32)
    normed, _ = normalize(x)
    first = (normed * gain_ref[...] + shift_ref[...]).astype(BF)
    fw = dot_nn(spread_ref[...], first).astype(BF)
    fw_ref[0] = fw
    for g in range(4):
        projected = dot_nn(fw, wqkv_ref[g])
        qkv_ref[0, g] = (projected * qkv_scale_ref[...] + qkv_shift_ref[g]).astype(BF)

    def window(w, carry):
        rows = pl.ds(pl.multiple_of(w * WP, WP), WP)
        for g in range(4):
            q = qkv_ref[0, g, rows, 0:GL]
            k = qkv_ref[0, g, rows, GL : 2 * GL]
            v = qkv_ref[0, g, rows, 2 * GL : 3 * GL]
            st = dot_nt(k, block_diagonal(q, head_mask_ref[...])) + bias_ref[w, g]
            e = jnp.exp(st - jnp.max(st, 0, keepdims=True))
            pt = (e * (1.0 / jnp.sum(e, 0, keepdims=True))).astype(BF)
            p_ref[0, w, g] = pt
            how_ref[rows, g * GL : (g + 1) * GL] = pick_diagonal(dot_tn(pt, v)).astype(BF)
        return carry

    lax.fori_loop(0, NW, window, 0)
    ho = dot_nn(gather_ref[...], how_ref[...]).astype(BF)
    ho_ref[0] = ho
    mid_ref[0] = x + (dot_nn(ho, wproj_ref[...]) + bproj_ref[...])


def whole(shape):
    return pl.BlockSpec(shape, lambda i: (0,) * len(shape))


def per(shape):
    return pl.BlockSpec((1,) + shape, lambda i: (i,) + (0,) * len(shape))


def attn_fwd(x, gain, shift, spread, gather, head_mask, wqkv, qkv_scale, qkv_shift, bias, wproj, bproj):
    n = x.shape[0]
    return pl.pallas_call(
        attn_fwd_body,
        grid=(n,),
        in_specs=[
            per((TP, D)), whole((1, D)), whole((1, D)), whole((ROWS, TP)), whole((TP, ROWS)), whole((GH * WP, GL)),
            whole((4, D, 3 * GL)), whole((1, 3 * GL)), whole((4, 1, 3 * GL)), whole((NW, 4, WP, GH * WP)),
            whole((D, D)), whole((1, D)),
        ],
        out_specs=[per((ROWS, D)), per((4, ROWS, 3 * GL)), per((NW, 4, WP, GH * WP)), per((TP, D)), per((TP, D))],
        out_shape=[
            jax.ShapeDtypeStruct((n, ROWS, D), BF),
            jax.ShapeDtypeStruct((n, 4, ROWS, 3 * GL), BF),
            jax.ShapeDtypeStruct((n, NW, 4, WP, GH * WP), BF),
            jax.ShapeDtypeStruct((n, TP, D), BF),
            jax.ShapeDtypeStruct((n, TP, D), F32),
        ],
        scratch_shapes=[pltpu.VMEM((ROWS, D), BF)],
        name="attn_fwd",
        compiler_params=pltpu.CompilerParams(vmem_limit_bytes=48 << 20),
        cost_estimate=pl.CostEstimate(flops=n * 2 * 256 * 512 * 2600, bytes_accessed=n * 2 << 20, transcendentals=0),
    )(x, gain, shift, spread, gather, head_mask, wqkv, qkv_scale, qkv_shift, bias, wproj, bproj)


def gelu_parts(v):
    cdf = 0.5 * (1.0 + lax.erf(v * 0.5**0.5))
    pdf = jnp.exp(-0.5 * v * v) * (2.0 * math.pi) ** (-0.5)
    return v * cdf, cdf + v * pdf


BLK = 416


def mlp_fwd_body(mid_ref, gain_ref, shift_ref, hw_ref, hb_ref, ow_ref, ob_ref, alive_ref, second_ref, act_ref, slope_ref, y_ref, acc_ref):
    c = pl.program_id(0)
    rows_total = mid_ref.shape[0]

    @pl.when(c == 0)
    def _():
        mid = mid_ref[...]
        normed, _ = normalize(mid)
        second_ref[...] = (normed * gain_ref[...] + shift_ref[...]).astype(BF)
        acc_ref[...] = mid + ob_ref[...]

    def block(b, carry):
        rows = pl.ds(pl.multiple_of(b * BLK, BLK), BLK)
        pre = dot_nn(second_ref[rows, :], hw_ref[0]) + hb_ref[0]
        act, slope = gelu_parts(pre)
        act = act.astype(BF)
        act_ref[0, rows, :] = act
        slope_ref[0, rows, :] = slope.astype(BF)
        acc_ref[rows, :] += dot_nn(act, ow_ref[0])
        return carry

    lax.fori_loop(0, rows_total // BLK, block, 0)

    @pl.when(c == pl.num_programs(0) - 1)
    def _():
        y_ref[...] = (acc_ref[...] * alive_ref[...]).astype(BF)


def mlp_fwd(mid, gain, shift, hw, hb, ow, ob, alive):
    r = mid.shape[0]
    nc, _, fc = hw.shape
    return pl.pallas_call(
        mlp_fwd_body,
        grid=(nc,),
        in_specs=[
            whole((r, D)), whole((1, D)), whole((1, D)), per((D, fc)), per((1, fc)), per((fc, D)), whole((1, D)), whole((r, 1)),
        ],
        out_specs=[whole((r, D)), per((r, fc)), per((r, fc)), whole((r, D))],
        out_shape=[
            jax.ShapeDtypeStruct((r, D), BF),
            jax.ShapeDtypeStruct((nc, r, fc), BF),
            jax.ShapeDtypeStruct((nc, r, fc), BF),
            jax.ShapeDtypeStruct((r, D), BF),
        ],
        scratch_shapes=[pltpu.VMEM((r, D), F32)],
        name="mlp_fwd",
        compiler_params=pltpu.CompilerParams(vmem_limit_bytes=48 << 20),
        cost_estimate=pl.CostEstimate(flops=4 * r * D * 2048, bytes_accessed=12 << 20, transcendentals=0),
    )(mid, gain, shift, hw, hb, ow, ob, alive)


def mlp_bwd_body(
    g_ref, alive_ref, act_ref, slope_ref, hw_ref, ow_ref, second_ref, mid_ref, gain_ref,
    ghw_ref, gow_ref, ghb_ref, gmid_ref, small_ref, gy_ref, gyt_ref, sect_ref, gp_ref, acc_ref,
):
    c = pl.program_id(0)
    rows_total = mid_ref.shape[0]

    @pl.when(c == 0)
    def _():
        gy = g_ref[...].astype(F32) * alive_ref[...]
        small_ref[0:1] = jnp.sum(gy, 0, keepdims=True)
        gy = gy.astype(BF)
        gy_ref[...] = gy
        gyt_ref[...] = gy.T
        sect_ref[...] = second_ref[...].T
        acc_ref[...] = jnp.zeros_like(acc_ref)

    ghb_ref[0] = jnp.zeros_like(ghb_ref[0])

    def block(b, carry):
        rows = pl.ds(pl.multiple_of(b * BLK, BLK), BLK)
        gp = dot_nt(gy_ref[rows, :], ow_ref[0]) * slope_ref[0, rows, :].astype(F32)
        ghb_ref[0] += jnp.sum(gp, 0, keepdims=True)
        gp = gp.astype(BF)
        gp_ref[rows, :] = gp
        acc_ref[rows, :] += dot_nt(gp, hw_ref[0])
        return carry

    lax.fori_loop(0, rows_total // BLK, block, 0)
    ghw_ref[0] = dot_nn(sect_ref[...], gp_ref[...]).astype(BF)
    gow_ref[0] = dot_nn(gyt_ref[...], act_ref[0]).astype(BF)

    @pl.when(c == pl.num_programs(0) - 1)
    def _():
        e = acc_ref[...]
        normed, inverse = normalize(mid_ref[...])
        small_ref[2:3] = jnp.sum(e * normed, 0, keepdims=True)
        small_ref[3:4] = jnp.sum(e, 0, keepdims=True)
        gmid = gy_ref[...].astype(F32) + norm_back(e, normed, inverse, gain_ref[...])
        small_ref[1:2] = jnp.sum(gmid, 0, keepdims=True)
        gmid_ref[...] = gmid


def mlp_bwd(g, alive, act, slope, hw, ow, second, mid, gain):
    r = mid.shape[0]
    nc, _, fc = hw.shape
    return pl.pallas_call(
        mlp_bwd_body,
        grid=(nc,),
        in_specs=[
            whole((r, D)), whole((r, 1)), per((r, fc)), per((r, fc)), per((D, fc)), per((fc, D)), whole((r, D)), whole((r, D)), whole((1, D)),
        ],
        out_specs=[per((D, fc)), per((D, fc)), per((1, fc)), whole((r, D)), whole((4, D))],
        out_shape=[
            jax.ShapeDtypeStruct((nc, D, fc), BF),
            jax.ShapeDtypeStruct((nc, D, fc), BF),
            jax.ShapeDtypeStruct((nc, 1, fc), F32),
            jax.ShapeDtypeStruct((r, D), F32),
            jax.ShapeDtypeStruct((4, D), F32),
        ],
        scratch_shapes=[
            pltpu.VMEM((r, D), BF), pltpu.VMEM((D, r), BF), pltpu.VMEM((D, r), BF), pltpu.VMEM((r, fc), BF), pltpu.VMEM((r, D), F32),
        ],
        name="mlp_bwd",
        compiler_params=pltpu.CompilerParams(vmem_limit_bytes=48 << 20),
        cost_estimate=pl.CostEstimate(flops=8 * r * D * 2048, bytes_accessed=16 << 20, transcendentals=0),
    )(g, alive, act, slope, hw, ow, second, mid, gain)


def attn_bwd_body(
    x_ref, gmid_ref, fw_ref, qkv_ref, p_ref, ho_ref, gain_ref, spread_ref, gather_ref, head_mask_ref, wqkv_ref, wproj_ref,
    gin_ref, gqkv_ref, gproj_ref, gqv_ref, gtab_ref, small_ref, gw_ref, dq_ref, fwt_ref, hot_ref, gmb_ref,
):
    i = pl.program_id(0)
    last = pl.num_programs(0) - 1

    @pl.when(i == 0)
    def _():
        gqv_ref[...] = jnp.zeros_like(gqv_ref)
        gtab_ref[...] = jnp.zeros_like(gtab_ref)
        small_ref[...] = jnp.zeros_like(small_ref)

    gmid = gmid_ref[0]
    gmb = gmid.astype(BF)
    gmb_ref[i] = gmb
    heads = dot_nt(gmb, wproj_ref[...]).astype(BF)
    gw_ref[...] = dot_nn(spread_ref[...], heads).astype(BF)
    base = pl.multiple_of(i * ROWS, ROWS)
    fwt_ref[:, pl.ds(base, ROWS)] = fw_ref[0].T
    scale = HD ** (-0.5)

    def window(w, carry):
        rows = pl.ds(pl.multiple_of(w * WP, WP), WP)
        out_rows = pl.ds(pl.multiple_of(base + w * WP, WP), WP)
        for g in range(4):
            q = qkv_ref[0, g, rows, 0:GL]
            k = qkv_ref[0, g, rows, GL : 2 * GL]
            v = qkv_ref[0, g, rows, 2 * GL : 3 * GL]
            pt = p_ref[0, w, g]
            head_mask = head_mask_ref[...]
            bd_grad = block_diagonal(gw_ref[rows, g * GL : (g + 1) * GL], head_mask)
            ptf = pt.astype(F32)
            t = dot_nt(v, bd_grad)
            pd = t * ptf
            ds = pd - ptf * jnp.sum(pd, 0, keepdims=True)
            gtab_ref[g] += ds
            dsb = ds.astype(BF)
            dv = dot_nn(pt, bd_grad)
            dk = dot_nn(dsb, block_diagonal(q, head_mask))
            dq = pick_diagonal(dot_tn(dsb, k)) * scale
            gqv_ref[g, 0:1] += jnp.sum(dq, 0, keepdims=True)
            gqv_ref[g, 1:2] += jnp.sum(dv, 0, keepdims=True)
            dq_ref[g, out_rows, 0:GL] = dq.astype(BF)
            dq_ref[g, out_rows, GL : 2 * GL] = dk.astype(BF)
            dq_ref[g, out_rows, 2 * GL : 3 * GL] = dv.astype(BF)
        return carry

    lax.fori_loop(0, NW, window, 0)
    image_rows = pl.ds(base, ROWS)
    e = dot_nt(dq_ref[0, image_rows, :], wqkv_ref[0])
    for g in range(1, 4):
        e += dot_nt(dq_ref[g, image_rows, :], wqkv_ref[g])
    e = dot_nn(gather_ref[...], e.astype(BF))
    normed, inverse = normalize(x_ref[0].astype(F32))
    small_ref[0:1] += jnp.sum(e * normed, 0, keepdims=True)
    small_ref[1:2] += jnp.sum(e, 0, keepdims=True)
    gin_ref[0] = (gmid + norm_back(e, normed, inverse, gain_ref[...])).astype(BF)

    hot_ref[i] = ho_ref[0].T

    @pl.when(i == last)
    def _():
        for g in range(4):
            gqkv_ref[g] = dot_nn(fwt_ref[...], dq_ref[g]).astype(BF)
        acc = dot_nn(hot_ref[0], gmb_ref[0])
        for b in range(1, hot_ref.shape[0]):
            acc += dot_nn(hot_ref[b], gmb_ref[b])
        gproj_ref[...] = acc.astype(BF)


def attn_bwd(x, gmid, fw, qkv, p, ho, gain, spread, gather, head_mask, wqkv, wproj):
    n = x.shape[0]
    return pl.pallas_call(
        attn_bwd_body,
        grid=(n,),
        in_specs=[
            per((TP, D)), per((TP, D)), per((ROWS, D)), per((4, ROWS, 3 * GL)), per((NW, 4, WP, GH * WP)), per((TP, D)),
            whole((1, D)), whole((ROWS, TP)), whole((TP, ROWS)), whole((GH * WP, GL)), whole((4, D, 3 * GL)), whole((D, D)),
        ],
        out_specs=[
            per((TP, D)), whole((4, D, 3 * GL)), whole((D, D)), whole((4, 2, GL)), whole((4, WP, GH * WP)), whole((2, D)),
        ],
        out_shape=[
            jax.ShapeDtypeStruct((n, TP, D), BF),
            jax.ShapeDtypeStruct((4, D, 3 * GL), BF),
            jax.ShapeDtypeStruct((D, D), BF),
            jax.ShapeDtypeStruct((4, 2, GL), F32),
            jax.ShapeDtypeStruct((4, WP, GH * WP), F32),
            jax.ShapeDtypeStruct((2, D), F32),
        ],
        scratch_shapes=[
            pltpu.VMEM((ROWS, D), BF), pltpu.VMEM((4, n * ROWS, 3 * GL), BF), pltpu.VMEM((D, n * ROWS), BF),
            pltpu.VMEM((n, D, TP), BF), pltpu.VMEM((n, TP, D), BF),
        ],
        name="attn_bwd",
        compiler_params=pltpu.CompilerParams(vmem_limit_bytes=48 << 20),
        cost_estimate=pl.CostEstimate(flops=n * 4 * 256 * 512 * 2600, bytes_accessed=n * 3 << 20, transcendentals=0),
    )(x, gmid, fw, qkv, p, ho, gain, spread, gather, head_mask, wqkv, wproj)


def window_maps(offset):
    token = jnp.arange(TP, dtype=jnp.int32)
    r = (token // GRID - offset) % GRID
    c = (token % GRID - offset) % GRID
    slot = ((r // WIN) * 2 + c // WIN) * WP + (r % WIN) * WIN + c % WIN
    slot = jnp.where(token < TOK, slot, -1)
    spread = (jnp.arange(ROWS, dtype=jnp.int32)[:, None] == slot[None, :]).astype(BF)
    return spread, spread.T


def region_differs():
    w = jnp.arange(NW, dtype=jnp.int32)
    a = jnp.arange(WP, dtype=jnp.int32)
    r = (w // 2)[:, None] * WIN + (a // WIN)[None, :]
    c = (w % 2)[:, None] * WIN + (a % WIN)[None, :]

    def band(t):
        return (t >= GRID - WIN).astype(jnp.int32) + (t >= GRID - SHIFT).astype(jnp.int32)

    label = band(r) * 3 + band(c)
    return (label[:, :, None] != label[:, None, :]).astype(F32)


def bias_tables(table, rel_index, masked):
    rel = jnp.pad(rel_index.T, ((0, WP - POS), (0, WP - POS)), constant_values=-1).reshape(-1)
    onehot = (jnp.arange(RELS, dtype=jnp.int32)[:, None] == rel[None, :]).astype(BF)
    flat = jnp.dot(table, onehot, preferred_element_type=F32)
    position = flat.reshape(4, GH, WP, WP).transpose(0, 2, 1, 3)
    key_pad = jnp.where(jnp.arange(WP) < POS, 0.0, -1e30).astype(F32)[:, None]
    extra = key_pad + (MASK_VALUE * region_differs() if masked else jnp.zeros((NW, WP, WP), F32))
    return (position[None] + extra[:, None, :, None, :]).reshape(NW, 4, WP, GH * WP)


def table_grad(gtab, rel_index):
    rel = jnp.pad(rel_index.T, ((0, WP - POS), (0, WP - POS)), constant_values=-1).reshape(-1)
    onehot = (rel[:, None] == jnp.arange(RELS, dtype=jnp.int32)[None, :]).astype(F32)
    flat = gtab.reshape(4, WP, GH, WP).transpose(0, 2, 1, 3).reshape(H, WP * WP)
    return jnp.dot(flat, onehot, precision=lax.Precision.HIGHEST)


def qkv_order(w):
    lead = w.shape[:-1]
    return jnp.swapaxes(w.reshape(*lead, GH, 3, HD), -3, -2).reshape(*lead, 3 * GL)


def head_masks():
    row = jnp.arange(GH * WP, dtype=jnp.int32) // WP
    lane = jnp.arange(GL, dtype=jnp.int32) // HD
    return (row[:, None] == lane[None, :]).astype(BF)


def rows_of(vector):
    return vector.astype(F32).reshape(1, -1)


SMALL = ("gain", "shift", "qv", "table", "bproj", "mgain", "mshift", "hb", "ob")


def pack_small(parts):
    return jnp.concatenate([part.reshape(-1) for part in parts])


def unpack_small(packed, shapes):
    out, at = [], 0
    for shape in shapes:
        size = math.prod(shape)
        piece = packed[:, at : at + size]
        out.append(piece.reshape((piece.shape[0] * shape[0],) + tuple(shape[1:])))
        at += size
    return out


def qkv_terms(qv):
    qv = qv.astype(F32).reshape(4, GH, 2, HD)
    shift = jnp.concatenate(
        [
            qv[:, :, 0].reshape(4, 1, GL) * HD ** (-0.5),
            jnp.zeros((4, 1, GL), F32),
            qv[:, :, 1].reshape(4, 1, GL),
        ],
        2,
    )
    scale = jnp.concatenate([jnp.full((1, GL), HD ** (-0.5), F32), jnp.ones((1, 2 * GL), F32)], 1)
    return scale, shift


def qkv_unorder(w):
    lead = w.shape[:-1]
    return jnp.swapaxes(w.reshape(*lead, 3, GH, HD), -3, -2).reshape(*lead, 3 * GL)


def layer_forward(x, weights, alive_rows, maps, head_mask):
    count = x.shape[0]
    spread, gather = maps
    fw, qkv, p, ho, mid = attn_fwd(
        x, weights["gain"], weights["shift"], spread, gather, head_mask, weights["wqkv"], weights["qkv_scale"],
        weights["qkv_shift"], weights["bias"], weights["wproj"], weights["bproj"],
    )
    mid = mid.reshape(count * TP, D)
    second, act, slope, y = mlp_fwd(
        mid, weights["mgain"], weights["mshift"], weights["hw"], weights["hb"], weights["ow"], weights["ob"], alive_rows
    )
    return y.reshape(count, TP, D), (x, fw, qkv, p, ho, mid, second, act, slope)


def layer_backward(cot, kept, weights, alive_rows, maps, head_mask):
    x, fw, qkv, p, ho, mid, second, act, slope = kept
    count = x.shape[0]
    ghw, gow, ghb, gmid, small_m = mlp_bwd(
        cot.reshape(count * TP, D), alive_rows, act, slope, weights["hw"], weights["ow"], second, mid, weights["mgain"]
    )
    gin, gqkv, gproj, gqv, gtab, small_a = attn_bwd(
        x, gmid.reshape(count, TP, D), fw, qkv, p, ho, weights["gain"], maps[0], maps[1], head_mask, weights["wqkv"], weights["wproj"]
    )
    return gin, (ghw, gow, gqkv, gproj), (ghb, small_m, gqv, gtab, small_a)


def local(
    images, cotangent, counts, rel_index, pre_attn_gain, pre_attn_bias, qkv_weight, qv_bias, bias_table, proj_weight, proj_bias,
    pre_mlp_gain, pre_mlp_bias, hidden_weight, hidden_bias, out_weight, out_bias,
):
    core = lax.axis_index("pipe")
    first_core = core == 0
    batches, slots = images.shape[:2]
    half = slots // 2

    def own_slots(array):
        mine = lax.dynamic_slice_in_dim(array, core * half, half, 1).reshape(batches * half, TOK, D)
        return jnp.pad(mine, ((0, 0), (0, TP - TOK), (0, 0)))

    x0 = own_slots(images)
    cot = own_slots(cotangent)
    slot_ids = lax.axis_index("tensor") * slots + core * half + jnp.arange(half, dtype=jnp.int32)
    alive = (slot_ids[None, :] < counts).astype(F32).reshape(-1)
    alive_rows = (alive[:, None] * (jnp.arange(TP) < TOK).astype(F32)[None, :]).reshape(-1, 1)

    small_in = (pre_attn_gain, pre_attn_bias, qv_bias, bias_table, proj_bias, pre_mlp_gain, pre_mlp_bias, hidden_bias, out_bias)
    shapes = [member.shape[1:] for member in small_in]
    packed = lax.all_gather(lax.all_gather(pack_small(small_in), "tensor"), "pipe")

    def both(member, axis):
        return lax.all_gather(lax.all_gather(member[0], "tensor", axis=axis, tiled=True), "pipe")

    wqkv2, wproj2, hw2, ow2 = both(qkv_weight, 1), both(proj_weight, 0), both(hidden_weight, 1), both(out_weight, 0)
    layers = []
    for l in range(2):
        small = dict(zip(SMALL, unpack_small(packed[l], shapes)))
        scale, shift = qkv_terms(small["qv"])
        layers.append(
            dict(
                gain=rows_of(small["gain"]), shift=rows_of(small["shift"]), bproj=rows_of(small["bproj"]),
                mgain=rows_of(small["mgain"]), mshift=rows_of(small["mshift"]), ob=rows_of(small["ob"]),
                hb=small["hb"].astype(F32).reshape(4, 1, -1), qkv_scale=scale, qkv_shift=shift,
                bias=bias_tables(small["table"], rel_index, l == 1),
                wqkv=qkv_order(wqkv2[l].reshape(D, 4, 3 * GL).transpose(1, 0, 2)), wproj=wproj2[l],
                hw=hw2[l].reshape(D, 4, -1).transpose(1, 0, 2), ow=ow2[l].reshape(4, -1, D),
            )
        )
    head_mask = head_masks()
    maps = [window_maps(l * SHIFT) for l in range(2)]
    y0, kept0 = layer_forward(x0, layers[0], alive_rows, maps[0], head_mask)
    y1, kept1 = layer_forward(y0, layers[1], alive_rows, maps[1], head_mask)
    g1, big1, little1 = layer_backward(cot, kept1, layers[1], alive_rows, maps[1], head_mask)
    g0, big0, little0 = layer_backward(g1, kept0, layers[0], alive_rows, maps[0], head_mask)

    def assemble(mine0, mine1):
        sent = lax.ppermute(jnp.where(first_core, mine1, mine0), "pipe", [(0, 1), (1, 0)])
        mine = jnp.where(first_core, mine0, mine1)
        mine, sent = (part[:, :TOK].reshape(batches, half, TOK, D) for part in (mine, sent))
        low, high = jnp.where(first_core, mine, sent), jnp.where(first_core, sent, mine)
        return jnp.concatenate([low, high], 1)[None]

    block_out = assemble(y0, y1)
    input_grad = assemble(g0, g1)

    def full(big):
        ghw, gow, gqkv, gproj = big
        return (
            qkv_unorder(gqkv).transpose(1, 0, 2).reshape(D, 3 * D), gproj,
            ghw.transpose(1, 0, 2).reshape(D, -1), gow.transpose(0, 2, 1).reshape(-1, D),
        )

    def reduced(pair, axis):
        mine = lax.psum_scatter(jnp.stack(pair), "pipe", scatter_dimension=0, tiled=False)
        mine = lax.psum_scatter(mine, "tensor", scatter_dimension=axis, tiled=True)
        return lax.psum(mine, "dp").astype(F32)[None]

    gqkv, gproj, ghw, gow = (reduced(pair, axis) for pair, axis in zip(zip(full(big0), full(big1)), (1, 0, 1, 0)))

    def little(terms):
        ghb, small_m, gqv, gtab, small_a = terms
        qv = jnp.swapaxes(gqv.reshape(4, 2, GH, HD), 1, 2).reshape(-1)
        return (
            small_a[0], small_a[1], qv, table_grad(gtab, rel_index), small_m[1], small_m[2], small_m[3], ghb.reshape(-1), small_m[0],
        )

    totals = lax.psum(jnp.stack([pack_small(little(little0)), pack_small(little(little1))]), ("pipe", "dp", "tensor"))
    mine = jnp.where(first_core, totals[0], totals[1])
    shards = lax.axis_size("tensor")
    outs, at = [], 0
    for shape in shapes:
        whole_shape = (shape[0] * shards,) + tuple(shape[1:])
        size = math.prod(whole_shape)
        piece = mine[at : at + size].reshape(whole_shape)
        outs.append(lax.dynamic_slice_in_dim(piece, lax.axis_index("tensor") * shape[0], shape[0], 0)[None])
        at += size
    gain_g, shift_g, qv_g, table_g, bproj_g, mgain_g, mshift_g, hb_g, ob_g = outs
    return (
        block_out, input_grad, gain_g, shift_g, gqkv, qv_g, table_g, gproj, bproj_g, mgain_g, mshift_g, ghw, hb_g, gow, ob_g,
    )


def solution(mesh):
    return jax.shard_map(
        local,
        mesh=mesh,
        in_specs=(
            P(None, ("dp", "tensor"), None, None),
            P(None, ("dp", "tensor"), None, None),
            P(None, "dp"),
            P(),
            P("pipe", "tensor"),
            P("pipe", "tensor"),
            P("pipe", None, "tensor"),
            P("pipe", "tensor"),
            P("pipe", "tensor", None),
            P("pipe", "tensor", None),
            P("pipe", "tensor"),
            P("pipe", "tensor"),
            P("pipe", "tensor"),
            P("pipe", None, "tensor"),
            P("pipe", "tensor"),
            P("pipe", "tensor", None),
            P("pipe", "tensor"),
        ),
        out_specs=(
            P("pipe", None, ("dp", "tensor"), None, None),
            P("pipe", None, ("dp", "tensor"), None, None),
            P("pipe", "tensor"),
            P("pipe", "tensor"),
            P("pipe", None, "tensor"),
            P("pipe", "tensor"),
            P("pipe", "tensor", None),
            P("pipe", "tensor", None),
            P("pipe", "tensor"),
            P("pipe", "tensor"),
            P("pipe", "tensor"),
            P("pipe", None, "tensor"),
            P("pipe", "tensor"),
            P("pipe", "tensor", None),
            P("pipe", "tensor"),
        ),
        check_vma=False,
    )
```

time: 1520 us -> 815 us (0.54)
  matrix products: 318 us -> 8.22 us
  local copies, waits for them, and re-layouts: 346 us -> 137 us
  Pallas kernels: 0 us -> 145 us
  other arithmetic: 156 us -> 33.8 us
  waiting for transfers between devices: 531 us -> 422 us
  blocking collectives: 122 us -> 42.3 us
  starting transfers between devices: 17.3 us -> 1.44 us
    reduce_scatter x15 -> x7, waiting for transfers between devices: 439 us -> 115 us  [the longest x3 110 us: reduced(): mine = lax.psum_scatter(mine, 'tensor', scatter_dimension=axis, tiled=True)]
    dot_general x96 -> x4, matrix products: 318 us -> 8.22 us  [the longest x2 4.75 us: table_grad(): return jnp.dot(flat, onehot, precision=lax.Precision.HIGHEST)]
    convert_element_type x45 -> x4, local copies, waits for them, and re-layouts: 194 us -> 0.19 us  [the longest x2 0.17 us: qkv_terms(): qv = qv.astype(F32).reshape(4, GH, 2, HD)]
    pallas_call x0 -> x8, Pallas kernels: none -> 145 us  [the longest x2 57.5 us: attn_bwd(): pl.pallas_call(attn_bwd_body, grid=(n,), in_specs=[per((TP, D)), per((TP,...]
    psum x1 -> x2, waiting for transfers between devices: 45.7 us -> 177 us  [the longest x1 125 us: local(): lax.psum(jnp.stack([pack_small(little(little0)), pack_small(little(little...]
    all_gather x3 -> x7, waiting for transfers between devices: 0.04 us -> 89.4 us  [the longest x3 82.2 us: both(): lax.all_gather(member[0], 'tensor', axis=axis, tiled=True)]
    all_gather x10 -> x2, blocking collectives: 112 us -> 24.6 us  [the longest x1 22.8 us: both(): lax.all_gather(member[0], 'tensor', axis=axis, tiled=True)]
    reduce_sum x43 -> x0, other arithmetic: 48.9 us -> none  [the longest x10 10.8 us: norm_back(): jnp.sum(grad_out * normed, (0, 1))]
  transfers between devices with their start and end apart: 33 -> 19, of which waited for: 17 -> 11; matrix products, arithmetic and copies ran while one was open for 35% -> 16% of each run, Pallas kernels for 0% -> 2%
where the time goes in v1:
time: 815 us; the launch traced here: 806 us
  waiting for transfers between devices  422 us (52%)
  Pallas kernels  145 us (18%)
  local copies, waits for them, and re-layouts  137 us (17%)
  blocking collectives  42.3 us (5%)
  other arithmetic  33.8 us (4%)
  between operations  16 us (2%)
  matrix products  8.22 us (1%)
    psum x1, waiting for transfers between devices, local(): lax.psum(jnp.stack([pack_small(little(little0)), pack_small(little(little...  125 us
    reduce_scatter x3, waiting for transfers between devices, reduced(): mine = lax.psum_scatter(mine, 'tensor', scatter_dimension=axis, tiled=True)  110 us
    all_gather x3, waiting for transfers between devices, both(): lax.all_gather(member[0], 'tensor', axis=axis, tiled=True)  82.2 us
    pallas_call x2, Pallas kernels, attn_bwd(): pl.pallas_call(attn_bwd_body, grid=(n,), in_specs=[per((TP, D)), per((TP,...  57.5 us
    psum x1, waiting for transfers between devices, reduced(): return lax.psum(mine, 'dp').astype(F32)[None]  52.3 us
    unnamed x18, waiting for transfers between devices  40.3 us
    unnamed x177, local copies, waits for them, and re-layouts  38.4 us
    pallas_call x2, Pallas kernels, attn_fwd(): pl.pallas_call(attn_fwd_body, grid=(n,), in_specs=[per((TP, D)), whole((1...  37 us
  transfers between devices with their start and end apart: 19, of which 11 were waited for; matrix products, arithmetic and copies ran while one was open for 16% of the time, Pallas kernels for 2%

profile of v1, /device:TPU:0, one launch (start us, length us, event | category | flops | bytes accessed | tf_op | source)
XLA Modules:
  0.0 806.1 jit_solution(11024655152369078844)
XLA Ops:
  9.5 22.8 %all-gather.4 = bf16[1,512,512]{2,1,0:T(8,128)(2,1)} all-gather(bf16[1,128,512]{2,1,0:T(8,128)(2,1)} %param.26), channel_id=6, replica_groups=mesh['pipe'=2,'dp'=4,'tensor'=4] {'tensor'}, dimensions={1}, use_global_device_ids=true | all-gather | bytes 655360 | tf_op jit(solution)/shard_map/all_gather | solution.py:507
  32.4 19.2 %all-gather.19.cloned.1.call-done = bf16[1,512,1536]{2,1,0:T(8,128)(2,1)} async-done(((bf16[1,512,384]{2,1,0:T(8,128)(2,1)}), bf16[1,512,1536]{2,1,0:T(8,128)(2,1)}) %all-gather.19.cloned.1.call-update) | async-done | bytes 1572880 | tf_op jit(solution)/shard_map/all_gather | solution.py:507
  51.7 47.3 %all-gather.25.cloned.1.call-done = bf16[1,512,2048]{2,1,0:T(8,128)(2,1)} async-done(((bf16[1,512,512]{2,1,0:T(8,128)(2,1)}), bf16[1,512,2048]{2,1,0:T(8,128)(2,1)}) %all-gather.25.cloned.1.call-update) | async-done | bytes 2097168 | tf_op jit(solution)/shard_map/all_gather | solution.py:507
  101.0 17.7 %all-reduce.3 = bf16[8848]{0:T(1024)(128)(2,1)S(1)} all-reduce(bf16[8848]{0:T(1024)(128)(2,1)S(1)} %dynamic-update-slice), channel_id=2, replica_groups=mesh['pipe'=2,'dp'=4,'tensor'=4] {'tensor'}, use_global_device_ids=true, to_apply=%add.3 | all-reduce | flops 8848 | bytes 35392
  129.9 15.6 %all-gather.29.cloned.1.call-done = bf16[1,2048,512]{2,1,0:T(8,128)(2,1)} async-done(((bf16[1,512,512]{2,1,0:T(8,128)(2,1)}), bf16[1,2048,512]{2,1,0:T(8,128)(2,1)}) %all-gather.29.cloned.1.call-update) | async-done | bytes 2097168 | tf_op jit(solution)/shard_map/all_gather | solution.py:507
  147.5 2.4 add.488
  162.3 7.2 all-gather.21.cloned.1.call-done
  169.5 3.7 fusion.29
  178.6 3.3 copy.80
  181.9 3.0 copy.81
  184.9 2.6 copy.82.wqkv_ref
  193.7 18.5 %attn_fwd.2 = (bf16[4,256,512]{2,1,0:T(8,128)(2,1)S(1)}, bf16[4,4,256,384]{3,2,1,0:T(8,128)(2,1)}, bf16[4,4,4,64,256]{4,3,2,1,0:T(8,128)(2,1)}, bf16[4,208,512]{2,1,0:T(8,128)(2,1)S(1)}, f32[4,208,512]{2,1,0:T(8,128)}) custom-call(bf16[4,208,512]{2,1,0:T(8,128)(2,1)S(1)} %pad.14.x_ref, f32[1,512]{1,0:T(1,128)S(1)} %bitcast.180, f32[1,512]{1,0:T(1,128)S(1)} %bitcast.195, ...), custom_call_target="tpu_custom_call" | custom-call | flops 2726297600 | bytes 8388608 | tf_op jit(solution)/shard_map/attn_fwd/pallas_call | solution.py:113
  214.1 4.1 fusion.28
  218.2 2.5 copy.113
  220.7 2.8 copy.77
  223.5 4.6 copy.114
  228.1 4.1 copy.84
  232.3 4.6 fusion.27
  237.0 10.1 %mlp_fwd.2 = (bf16[832,512]{1,0:T(8,128)(2,1)S(1)}, bf16[4,832,512]{2,1,0:T(8,128)(2,1)}, bf16[4,832,512]{2,1,0:T(8,128)(2,1)}, bf16[832,512]{1,0:T(8,128)(2,1)S(1)}) custom-call(f32[832,512]{1,0:T(8,128)S(1)} %bitcast.196, f32[1,512]{1,0:T(1,128)S(1)} %bitcast.182, f32[1,512]{1,0:T(1,128)S(1)} %bitcast.193, bf16[4,512,512]{2,1,0:T(8,128)(2,1)S(1)} %bitcast.171, ...), custom_call_target="tpu_custom_call" | custom-call | flops 3489660928 | bytes 12582912 | tf_op jit(solution)/shard_map/mlp_fwd/pallas_call | solution.py:176
  248.2 18.5 %attn_fwd.3 = (bf16[4,256,512]{2,1,0:T(8,128)(2,1)S(1)}, bf16[4,4,256,384]{3,2,1,0:T(8,128)(2,1)}, bf16[4,4,4,64,256]{4,3,2,1,0:T(8,128)(2,1)}, bf16[4,208,512]{2,1,0:T(8,128)(2,1)S(1)}, f32[4,208,512]{2,1,0:T(8,128)}) custom-call(bf16[4,208,512]{2,1,0:T(8,128)(2,1)S(1)} %bitcast.164, f32[1,512]{1,0:T(1,128)S(1)} %bitcast.184, f32[1,512]{1,0:T(1,128)S(1)} %bitcast.191, ...), custom_call_target="tpu_custom_call" | custom-call | flops 2726297600 | bytes 8388608 | tf_op jit(solution)/shard_map/attn_fwd/pallas_call | solution.py:113
  270.1 10.0 %mlp_fwd.3 = (bf16[832,512]{1,0:T(8,128)(2,1)S(1)}, bf16[4,832,512]{2,1,0:T(8,128)(2,1)}, bf16[4,832,512]{2,1,0:T(8,128)(2,1)}, bf16[832,512]{1,0:T(8,128)(2,1)S(1)}) custom-call(f32[832,512]{1,0:T(8,128)S(1)} %bitcast.199, f32[1,512]{1,0:T(1,128)S(1)} %bitcast.186, f32[1,512]{1,0:T(1,128)S(1)} %bitcast.189, bf16[4,512,512]{2,1,0:T(8,128)(2,1)S(1)} %bitcast.174, ...), custom_call_target="tpu_custom_call" | custom-call | flops 3489660928 | bytes 12582912 | tf_op jit(solution)/shard_map/mlp_fwd/pallas_call | solution.py:176
  280.1 15.5 %mlp_bwd.2 = (bf16[4,512,512]{2,1,0:T(8,128)(2,1)}, bf16[4,512,512]{2,1,0:T(8,128)(2,1)}, f32[4,1,512]{2,1,0:T(1,128)S(1)}, f32[832,512]{1,0:T(8,128)S(1)}, f32[4,512]{1,0:T(4,128)S(1)}) custom-call(bf16[832,512]{1,0:T(8,128)(2,1)S(1)} %bitcast.175, f32[832,1]{1,0:T(8,128)S(1)} %copy-done.15, bf16[4,832,512]{2,1,0:T(8,128)(2,1)} %get-tuple-element.59.act_ref, ...), custom_call_target="tpu_custom_call" | custom-call | flops 6979321856 | bytes 16777216 | tf_op jit(solution)/shard_map/mlp_bwd/pallas_call | solution.py:242
  296.7 28.6 %attn_bwd.2 = (bf16[4,208,512]{2,1,0:T(8,128)(2,1)S(1)}, bf16[4,512,384]{2,1,0:T(8,128)(2,1)}, bf16[512,512]{1,0:T(8,128)(2,1)S(1)}, f32[4,2,128]{2,1,0:T(2,128)...) custom-call(bf16[4,208,512]{2,1,0:T(8,128)(2,1)S(1)} %bitcast.165, f32[4,208,512]{2,1,0:T(8,128)} %bitcast.201, ...), custom_call_target="tpu_custom_call" | custom-call | flops 5452595200 | bytes 12582912 | tf_op jit(solution)/shard_map/attn_bwd/pallas_call | solution.py:338
  326.3 15.4 %mlp_bwd.3 = (bf16[4,512,512]{2,1,0:T(8,128)(2,1)}, bf16[4,512,512]{2,1,0:T(8,128)(2,1)}, f32[4,1,512]{2,1,0:T(1,128)S(1)}, f32[832,512]{1,0:T(8,128)S(1)}, f32[4,512]{1,0:T(4,128)S(1)}) custom-call(bf16[832,512]{1,0:T(8,128)(2,1)S(1)} %bitcast.170, f32[832,1]{1,0:T(8,128)S(1)} %copy-done.15, bf16[4,832,512]{2,1,0:T(8,128)(2,1)} %get-tuple-element.68.act_ref, ...), custom_call_target="tpu_custom_call" | custom-call | flops 6979321856 | bytes 16777216 | tf_op jit(solution)/shard_map/mlp_bwd/pallas_call | solution.py:242
  342.9 28.9 %attn_bwd.3 = (bf16[4,208,512]{2,1,0:T(8,128)(2,1)S(1)}, bf16[4,512,384]{2,1,0:T(8,128)(2,1)}, bf16[512,512]{1,0:T(8,128)(2,1)S(1)}, f32[4,2,128]{2,1,0:T(2,128)...) custom-call(bf16[4,208,512]{2,1,0:T(8,128)(2,1)S(1)} %copy-done.8, f32[4,208,512]{2,1,0:T(8,128)} %bitcast.198, ...), custom_call_target="tpu_custom_call" | custom-call | flops 5452595200 | bytes 12582912 | tf_op jit(solution)/shard_map/attn_bwd/pallas_call | solution.py:338
  373.3 2.6 copy.95
  375.9 2.7 copy.96
  378.6 2.6 copy.99
  381.2 2.6 copy.97
  383.8 2.7 copy.98
  386.5 2.6 copy.100
  389.1 3.9 pad_maximum_fusion.2
  395.4 4.2 copy.103
  399.6 4.3 copy.104
  403.9 4.9 pad_maximum_fusion.1
  408.8 4.2 copy.101
  413.0 4.2 copy.102
  417.2 4.7 pad_maximum_fusion
  440.1 2.6 copy.110
  443.9 5.2 reduce-scatter.17.cloned.1.call-done
  451.6 125.1 %all-reduce.8.cloned.1.call-done = f32[2,8848]{1,0:T(2,128)} async-done(((f32[2,8848]{1,0:T(2,128)}), f32[2,8848]{1,0:T(2,128)}) %all-reduce.8.cloned.1.call-update) | async-done | bytes 70800 | tf_op jit(solution)/shard_map/psum | solution.py:562
  579.9 37.3 %reduce-scatter.25.cloned.1.call-done = bf16[384,512]{1,0:T(8,128)(2,1)} async-done(((bf16[1536,512]{1,0:T(8,128)(2,1)}), bf16[384,512]{1,0:T(8,128)(2,1)}) %reduce-scatter.25.cloned.1.call-update) | async-done | bytes 393232
  619.1 21.0 %reduce-scatter.15.cloned.1.call-done = bf16[128,512]{1,0:T(8,128)(2,1)} async-done(((bf16[512,512]{1,0:T(8,128)(2,1)}), bf16[128,512]{1,0:T(8,128)(2,1)}) %reduce-scatter.15.cloned.1.call-update) | async-done | bytes 131088 | tf_op jit(solution)/shard_map/reduce_scatter | solution.py:550
  640.0 44.1 %reduce-scatter.23.cloned.1.call-done = bf16[512,512]{1,0:T(8,128)(2,1)} async-done(((bf16[2048,512]{1,0:T(8,128)(2,1)}), bf16[512,512]{1,0:T(8,128)(2,1)}) %reduce-scatter.23.cloned.1.call-update) | async-done | bytes 524304 | tf_op jit(solution)/shard_map/reduce_scatter | solution.py:550
  684.1 45.0 %reduce-scatter.19.cloned.1.call-done = bf16[512,512]{0,1:T(8,128)(2,1)} async-done(((bf16[512,2048]{0,1:T(8,128)(2,1)}), bf16[512,512]{0,1:T(8,128)(2,1)}) %reduce-scatter.19.cloned.1.call-update) | async-done | bytes 524304 | tf_op jit(solution)/shard_map/reduce_scatter | solution.py:550
  733.6 2.8 copy.106
  737.9 2.8 copy.105
  740.7 52.3 %all-reduce.10.cloned.1.call-done = (bf16[1,512,512]{1,2,0:T(8,128)(2,1)}, bf16[1,512,384]{2,1,0:T(8,128)(2,1)}, bf16[1,128,512]{2,1,0:T(8,128)(2,1)}, bf16[1,512,512]{2,1,0:T(8,128)(2,1)}) async-done(((bf16[1,512,512]{1,2,0:T(8,128)(2,1)}, bf16[1,512,384]{2,1,0:T(8,128)(2,1)}, bf16[1,128,512]{2,1,0:T(8,128)(2,1)}, bf16[1,512,512]{2,1,0:T(8,128)(2,1)}), (bf16[1,512,512]{1,2,0:T(8,128)(2,1)}, ...) | async-done | bytes 1572880 | tf_op jit(solution)/shard_map/psum | solution.py:551
  (324 shorter events, 92.8 us)
Async XLA Ops:
  7.2 119.3 %copy-start = (bf16[4,2,196,512]{3,1,2,0:T(2,128)(2,1)S(1)}, bf16[4,2,196,512]{3,1,2,0:T(2,128)(2,1)}, u32[]{:S(2)}) copy-start(bf16[4,2,196,512]{3,1,2,0:T(2,128)(2,1)} %param.17) | copy-start | bytes 4816900
  7.2 44.5 %all-gather.19.cloned.1.call-start = ((), (), s32[]{:S(2)}) async-start(), calls=%async_computation.16 | async-start | bytes 1966080 | tf_op jit(solution)/shard_map/all_gather | solution.py:507
  7.9 91.1 %all-gather.25.cloned.1.call-start = ((), (), s32[]{:S(2)}) async-start(), calls=%async_computation.19 | async-start | bytes 2621440 | tf_op jit(solution)/shard_map/all_gather | solution.py:507
  8.7 136.8 %all-gather.29.cloned.1.call-start = ((), (), s32[]{:S(2)}) async-start(), calls=%async_computation.21 | async-start | bytes 2621440 | tf_op jit(solution)/shard_map/all_gather | solution.py:507
  9.4 150.6 %all-gather.23.cloned.1.call-start = ((), (), s32[]{:S(2)}) async-start(), calls=%async_computation.18 | async-start | bytes 1572864 | tf_op jit(solution)/shard_map/all_gather | solution.py:507
  32.3 66.9 %copy-start.71 = (bf16[1,4,169]{2,1,0:T(4,128)(2,1)S(1)}, bf16[1,4,169]{2,1,0:T(4,128)(2,1)}, u32[]{:S(2)}) copy-start(bf16[1,4,169]{2,1,0:T(4,128)(2,1)} %param.25) | copy-start | bytes 4060
  32.3 67.0 %copy-start.70 = (bf16[1,512]{1,0:T(2,128)(2,1)S(1)}, bf16[1,512]{1,0:T(2,128)(2,1)}, u32[]{:S(2)}) copy-start(bf16[1,512]{1,0:T(2,128)(2,1)} %param.31) | copy-start | bytes 3076
  32.3 67.0 %copy-start.72 = (bf16[1,256]{1,0:T(2,128)(2,1)S(1)}, bf16[1,256]{1,0:T(2,128)(2,1)}, u32[]{:S(2)}) copy-start(bf16[1,256]{1,0:T(2,128)(2,1)} %param.24) | copy-start | bytes 1540
  32.3 67.0 %copy-start.80 = (u32[32]{0:T(128)S(1)}, u32[32]{0:T(128)}, u32[]{:S(2)}) copy-start(u32[32]{0:T(128)} %constant.224) | copy-start | bytes 388
  32.3 68.3 %copy-start.73 = (bf16[1,128]{1,0:T(2,128)(2,1)S(1)}, bf16[1,128]{1,0:T(2,128)(2,1)}, u32[]{:S(2)}) copy-start(bf16[1,128]{1,0:T(2,128)(2,1)} %param.21) | copy-start | bytes 772
  32.3 68.3 %copy-start.74 = (bf16[1,128]{1,0:T(2,128)(2,1)S(1)}, bf16[1,128]{1,0:T(2,128)(2,1)}, u32[]{:S(2)}) copy-start(bf16[1,128]{1,0:T(2,128)(2,1)} %param.22) | copy-start | bytes 772
  32.3 68.3 %copy-start.75 = (bf16[1,128]{1,0:T(2,128)(2,1)S(1)}, bf16[1,128]{1,0:T(2,128)(2,1)}, u32[]{:S(2)}) copy-start(bf16[1,128]{1,0:T(2,128)(2,1)} %param.27) | copy-start | bytes 772
  32.3 68.3 %copy-start.76 = (bf16[1,128]{1,0:T(2,128)(2,1)S(1)}, bf16[1,128]{1,0:T(2,128)(2,1)}, u32[]{:S(2)}) copy-start(bf16[1,128]{1,0:T(2,128)(2,1)} %param.28) | copy-start | bytes 772
  32.3 68.3 %copy-start.77 = (bf16[1,128]{1,0:T(2,128)(2,1)S(1)}, bf16[1,128]{1,0:T(2,128)(2,1)}, u32[]{:S(2)}) copy-start(bf16[1,128]{1,0:T(2,128)(2,1)} %param.29) | copy-start | bytes 772
  32.3 68.3 %copy-start.78 = (bf16[1,128]{1,0:T(2,128)(2,1)S(1)}, bf16[1,128]{1,0:T(2,128)(2,1)}, u32[]{:S(2)}) copy-start(bf16[1,128]{1,0:T(2,128)(2,1)} %param.33) | copy-start | bytes 772
  32.4 88.6 %copy-start.65 = (s32[49,49]{1,0:T(8,128)S(1)}, s32[49,49]{1,0:T(8,128)}, u32[]{:S(2)}) copy-start(s32[49,49]{1,0:T(8,128)} %param.20) | copy-start | bytes 28816
  32.4 137.1 %all-gather.21.cloned.1.call-start = ((), (), s32[]{:S(2)}) async-start(), calls=%async_computation.17 | async-start | bytes 4718592 | tf_op jit(solution)/shard_map/all_gather | solution.py:507
  51.7 69.6 %copy-start.79 = (s32[4,1]{0,1:T(1,128)S(1)}, s32[4,1]{0,1:T(1,128)}, u32[]{:S(2)}) copy-start(s32[4,1]{0,1:T(1,128)} %param.19) | copy-start | bytes 52
  51.7 162.4 %all-gather.27.cloned.1.call-start = ((), (), s32[]{:S(2)}) async-start(), calls=%async_computation.20 | async-start | bytes 6291456 | tf_op jit(solution)/shard_map/all_gather | solution.py:507
  99.1 133.2 %all-gather.31.cloned.1.call-start = ((), (), s32[]{:S(2)}) async-start(), calls=%async_computation.22 | async-start | bytes 6291456 | tf_op jit(solution)/shard_map/all_gather | solution.py:507
  145.5 294.6 %reduce-scatter.11.cloned.1.call-start = ((), (), s32[]{:S(2)}) async-start(), calls=%async_computation.9 | async-start | bytes 4718592 | tf_op jit(solution)/shard_map/reduce_scatter | solution.py:549
  147.5 40.0 %copy-start.7 = (bf16[4,208,512]{2,1,0:T(8,128)(2,1)}, bf16[4,208,512]{2,1,0:T(8,128)(2,1)S(1)}, u32[]{:S(2)}) copy-start(bf16[4,208,512]{2,1,0:T(8,128)(2,1)S(1)} %pad.14.x_ref) | copy-start | bytes 2555908
  223.5 13.4 %copy-start.2 = (bf16[512,4,512]{2,0,1:T(8,128)(2,1)}, bf16[512,4,512]{2,0,1:T(8,128)(2,1)S(1)}, u32[]{:S(2)}) copy-start(bf16[512,4,512]{2,0,1:T(8,128)(2,1)S(1)} %copy.77) | copy-start | bytes 6291460
  248.2 20.4 %copy-start.3 = (bf16[512,4,512]{2,0,1:T(8,128)(2,1)S(1)}, bf16[512,4,512]{2,0,1:T(8,128)(2,1)}, u32[]{:S(2)}) copy-start(bf16[512,4,512]{2,0,1:T(8,128)(2,1)} %copy.84) | copy-start | bytes 6291460
  248.2 20.4 %copy-start.30 = (f32[4,128]{1,0:T(4,128)S(1)}, f32[4,128]{1,0:T(4,128)}, u32[]{:S(2)}) copy-start(f32[4,128]{1,0:T(4,128)} %get-tuple-element.162) | copy-start | bytes 6148
  248.2 20.4 %copy-start.31 = (f32[4,128]{1,0:T(4,128)S(1)}, f32[4,128]{1,0:T(4,128)}, u32[]{:S(2)}) copy-start(f32[4,128]{1,0:T(4,128)} %get-tuple-element.160) | copy-start | bytes 6148
  248.2 20.4 %copy-start.32 = (f32[4,128]{1,0:T(4,128)S(1)}, f32[4,128]{1,0:T(4,128)}, u32[]{:S(2)}) copy-start(f32[4,128]{1,0:T(4,128)} %get-tuple-element.161) | copy-start | bytes 6148
  280.1 16.7 %copy-start.48 = (bf16[4,256,512]{2,1,0:T(8,128)(2,1)S(1)}, bf16[4,256,512]{2,1,0:T(8,128)(2,1)}, u32[]{:S(2)}) copy-start(bf16[4,256,512]{2,1,0:T(8,128)(2,1)} %copy-done.47) | copy-start | bytes 3145732
  280.1 16.7 %copy-start.52 = (bf16[4,208,512]{2,1,0:T(8,128)(2,1)S(1)}, bf16[4,208,512]{2,1,0:T(8,128)(2,1)}, u32[]{:S(2)}) copy-start(bf16[4,208,512]{2,1,0:T(8,128)(2,1)} %copy-done.51) | copy-start | bytes 2555908
  296.7 29.5 %copy-start.54 = (bf16[832,512]{1,0:T(8,128)(2,1)S(1)}, bf16[832,512]{1,0:T(8,128)(2,1)}, u32[]{:S(2)}) copy-start(bf16[832,512]{1,0:T(8,128)(2,1)} %copy-done.53) | copy-start | bytes 2555908
  326.3 16.6 %copy-start.8 = (bf16[4,208,512]{2,1,0:T(8,128)(2,1)S(1)}, bf16[4,208,512]{2,1,0:T(8,128)(2,1)}, u32[]{:S(2)}) copy-start(bf16[4,208,512]{2,1,0:T(8,128)(2,1)} %copy-done.7) | copy-start | bytes 2555908
  326.3 16.6 %copy-start.11 = (bf16[512,512]{1,0:T(8,128)(2,1)S(1)}, bf16[512,512]{1,0:T(8,128)(2,1)}, u32[]{:S(2)}) copy-start(bf16[512,512]{1,0:T(8,128)(2,1)} %get-tuple-element.159.wproj_ref) | copy-start | bytes 1572868
  326.3 16.6 %copy-start.19 = (bf16[256,208]{1,0:T(8,128)(2,1)S(1)}, bf16[256,208]{1,0:T(8,128)(2,1)}, u32[]{:S(2)}) copy-start(bf16[256,208]{1,0:T(8,128)(2,1)} %fusion.4.spread_ref) | copy-start | bytes 319492
  326.3 16.6 %copy-start.22 = (bf16[208,256]{1,0:T(8,128)(2,1)S(1)}, bf16[208,256]{1,0:T(8,128)(2,1)}, u32[]{:S(2)}) copy-start(bf16[208,256]{1,0:T(8,128)(2,1)} %fusion.6.gather_ref) | copy-start | bytes 319492
  326.3 16.6 %copy-start.27 = (f32[4,128]{1,0:T(4,128)S(1)}, f32[4,128]{1,0:T(4,128)}, u32[]{:S(2)}) copy-start(f32[4,128]{1,0:T(4,128)} %get-tuple-element.170) | copy-start | bytes 6148
  326.3 16.6 %copy-start.46 = (bf16[4,256,512]{2,1,0:T(8,128)(2,1)S(1)}, bf16[4,256,512]{2,1,0:T(8,128)(2,1)}, u32[]{:S(2)}) copy-start(bf16[4,256,512]{2,1,0:T(8,128)(2,1)} %copy-done.45) | copy-start | bytes 3145732
  326.3 16.6 %copy-start.50 = (bf16[4,208,512]{2,1,0:T(8,128)(2,1)S(1)}, bf16[4,208,512]{2,1,0:T(8,128)(2,1)}, u32[]{:S(2)}) copy-start(bf16[4,208,512]{2,1,0:T(8,128)(2,1)} %copy-done.49) | copy-start | bytes 2555908
  393.0 50.0 %reduce-scatter.13.cloned.1.call-start = ((), (), s32[]{:S(2)}) async-start(), calls=%async_computation.10 | async-start | bytes 1572864 | tf_op jit(solution)/shard_map/reduce_scatter | solution.py:549
  395.3 48.0 %reduce-scatter.21.cloned.1.call-start = ((), (), s32[]{:S(2)}) async-start(), calls=%async_computation.14 | async-start | bytes 6291456 | tf_op jit(solution)/shard_map/reduce_scatter | solution.py:549
  408.8 40.3 %reduce-scatter.17.cloned.1.call-start = ((), (), s32[]{:S(2)}) async-start(), calls=%async_computation.12 | async-start | bytes 6291456 | tf_op jit(solution)/shard_map/reduce_scatter | solution.py:549
  421.9 154.8 %all-reduce.8.cloned.1.call-start = ((), (), s32[]{:S(2)}) async-start(), calls=%async_computation.8 | async-start | bytes 143360 | tf_op jit(solution)/shard_map/psum | solution.py:562
  440.0 177.1 %reduce-scatter.25.cloned.1.call-start = ((), (), s32[]{:S(2)}) async-start(), calls=%async_computation.23 | async-start | bytes 1966080
  442.7 197.3 %reduce-scatter.15.cloned.1.call-start = ((), (), s32[]{:S(2)}) async-start(), calls=%async_computation.11 | async-start | bytes 655360 | tf_op jit(solution)/shard_map/reduce_scatter | solution.py:550
  443.3 240.8 %reduce-scatter.23.cloned.1.call-start = ((), (), s32[]{:S(2)}) async-start(), calls=%async_computation.15 | async-start | bytes 2621440 | tf_op jit(solution)/shard_map/reduce_scatter | solution.py:550
  443.9 285.2 %reduce-scatter.19.cloned.1.call-start = ((), (), s32[]{:S(2)}) async-start(), calls=%async_computation.13 | async-start | bytes 2621440 | tf_op jit(solution)/shard_map/reduce_scatter | solution.py:550
  449.1 343.9 %all-reduce.10.cloned.1.call-start = ((), (), s32[]{:S(2)}) async-start(), calls=%async_computation.24 | async-start | bytes 3145728 | tf_op jit(solution)/shard_map/psum | solution.py:551
  450.1 282.0 %collective-permute-start.1 = (bf16[4,208,512]{2,1,0:T(8,128)(2,1)}, bf16[4,208,512]{2,1,0:T(8,128)(2,1)}, u32[]{:S(2)}, u32[]{:S(2)}) collective-permute-start(bf16[4,208,512]{2,1,0:T(8,128)(2,1)} %broadcast_select_fusion.1), channel_id=1, source_target_pairs={{0,16},{16,0},{1,17},{17,1},{2,18},{18,2},{3,19},{19,3},{4,20},{20... | collective-permute-start | bytes 2555912 | tf_op jit(solution)/shard_map/ppermute | solution.py:532
  451.5 284.9 %collective-permute-start = (bf16[4,208,512]{2,1,0:T(8,128)(2,1)}, bf16[4,208,512]{2,1,0:T(8,128)(2,1)}, u32[]{:S(2)}, u32[]{:S(2)}) collective-permute-start(bf16[4,208,512]{2,1,0:T(8,128)(2,1)} %broadcast_select_fusion), channel_id=1, source_target_pairs={{0,16},{16,0},{1,17},{17,1},{2,18},{18,2},{3,19},{19,3},{4,20},{20... | collective-permute-start | bytes 2555912 | tf_op jit(solution)/shard_map/ppermute | solution.py:532
  (52 other events, 237.2 us)
Sparse Core Ops, SparseCore 0:
  9.6 42.0 all-gather.18
  53.2 45.7 all-gather.24
  100.6 44.8 all-gather.28
  146.9 7.8 all-gather.22
  156.2 13.2 all-gather.20
  170.9 14.8 all-gather.26
  187.3 14.8 all-gather.30
  393.1 12.2 reduce-scatter.10
  408.3 9.6 reduce-scatter.12
  420.1 13.2 reduce-scatter.20
  435.7 13.3 reduce-scatter.16
  455.1 121.5 all-reduce.7
  579.6 37.5 reduce-scatter.24
  619.3 20.6 reduce-scatter.14
  642.2 41.8 reduce-scatter.22
  686.2 42.8 reduce-scatter.18
  732.9 60.0 all-reduce.9

commit v2 on v1

v2 whole, which is shorter than its diff:
```python
import functools
import math

import jax
import jax.numpy as jnp
from jax import lax
from jax.experimental import pallas as pl
from jax.experimental.pallas import tpu as pltpu
from jax.sharding import PartitionSpec as P

D = 512
H = 16
HD = 32
WIN = 7
GRID = 14
SHIFT = 3
TOK = 196
RELS = 169
POS = WIN * WIN
NW = 4
WP = 64
TP = 208
ROWS = NW * WP
GH = 4
GL = GH * HD
BLK = 832
SUB_FWD = 208
SUB_BWD = 416
CHUNK = 64
AT_ONCE = 2
LATE = "late"
LINES = 32
GAIN, SHIFT_ROW, QV, TABLE, BPROJ, MGAIN, MSHIFT, HB, OB = 0, 1, 2, 4, 12, 13, 14, 15, 19
PLACES = (1, 3, 2, 0)
EPSILON = 1e-05
MASK_VALUE = -100.0
SHUT = -1e30
F32 = jnp.float32
BF = jnp.bfloat16
ANY = pl.BlockSpec(memory_space=pl.ANY)
VMEM_LIMIT = 60 << 20


def dot_nn(a, b):
    return lax.dot_general(a, b, (((1,), (0,)), ((), ())), preferred_element_type=F32)


def dot_nt(a, b):
    return lax.dot_general(a, b, (((1,), (1,)), ((), ())), preferred_element_type=F32)


def dot_tn(a, b):
    return lax.dot_general(a, b, (((0,), (0,)), ((), ())), preferred_element_type=F32)


def iota(shape, axis):
    return lax.broadcasted_iota(jnp.int32, shape, axis)


def normalize(rows):
    center = rows - jnp.mean(rows, -1, keepdims=True)
    inverse = lax.rsqrt(jnp.mean(center * center, -1, keepdims=True) + EPSILON)
    return center * inverse, inverse


def norm_back(grad_out, normed, inverse, gain):
    scaled = grad_out * gain
    return inverse * (
        scaled
        - jnp.mean(scaled, -1, keepdims=True)
        - normed * jnp.mean(scaled * normed, -1, keepdims=True)
    )


def remote(source, target, sems, axis, index):
    return pltpu.make_async_remote_copy(
        src_ref=source, dst_ref=target, send_sem=sems[0], recv_sem=sems[1], device_id={axis: index},
        device_id_type=pl.DeviceIdType.MESH,
    )


def place_in_mesh():
    return lax.axis_index("pipe"), lax.axis_index("dp"), lax.axis_index("tensor")


def greet():
    core, dp, shard = place_in_mesh()
    barrier = pltpu.get_barrier_semaphore()

    def signal(axis, index):
        pl.semaphore_signal(barrier, inc=1, device_id={axis: index}, device_id_type=pl.DeviceIdType.MESH)

    signal("pipe", 1 - core)
    for k in (1, 2, 3):
        signal("dp", dp ^ k)
        signal("tensor", lax.rem(shard + k, 4))
    pl.semaphore_wait(barrier, 7)


def quarter(half, j):
    core, dp, _ = place_in_mesh()
    return pl.ds(pl.multiple_of((core ^ half) * 256 + (dp ^ j) * CHUNK, CHUNK), CHUNK)


def by_core(action):
    for which in (0, 1):

        @pl.when(lax.axis_index("pipe") == which)
        def _():
            action(which)


def sems(*shape):
    return [pltpu.SemaphoreType.DMA(shape), pltpu.SemaphoreType.DMA(shape)]


class Part:
    plan = ()
    deferred = False

    def __init__(self, inputs=(), outputs=(), scratch=()):
        self.inputs, self.outputs, self.scratch = list(inputs), list(outputs), list(scratch)

    def bind(self, ins, outs, kept):
        self.ins, self.outs, self.kept = ins, outs, kept


class Weights(Part):
    def __init__(self, count, layer, whole=None, own=None, other=None, pieces=None):
        self.count, self.layer, self.whole = count, layer, whole
        inputs = [whole] if whole is not None else [*own, *other, *[piece for group in pieces for piece in group]]
        super().__init__(inputs, (), [pltpu.VMEM((count, 4, D, D), BF), pltpu.SemaphoreType.DMA((9 * count,))])

    def shard(self, mine, b):
        store, sem = self.kept
        if self.whole is not None:
            return pltpu.make_async_copy(self.ins[0].at[b, 0], store.at[b, 0], sem.at[b * 9])
        owns, others = self.ins[: self.count], self.ins[self.count : 2 * self.count]
        return pltpu.make_async_copy((owns if mine else others)[b], store.at[b, 0], sem.at[b * 9])

    def rest(self):
        store, sem = self.kept
        if self.whole is not None:
            return [
                pltpu.make_async_copy(self.ins[0].at[b, pl.ds(1, 3)], store.at[b, pl.ds(1, 3)], sem.at[b * 9 + 1])
                for b in range(self.count)
            ]
        return [
            pltpu.make_async_copy(
                self.ins[2 * self.count + b * 8 + half * 4 + j], store.at[b, pl.ds(1, 3), quarter(half, j), :],
                sem.at[b * 9 + half * 4 + j + 1],
            )
            for b in range(self.count)
            for half in range(2)
            for j in range(4)
        ]

    def load(self):
        if self.whole is not None:
            for b in range(self.count):
                self.shard(True, b).start()
        else:

            def shards(core):
                for b in range(self.count):
                    self.shard(core == self.layer, b).start()

            by_core(shards)
        for copy in self.rest():
            copy.start()

    def wait_shard(self):
        for b in range(self.count):
            self.shard(True, b).wait()

    def wait_rest(self):
        for copy in self.rest():
            copy.wait()


class Stored(Part):
    def __init__(self, *arrays):
        super().__init__(arrays, (), [pltpu.VMEM(a.shape, a.dtype) for a in arrays] + [pltpu.SemaphoreType.DMA((len(arrays),))])

    def copies(self):
        return [pltpu.make_async_copy(ref, kept, self.kept[-1].at[n]) for n, (ref, kept) in enumerate(zip(self.ins, self.kept))]

    def load(self):
        for copy in self.copies():
            copy.start()

    def wait(self):
        for copy in self.copies():
            copy.wait()


class Keep(Part):
    def __init__(self, *shapes):
        super().__init__((), [jax.ShapeDtypeStruct(shape, BF) for shape in shapes], [pltpu.SemaphoreType.DMA((len(shapes),))])

    def copies(self, refs):
        return [pltpu.make_async_copy(ref, out, self.kept[0].at[n]) for n, (ref, out) in enumerate(zip(refs, self.outs))]

    def start(self, *refs):
        for copy in self.copies(refs):
            copy.start()

    def wait(self, *refs):
        for copy in self.copies(refs):
            copy.wait()


class Near(Part):
    def __init__(self, layer, own, other, plan=(), deferred=False):
        self.layer, self.plan, self.deferred = layer, plan, deferred
        inputs = [] if own is None else [own, other]
        super().__init__(inputs, [jax.ShapeDtypeStruct((3, CHUNK, D), BF)], sems(3))

    def copy(self, mine, k):
        _, _, shard = place_in_mesh()
        source = self.ins[0 if mine else 1].at[quarter(0, 0), :]
        return remote(source, self.outs[0].at[k - 1], [sem.at[k - 1] for sem in self.kept], "tensor", lax.rem(shard + 4 - k, 4))

    def start(self):
        def sends(core):
            for k in (2, 1, 3):
                self.copy(core == self.layer, k).start()

        by_core(sends)

    def finish(self):
        for k in (1, 2, 3):
            self.copy(True, k).wait()

    def end(self):
        if not any(what == "finish" for _, what in self.plan):
            self.finish()


class Far(Part):
    def __init__(self, near, plan=(), source=None, deferred=False):
        self.plan, self.source, self.deferred = plan, source, deferred
        shape = jax.ShapeDtypeStruct((3, CHUNK, D), BF)
        super().__init__([] if near is None else [near], [shape] * 7, sems(2, 2) + sems(2) + sems(4))

    def rows(self, j):
        return pl.ds((j - 1) * 32, 32)

    def across(self, j, half):
        _, dp, _ = place_in_mesh()
        rows = self.rows(j if half == 0 else 3 - j)
        return remote(
            self.ins[0].at[:, rows], self.outs[j - 1].at[:, rows], [sem.at[j - 1, half] for sem in self.kept[:2]], "dp", dp ^ j
        )

    def onward(self, j):
        _, dp, _ = place_in_mesh()
        rows = self.rows(j)
        return remote(
            self.outs[j - 1].at[:, rows], self.outs[2].at[:, rows], [sem.at[j - 1] for sem in self.kept[2:4]], "dp", dp ^ (3 - j)
        )

    def over(self, j):
        core, _, _ = place_in_mesh()
        source = self.ins[0] if j == 0 else self.outs[j - 1]
        return remote(source, self.outs[3 + j], [sem.at[j] for sem in self.kept[4:]], "pipe", 1 - core)

    def start(self):
        for half in (0, 1):
            for j in (1, 2):
                self.across(j, half).start()
        self.over(0).start()

    def turn(self):
        for j in (1, 2):
            self.across(j, 0).wait()
        for j in (1, 2):
            self.onward(j).start()

    def rest(self):
        for j in (1, 2):
            self.across(j, 1).wait()
            self.over(j).start()

    def last(self):
        for j in (1, 2):
            self.onward(j).wait()
        self.over(3).start()

    def end(self):
        for j in range(4):
            self.over(j).wait()


class FarFirst(Part):
    def __init__(self, near, plan=(), source=None, deferred=False):
        self.plan, self.source, self.deferred = plan, source, deferred
        shape = jax.ShapeDtypeStruct((3, CHUNK, D), BF)
        super().__init__([] if near is None else [near], [shape] * 5, sems(2) + sems(3))

    def across(self, j):
        _, dp, _ = place_in_mesh()
        return remote(self.ins[0], self.outs[j - 1], [sem.at[j - 1] for sem in self.kept[:2]], "dp", dp ^ j)

    def over(self, j):
        core, _, _ = place_in_mesh()
        source = self.ins[0] if j == 0 else self.outs[j - 1]
        return remote(source, self.outs[2 + j], [sem.at[j] for sem in self.kept[2:]], "pipe", 1 - core)

    def start(self):
        for j in (1, 2):
            self.across(j).start()
        self.over(0).start()

    def end(self):
        for j in (1, 2):
            self.across(j).wait()
            self.over(j).start()
        for j in range(3):
            self.over(j).wait()


class FarSecond(Part):
    def __init__(self, first, plan=()):
        self.plan = plan
        shape = jax.ShapeDtypeStruct((3, CHUNK, D), BF)
        super().__init__(first[:2], [shape] * 2, sems(2) + sems())

    def onward(self, j):
        _, dp, _ = place_in_mesh()
        rows = pl.ds((j - 1) * 32, 32)
        return remote(
            self.ins[j - 1].at[:, rows], self.outs[0].at[:, rows], [sem.at[j - 1] for sem in self.kept[:2]], "dp", dp ^ (3 - j)
        )

    def over(self):
        core, _, _ = place_in_mesh()
        return remote(self.outs[0], self.outs[1], self.kept[2:], "pipe", 1 - core)

    def start(self):
        for j in (1, 2):
            self.onward(j).start()

    def last(self):
        for j in (1, 2):
            self.onward(j).wait()
        self.over().start()

    def end(self):
        if not any(what == "last" for _, what in self.plan):
            self.last()
        self.over().wait()


def gathered(near, first, second):
    return [near, *first[:2], second[0], *first[2:], second[1]]


class ReduceFirst(Part):
    def __init__(self, pair, plan=(), rows=(0, CHUNK)):
        self.plan, (self.start_row, self.size) = plan, rows
        size = self.size
        half = pltpu.VMEM((4, 4, size, D), BF)
        super().__init__(
            pair,
            [jax.ShapeDtypeStruct((4, size, D), BF)],
            [half, half, pltpu.VMEM((2, 2, 2, size, D), BF), pltpu.VMEM((2, 2, size, D), BF), pltpu.VMEM((4, size, D), BF)]
            + sems() + sems(2) + sems(2) + [pltpu.SemaphoreType.DMA(()), pltpu.SemaphoreType.DMA(())],
        )

    def bind(self, ins, outs, kept):
        super().bind(ins, outs, kept)
        self.mine, self.came, self.first, self.second, self.total = kept[:5]

    def over(self):
        core, _, _ = place_in_mesh()
        source = self.ins[1].at[:, :, pl.ds(self.start_row, self.size)]
        return remote(source, self.came, self.kept[5:7], "pipe", 1 - core)

    def load(self):
        return pltpu.make_async_copy(self.ins[0].at[:, :, pl.ds(self.start_row, self.size)], self.mine, self.kept[11])

    def across(self, j):
        _, dp, _ = place_in_mesh()
        source = self.mine.at[pl.ds(j - 1, 2), pl.ds(2 * j - 2, 2)]
        return remote(source, self.first.at[j - 1], [sem.at[j - 1] for sem in self.kept[7:9]], "dp", dp ^ j)

    def onward(self, j):
        _, dp, _ = place_in_mesh()
        source = self.mine.at[2 if j == 1 else 0, pl.ds(2 * j - 2, 2)]
        return remote(source, self.second.at[j - 1], [sem.at[j - 1] for sem in self.kept[9:11]], "dp", dp ^ (3 - j))

    def start(self):
        self.over().start()
        self.load().start()

    def cores(self):
        self.over().wait()
        self.load().wait()

        def add(place, k):
            self.mine[place, k] = (self.mine[place, k].astype(F32) + self.came[place, k].astype(F32)).astype(BF)

        def sent(n, carry):
            add(n // 2, n % 2)
            add(n // 2 + 1, n % 2 + 2)
            return carry

        def kept(n, carry):
            add(3, n)
            add(2 - n // 2 * 2, n)
            return carry

        lax.fori_loop(0, 4, sent, 0)
        for j in (1, 2):
            self.across(j).start()
        lax.fori_loop(0, 4, kept, 0)

    def turn(self):
        for j in (1, 2):
            self.across(j).wait()

        def add(n, carry):
            self.mine[2, n] = (self.mine[2, n].astype(F32) + self.first[0, 1, n].astype(F32)).astype(BF)
            self.mine[0, n + 2] = (self.mine[0, n + 2].astype(F32) + self.first[1, 0, n].astype(F32)).astype(BF)
            return carry

        lax.fori_loop(0, 2, add, 0)
        for j in (1, 2):
            self.onward(j).start()

    def close(self):
        for j in (1, 2):
            self.onward(j).wait()

        def add(n, carry):
            for j in (1, 2):
                k = n + 2 * j - 2
                total = self.mine[3, k].astype(F32) + self.first[j - 1, j - 1, n].astype(F32)
                self.total[k] = (total + self.second[j - 1, n].astype(F32)).astype(BF)
            return carry

        lax.fori_loop(0, 2, add, 0)

    def end(self):
        self.close()
        copy = pltpu.make_async_copy(self.total, self.outs[0], self.kept[12])
        copy.start()
        copy.wait()


class ReduceTurn(ReduceFirst):
    def __init__(self, pair, plan=()):
        super().__init__(pair, plan)
        self.outputs = [jax.ShapeDtypeStruct((2, 2, CHUNK, D), BF), jax.ShapeDtypeStruct((4, CHUNK, D), BF)]
        self.scratch.append(pltpu.SemaphoreType.DMA((3,)))

    def end(self):
        for j in (1, 2):
            self.across(j).wait()

        def add(n, carry):
            self.mine[2, n] = (self.mine[2, n].astype(F32) + self.first[0, 1, n].astype(F32)).astype(BF)
            self.mine[0, n + 2] = (self.mine[0, n + 2].astype(F32) + self.first[1, 0, n].astype(F32)).astype(BF)
            for j in (1, 2):
                k = n + 2 * j - 2
                self.mine[3, k] = (self.mine[3, k].astype(F32) + self.first[j - 1, j - 1, n].astype(F32)).astype(BF)
            return carry

        lax.fori_loop(0, 2, add, 0)
        sem = self.kept[13]
        copies = [
            pltpu.make_async_copy(self.mine.at[2, pl.ds(0, 2)], self.outs[0].at[0], sem.at[0]),
            pltpu.make_async_copy(self.mine.at[0, pl.ds(2, 2)], self.outs[0].at[1], sem.at[1]),
            pltpu.make_async_copy(self.mine.at[3], self.outs[1], sem.at[2]),
        ]
        for copy in copies:
            copy.start()
        for copy in copies:
            copy.wait()


class ReduceOnward(Part):
    def __init__(self, given, plan=()):
        self.plan = plan
        base = pltpu.VMEM((4, CHUNK, D), BF)
        super().__init__(
            given, [jax.ShapeDtypeStruct((4, CHUNK, D), BF)],
            [base, pltpu.VMEM((2, 2, CHUNK, D), BF)] + sems(2) + [pltpu.SemaphoreType.DMA(()), pltpu.SemaphoreType.DMA(())],
        )

    def onward(self, j):
        _, dp, _ = place_in_mesh()
        return remote(self.ins[0].at[j - 1], self.kept[1].at[j - 1], [sem.at[j - 1] for sem in self.kept[2:4]], "dp", dp ^ (3 - j))

    def load(self):
        return pltpu.make_async_copy(self.ins[1], self.kept[0], self.kept[4])

    def start(self):
        for j in (1, 2):
            self.onward(j).start()
        self.load().start()

    def close(self):
        self.load().wait()
        for j in (1, 2):
            self.onward(j).wait()
        total = self.kept[0]

        def add(n, carry):
            for j in (1, 2):
                k = n + 2 * j - 2
                total[k] = (total[k].astype(F32) + self.kept[1][j - 1, n].astype(F32)).astype(BF)
            return carry

        lax.fori_loop(0, 2, add, 0)

    def end(self):
        self.close()
        copy = pltpu.make_async_copy(self.kept[0], self.outs[0], self.kept[5])
        copy.start()
        copy.wait()


class ReduceSecond(Part):
    def __init__(self, totals=None, size=CHUNK, plan=()):
        self.plan = plan
        line = pltpu.VMEM((size, D), BF)
        super().__init__(
            [totals] if totals is not None else [],
            [jax.ShapeDtypeStruct((size, D), BF)],
            [line, pltpu.VMEM((3, size, D), BF)] + sems(3) + [pltpu.SemaphoreType.DMA(()), pltpu.SemaphoreType.DMA(())],
        )

    def own(self):
        return pltpu.make_async_copy(self.ins[0].at[0], self.kept[0], self.kept[4])

    def along(self, k):
        _, _, shard = place_in_mesh()
        return remote(
            self.ins[0].at[k], self.kept[1].at[k - 1], [sem.at[k - 1] for sem in self.kept[2:4]], "tensor", lax.rem(shard + k, 4)
        )

    def start(self):
        for k in (2, 1, 3):
            self.along(k).start()
        self.own().start()

    def close(self):
        self.own().wait()
        for k in (1, 2, 3):
            self.along(k).wait()
        total = self.kept[0][...].astype(F32)
        for k in range(3):
            total += self.kept[1][k].astype(F32)
        self.kept[0][...] = total.astype(BF)

    def end(self):
        if not any(what == "close" for _, what in self.plan):
            self.close()
        copy = pltpu.make_async_copy(self.kept[0], self.outs[0], self.kept[5])
        copy.start()
        copy.wait()


class Share(Part):
    def __init__(self, piece=None, rows=(0, CHUNK), target=None, source=None, plan=()):
        self.start_row, self.size = rows
        self.target, self.after, self.plan, self.deferred = target, source, plan, source is not None
        super().__init__(
            [piece] if piece is not None else [],
            [jax.ShapeDtypeStruct((D, D), BF)] if target is None else [],
            [pltpu.VMEM((self.size, D), BF)] + sems(3) + [pltpu.SemaphoreType.DMA(()), pltpu.SemaphoreType.DMA(())],
        )

    def place(self):
        core, dp, _ = place_in_mesh()
        start = pl.multiple_of(core * 256 + dp * CHUNK, CHUNK) + self.start_row
        out = self.outs[0] if self.target is None else self.target.outs[0]
        return out.at[pl.ds(pl.multiple_of(start, self.size), self.size), :]

    def across(self, j):
        _, dp, _ = place_in_mesh()
        return remote(self.ins[0], self.place(), [sem.at[j - 1] for sem in self.kept[1:3]], "dp", dp ^ j)

    def load(self):
        return pltpu.make_async_copy(self.ins[0], self.kept[0], self.kept[3])

    def keep(self):
        return pltpu.make_async_copy(self.kept[0], self.place(), self.kept[4])

    def start(self):
        if self.after is not None:
            self.ins = [self.after.kept[0]]
        for j in (3, 1, 2):
            self.across(j).start()
        self.load().start()

    def end(self):
        self.load().wait()
        self.keep().start()
        for j in (1, 2, 3):
            self.across(j).wait()
        self.keep().wait()


class Deliver(Part):
    def __init__(self, of_layers):
        super().__init__(of_layers, [jax.ShapeDtypeStruct(of_layers[0].shape, BF)], sems())

    def send(self, core):
        return remote(self.ins[1 - core], self.outs[0], self.kept, "pipe", 1 - core)

    def start(self):
        by_core(lambda core: self.send(core).start())

    def end(self):
        self.send(0).wait()


def carried_call(body, parts, collective_id, *, grid, in_specs, inputs, out_specs, out_shape, scratch_shapes, name, cost):
    n_in, n_out, n_scratch = len(inputs), len(out_shape), len(scratch_shapes)
    counts = [(len(part.inputs), len(part.outputs), len(part.scratch)) for part in parts]

    def whole_body(*refs):
        refs = list(refs)

        def take(count, groups):
            mine = [refs.pop(0) for _ in range(count)]
            return mine, [[refs.pop(0) for _ in range(n)] for n in groups]

        mine, part_ins = take(n_in, [n for n, _, _ in counts])
        outs, part_outs = take(n_out, [n for _, n, _ in counts])
        kept, part_kept = take(n_scratch, [n for _, _, n in counts])
        for part, a, b, c in zip(parts, part_ins, part_outs, part_kept):
            part.bind(a, b, c)
        for part in parts:
            if getattr(part, "source", None) is not None:
                part.ins = [part.source.outs[0]]
        body(*mine, *outs, *kept)

    extra_in = [x for part in parts for x in part.inputs]
    extra_out = [x for part in parts for x in part.outputs]
    params = dict(vmem_limit_bytes=VMEM_LIMIT)
    if collective_id is not None:
        params.update(collective_id=collective_id, has_side_effects=True)
    results = pl.pallas_call(
        whole_body,
        grid_spec=pltpu.PrefetchScalarGridSpec(
            num_scalar_prefetch=0,
            grid=grid,
            in_specs=list(in_specs) + [ANY] * len(extra_in),
            out_specs=list(out_specs) + [ANY] * len(extra_out),
            scratch_shapes=list(scratch_shapes) + [x for part in parts for x in part.scratch],
        ),
        out_shape=list(out_shape) + extra_out,
        name=name,
        compiler_params=pltpu.CompilerParams(**params),
        cost_estimate=cost,
    )(*inputs, *extra_in)
    own, rest = results[:n_out], results[n_out:]
    given = []
    for _, n, _ in counts:
        given.append(rest[:n])
        rest = rest[n:]
    return own, given


def begin(weights, tasks):
    pl.when(pl.program_id(0) == 0)(weights.load)
    if tasks:

        @pl.when(pl.program_id(0) == 0)
        def _():
            greet()
            for task in tasks:
                if not task.deferred:
                    task.start()


def planned(tasks, point):
    return [getattr(task, what) for task in tasks for at, what in task.plan if at == point]


def step_end(tasks, steps):
    for step in range(steps):
        calls = planned(tasks, step)
        if step == steps - 1:
            calls += [task.end for task in tasks]
        if calls:

            @pl.when(pl.program_id(0) == step)
            def _():
                for call in calls:
                    call()


def whole(shape):
    return pl.BlockSpec(shape, lambda i: (0,) * len(shape))


def per(shape):
    return pl.BlockSpec((1,) + shape, lambda i: (i,) + (0,) * len(shape))


SMEM = pl.BlockSpec(memory_space=pltpu.SMEM)


def along_model(table_ref, layer, row, rolled):
    shard = lax.axis_index("tensor") if rolled else 0
    return jnp.concatenate([table_ref[(z - shard + 4) % 4, layer, row : row + 1, :].astype(F32) for z in range(4)], 1)


def window_token(shape, axis, offset):
    s = iota(shape, axis)
    w, a = s // WP, s % WP
    r = (w // 2) * WIN + a // WIN + offset
    c = (w % 2) * WIN + a % WIN + offset
    r, c = jnp.where(r >= GRID, r - GRID, r), jnp.where(c >= GRID, c - GRID, c)
    return jnp.where(a < POS, r * GRID + c, -1)


def spread_map(offset):
    return (window_token((ROWS, 1), 0, offset) == iota((ROWS, TP), 1)).astype(F32).astype(BF)


def gather_map(offset):
    return (window_token((1, ROWS), 1, offset) == iota((TP, ROWS), 0)).astype(F32).astype(BF)


def head_mask():
    return (iota((GH * WP, GL), 0) // WP == iota((GH * WP, GL), 1) // HD).astype(F32).astype(BF)


def region_mask(w):
    def band(a, which):
        place = which * WIN + a
        return (place >= GRID - WIN).astype(jnp.int32) + (place >= GRID - SHIFT).astype(jnp.int32)

    def label(a):
        return band(a // WIN, w // 2) * 3 + band(a % WIN, w % 2)

    keys = label(iota((WP, 1), 0))
    queries = label(iota((1, GH * WP), 1) % WP)
    return jnp.where(keys != queries, MASK_VALUE, 0.0).astype(F32)


def block_diagonal(rows, mask):
    return jnp.concatenate([rows] * GH, axis=0) * mask


def query_major(pt):
    turned = pt.T
    return jnp.concatenate([turned[h * WP : (h + 1) * WP] for h in range(GH)], axis=1)


def pick_diagonal(full):
    head = iota((WP, GL), 1) // HD
    out = full[0:WP]
    for h in range(1, GH):
        out = jnp.where(head == h, full[h * WP : (h + 1) * WP], out)
    return out


def permutation(size, source_of, inverse):
    rows = iota((size, size), 1 if inverse else 0)
    cols = iota((size, size), 0 if inverse else 1)
    return (rows == source_of(cols)).astype(F32).astype(BF)


def qkv_source(col):
    return (col % GL) // HD * (3 * HD) + col // GL * HD + col % HD


def qv_source(col):
    return (col % GL) // HD * (2 * HD) + col // GL * HD + col % HD


def attn_fwd_body(
    layer, rolled, weights, keep, tasks, x_ref, table_ref, bias_ref, fw_ref, qkv_ref, p_ref, ho_ref, mid_ref,
    xs_ref, how_ref, wq_ref, wpt_ref, vec_ref, shift_ref, spread_ref, gather_ref, mask_ref, region_ref,
):
    begin(weights, tasks)
    wa_ref = weights.kept[0].at[0]
    first_step = pl.program_id(0) == 0

    @pl.when(first_step)
    def _():
        for n, row in enumerate((GAIN, SHIFT_ROW, BPROJ)):
            vec_ref[n : n + 1, :] = along_model(table_ref, layer, row, rolled)
        for g in range(4):
            qv = table_ref[g, layer, QV : QV + 2, :].astype(F32)
            at = 3 * GL * g
            for n, (scale, shift) in enumerate(((HD ** (-0.5), qv[0:1] * HD ** (-0.5)), (1.0, 0.0), (1.0, qv[1:2]))):
                lanes = slice(at + n * GL, at + (n + 1) * GL)
                shift_ref[0:1, lanes] = jnp.full((1, GL), scale, F32)
                shift_ref[1:2, lanes] = shift + jnp.zeros((1, GL), F32)
        spread_ref[...] = spread_map(layer * SHIFT)
        gather_ref[...] = gather_map(layer * SHIFT)
        mask_ref[...] = head_mask()
        if layer:
            for w in range(NW):
                region_ref[w] = region_mask(w)
        else:
            xs_ref[...] = jnp.zeros_like(xs_ref)

    if layer:
        x = x_ref[0].astype(F32)
    else:
        xs_ref[0:TOK, :] = x_ref[0, lax.axis_index("pipe")]
        x = xs_ref[...].astype(F32)
    normed, _ = normalize(x)
    first = (normed * vec_ref[0:1, :] + vec_ref[1:2, :]).astype(BF)
    fw = dot_nn(spread_ref[...], first).astype(BF)
    fw_ref[0] = fw

    @pl.when(first_step)
    def _():
        weights.wait_shard()
        weights.wait_rest()
        for g in range(4):
            wq_ref[:, 3 * GL * g : 3 * GL * (g + 1)] = wa_ref[g, :, : 3 * GL]
            wpt_ref[:, g * GL : (g + 1) * GL] = wa_ref[g, :, 3 * GL :]
        keep.start(wq_ref, wpt_ref)

    for n in range(3):
        lanes = slice(n * D, (n + 1) * D)
        projected = dot_nn(fw, wq_ref[:, lanes])
        qkv_ref[0, :, lanes] = (projected * shift_ref[0:1, lanes] + shift_ref[1:2, lanes]).astype(BF)

    def windows(n, carry):
        chains = [(n * AT_ONCE + w, g) for w in range(AT_ONCE) for g in range(4)]

        def rows(w):
            return pl.ds(pl.multiple_of(w * WP, WP), WP)

        def part(w, g, n):
            return qkv_ref[0, rows(w), (3 * g + n) * GL : (3 * g + n + 1) * GL]

        scores = [dot_nt(part(w, g, 1), block_diagonal(part(w, g, 0), mask_ref[...])) for w, g in chains]
        probs = []
        for (w, g), st in zip(chains, scores):
            st = st + bias_ref[g]
            if layer:
                st = st + region_ref[w]
            e = jnp.exp(st - jnp.max(st, 0, keepdims=True))
            pt = (e * (1.0 / jnp.sum(e, 0, keepdims=True))).astype(BF)
            p_ref[0, w, g] = pt
            probs.append(pt)
        mixed = [dot_tn(pt, part(w, g, 2)) for (w, g), pt in zip(chains, probs)]
        for (w, g), out in zip(chains, mixed):
            how_ref[rows(w), g * GL : (g + 1) * GL] = pick_diagonal(out).astype(BF)
        return carry

    lax.fori_loop(0, NW // AT_ONCE, windows, 0)
    ho = dot_nn(gather_ref[...], how_ref[...]).astype(BF)
    ho_ref[0] = ho
    mid_ref[0] = x + (dot_nt(ho, wpt_ref[...]) + vec_ref[2:3, :])
    step_end(tasks, 4)

    @pl.when(pl.program_id(0) == pl.num_programs(0) - 1)
    def _():
        keep.wait(wq_ref, wpt_ref)


def attn_fwd(layer, rolled, x, table, bias, weights, tasks=(), collective_id=None):
    n = x.shape[0]
    keep = Keep((D, 3 * D), (D, D))
    return carried_call(
        functools.partial(attn_fwd_body, layer, rolled, weights, keep, tasks),
        [keep, weights, *tasks],
        collective_id,
        grid=(n,),
        in_specs=[per(x.shape[1:]), whole(table.shape), whole((4, WP, GH * WP))],
        inputs=(x, table, bias),
        out_specs=[per((ROWS, D)), per((ROWS, 3 * D)), per((NW, 4, WP, GH * WP)), per((TP, D)), per((TP, D))],
        out_shape=[
            jax.ShapeDtypeStruct((n, ROWS, D), BF),
            jax.ShapeDtypeStruct((n, ROWS, 3 * D), BF),
            jax.ShapeDtypeStruct((n, NW, 4, WP, GH * WP), BF),
            jax.ShapeDtypeStruct((n, TP, D), BF),
            jax.ShapeDtypeStruct((n, TP, D), F32),
        ],
        scratch_shapes=[
            pltpu.VMEM((TP, D), BF), pltpu.VMEM((ROWS, D), BF), pltpu.VMEM((D, 3 * D), BF), pltpu.VMEM((D, D), BF), pltpu.VMEM((8, D), F32),
            pltpu.VMEM((8, 3 * D), F32), pltpu.VMEM((ROWS, TP), BF), pltpu.VMEM((TP, ROWS), BF), pltpu.VMEM((GH * WP, GL), BF),
            pltpu.VMEM((NW, WP, GH * WP), F32),
        ],
        name="attn_fwd",
        cost=pl.CostEstimate(flops=n * 2 * 256 * 512 * 2600, bytes_accessed=n * 2 << 20, transcendentals=0),
    )


def gelu_parts(v):
    cdf = 0.5 * (1.0 + lax.erf(v * 0.5**0.5))
    pdf = jnp.exp(-0.5 * v * v) * (2.0 * math.pi) ** (-0.5)
    return v * cdf, cdf + v * pdf


def alive_of(counts_ref, m):
    slot = lax.axis_index("tensor") * 2 + lax.axis_index("pipe")
    return (slot < counts_ref[m, 0]).astype(F32)


def live_rows(counts_ref, m):
    return jnp.where(iota((TP, 1), 0) < TOK, alive_of(counts_ref, m), 0.0)


def mlp_fwd_body(
    layer, rolled, weights, keep, tasks, counts_ref, mid_ref, table_ref, second_ref, act_ref, slope_ref, y_ref, out_ref, acc_ref, hb_ref
):
    c = pl.program_id(0)
    rows_total = mid_ref.shape[0]
    begin(weights, tasks)
    wm_ref = weights.kept[0]

    @pl.when(c == 0)
    def _():
        for k in range(4):
            hb_ref[k] = jnp.concatenate([table_ref[k, layer, HB + n : HB + n + 1, :].astype(F32) for n in range(4)], 1)
        gain = along_model(table_ref, layer, MGAIN, rolled)
        shift = along_model(table_ref, layer, MSHIFT, rolled)
        mid = mid_ref[...]
        normed, _ = normalize(mid)
        second_ref[...] = (normed * gain + shift).astype(BF)
        acc_ref[...] = mid + along_model(table_ref, layer, OB, rolled)
        weights.wait_shard()

    @pl.when(c == 1)
    def _():
        weights.wait_rest()
        keep.start(wm_ref)

    def block(b, carry):
        parts = [pl.ds(pl.multiple_of(b * BLK + n * SUB_FWD, SUB_FWD), SUB_FWD) for n in range(BLK // SUB_FWD)]
        acts = []
        pre = [dot_nn(second_ref[rows, :], wm_ref[0, c]) for rows in parts]
        for rows, value in zip(parts, pre):
            act, slope = gelu_parts(value + hb_ref[c])
            act = act.astype(BF)
            act_ref[0, rows, :] = act
            slope_ref[0, rows, :] = slope.astype(BF)
            acts.append(act)
        outs = [dot_nn(act, wm_ref[1, c]) for act in acts]
        for rows, out in zip(parts, outs):
            acc_ref[rows, :] += out
        return carry

    lax.fori_loop(0, rows_total // BLK, block, 0)

    @pl.when(c == pl.num_programs(0) - 1)
    def _():
        for m in range(rows_total // TP):
            y = (acc_ref[m * TP : (m + 1) * TP, :] * live_rows(counts_ref, m)).astype(BF)
            y_ref[m] = y
            out_ref[m] = y[:TOK]
        keep.wait(wm_ref)

    step_end(tasks, 4)


def mlp_fwd(layer, rolled, counts, mid, table, weights, tasks=(), collective_id=None):
    r = mid.shape[0]
    n = r // TP
    keep = Keep((2, 4, D, D))
    return carried_call(
        functools.partial(mlp_fwd_body, layer, rolled, weights, keep, tasks),
        [keep, weights, *tasks],
        collective_id,
        grid=(4,),
        in_specs=[SMEM, whole((r, D)), whole(table.shape)],
        inputs=(counts, mid, table),
        out_specs=[whole((r, D)), per((r, D)), per((r, D)), whole((n, TP, D)), whole((n, TOK, D))],
        out_shape=[
            jax.ShapeDtypeStruct((r, D), BF),
            jax.ShapeDtypeStruct((4, r, D), BF),
            jax.ShapeDtypeStruct((4, r, D), BF),
            jax.ShapeDtypeStruct((n, TP, D), BF),
            jax.ShapeDtypeStruct((n, TOK, D), BF),
        ],
        scratch_shapes=[pltpu.VMEM((r, D), F32), pltpu.VMEM((4, 1, D), F32)],
        name="mlp_fwd",
        cost=pl.CostEstimate(flops=4 * r * D * 2048, bytes_accessed=12 << 20, transcendentals=0),
    )


def scatter_rows(place, value_ref, mine_ref, away_ref, index):
    core, dp = place
    for half, out_ref in enumerate((mine_ref, away_ref)):
        for n, j in enumerate(PLACES):
            start = (core ^ half) * 256 + (dp ^ j) * CHUNK
            out_ref[n, index] = value_ref[pl.ds(pl.multiple_of(start, CHUNK), CHUNK), :]


def where_in_plane(rolled):
    return (lax.axis_index("pipe"), lax.axis_index("dp")) if rolled else (jnp.int32(0), jnp.int32(0))


def by_shard(row):
    return jnp.concatenate([row[None, :, z * GL : (z + 1) * GL] for z in range(4)], 0)


def mlp_bwd_body(
    layer, rolled, weights, tasks, counts_ref, g_ref, act_ref, slope_ref, second_ref, mid_ref, table_ref,
    ghw_ref, ghw_away_ref, gow_ref, gow_away_ref, ghb_ref, gmid_ref, small_ref,
    gy_ref, gyt_ref, sect_ref, gp_ref, acc_ref, value_ref,
):
    c = pl.program_id(0)
    rows_total = mid_ref.shape[0]
    begin(weights, tasks)
    wm_ref = weights.kept[0]

    @pl.when(c == 0)
    def _():
        total = jnp.zeros((1, D), F32)
        for m in range(rows_total // TP):
            rows = slice(m * TP, (m + 1) * TP)
            if layer:
                gy_ref[rows, :] = jnp.zeros((TP, D), BF)
                gy = g_ref[m, lax.axis_index("pipe")].astype(F32) * alive_of(counts_ref, m)
                gy_ref[m * TP : m * TP + TOK, :] = gy.astype(BF)
            else:
                gy = g_ref[m].astype(F32) * live_rows(counts_ref, m)
                gy_ref[rows, :] = gy.astype(BF)
            total += jnp.sum(gy, 0, keepdims=True)
        small_ref[:, 0:1] = by_shard(total)
        gyt_ref[...] = gy_ref[...].T
        sect_ref[...] = second_ref[...].T
        acc_ref[...] = jnp.zeros_like(acc_ref)
        weights.wait()

    ghb_ref[0] = jnp.zeros_like(ghb_ref[0])

    def block(b, carry):
        parts = [pl.ds(pl.multiple_of(b * BLK + n * SUB_BWD, SUB_BWD), SUB_BWD) for n in range(BLK // SUB_BWD)]
        slopes = [dot_nt(gy_ref[rows, :], wm_ref[1, c]) for rows in parts]
        pres = []
        for rows, value in zip(parts, slopes):
            gp = value * slope_ref[0, rows, :].astype(F32)
            total = jnp.sum(gp, 0, keepdims=True)
            for n in range(4):
                ghb_ref[0, n : n + 1, :] += total[:, n * GL : (n + 1) * GL]
            gp = gp.astype(BF)
            gp_ref[rows, :] = gp
            pres.append(gp)
        outs = [dot_nt(gp, wm_ref[0, c]) for gp in pres]
        for rows, out in zip(parts, outs):
            acc_ref[rows, :] += out
        return carry

    lax.fori_loop(0, rows_total // BLK, block, 0)
    place = where_in_plane(rolled)
    value_ref[0] = dot_nn(sect_ref[...], gp_ref[...]).astype(BF)
    value_ref[1] = dot_nn(gyt_ref[...], act_ref[0]).astype(BF)
    scatter_rows(place, value_ref.at[0], ghw_ref, ghw_away_ref, 0)
    scatter_rows(place, value_ref.at[1], gow_ref, gow_away_ref, 0)

    @pl.when(c == pl.num_programs(0) - 1)
    def _():
        for call in planned(tasks, LATE):
            call()
        e = acc_ref[...]
        normed, inverse = normalize(mid_ref[...])
        small_ref[:, 2:3] = by_shard(jnp.sum(e * normed, 0, keepdims=True))
        small_ref[:, 3:4] = by_shard(jnp.sum(e, 0, keepdims=True))
        gmid = gy_ref[...].astype(F32) + norm_back(e, normed, inverse, along_model(table_ref, layer, MGAIN, rolled))
        small_ref[:, 1:2] = by_shard(jnp.sum(gmid, 0, keepdims=True))
        gmid_ref[...] = gmid

    step_end(tasks, 4)


PIECES = jax.ShapeDtypeStruct((4, 4, CHUNK, D), BF)


def mlp_bwd(layer, rolled, counts, g, act, slope, second, mid, table, weights, tasks=(), collective_id=None):
    r = mid.shape[0]
    pieces = pl.BlockSpec((4, 1, CHUNK, D), lambda i: (0, i, 0, 0))
    return carried_call(
        functools.partial(mlp_bwd_body, layer, rolled, weights, tasks),
        [weights, *tasks],
        collective_id,
        grid=(4,),
        in_specs=[SMEM, whole(g.shape), per((r, D)), per((r, D)), whole((r, D)), whole((r, D)), whole(table.shape)],
        inputs=(counts, g, act, slope, second, mid, table),
        out_specs=[pieces, pieces, pieces, pieces, per((4, GL)), whole((r, D)), whole((4, 4, GL))],
        out_shape=[
            PIECES, PIECES, PIECES, PIECES,
            jax.ShapeDtypeStruct((4, 4, GL), F32),
            jax.ShapeDtypeStruct((r, D), F32),
            jax.ShapeDtypeStruct((4, 4, GL), F32),
        ],
        scratch_shapes=[
            pltpu.VMEM((r, D), BF), pltpu.VMEM((D, r), BF), pltpu.VMEM((D, r), BF), pltpu.VMEM((r, D), BF),
            pltpu.VMEM((r, D), F32), pltpu.VMEM((2, D, D), BF),
        ],
        name="mlp_bwd",
        cost=pl.CostEstimate(flops=8 * r * D * 2048, bytes_accessed=16 << 20, transcendentals=0),
    )


def attn_bwd_body(
    layer, rolled, weights, tasks, x_ref, gmid_ref, fw_ref, qkv_ref, p_ref, ho_ref, table_ref,
    gin_ref, out_ref, ga_ref, ga_away_ref, gqv_ref, gtab_ref, small_ref,
    xs_ref, gw_ref, dq_ref, fwt_ref, hos_ref, gms_ref, value_ref, spread_ref, gather_ref, mask_ref, gain_ref,
):
    i = pl.program_id(0)
    last = pl.num_programs(0) - 1
    begin(weights, tasks)
    wq_ref, wpt_ref = weights.kept[:2]

    @pl.when(i == 0)
    def _():
        gqv_ref[...] = jnp.zeros_like(gqv_ref)
        gtab_ref[...] = jnp.zeros_like(gtab_ref)
        small_ref[...] = jnp.zeros_like(small_ref)
        spread_ref[...] = spread_map(layer * SHIFT)
        gather_ref[...] = gather_map(layer * SHIFT)
        mask_ref[...] = head_mask()
        gain_ref[...] = along_model(table_ref, layer, GAIN, rolled)
        if not layer:
            xs_ref[...] = jnp.zeros_like(xs_ref)

    gmid = gmid_ref[0]
    gmb = gmid.astype(BF)
    image = pl.ds(pl.multiple_of(i * TP, 16), TP)
    gms_ref[image, :] = gmb
    hos_ref[image, :] = ho_ref[0]
    base = pl.multiple_of(i * ROWS, ROWS)
    fwt_ref[:, pl.ds(base, ROWS)] = fw_ref[0].T

    @pl.when(i == 0)
    def _():
        weights.wait()

    heads = dot_nn(gmb, wpt_ref[...]).astype(BF)
    gw_ref[...] = dot_nn(spread_ref[...], heads).astype(BF)
    scale = HD ** (-0.5)

    def windows(n, carry):
        chains = [(n * AT_ONCE + w, g) for w in range(AT_ONCE) for g in range(4)]
        mask = mask_ref[...]

        def rows(w):
            return pl.ds(pl.multiple_of(w * WP, WP), WP)

        def part(w, g, n):
            return qkv_ref[0, rows(w), (3 * g + n) * GL : (3 * g + n + 1) * GL]

        bd_grads = [block_diagonal(gw_ref[rows(w), g * GL : (g + 1) * GL], mask) for w, g in chains]
        terms = [dot_nt(part(w, g, 2), bd_grad) for (w, g), bd_grad in zip(chains, bd_grads)]
        dvs = [dot_nn(p_ref[0, w, g], bd_grad) for (w, g), bd_grad in zip(chains, bd_grads)]
        scores = []
        for (w, g), term in zip(chains, terms):
            ptf = p_ref[0, w, g].astype(F32)
            pd = term * ptf
            ds = pd - ptf * jnp.sum(pd, 0, keepdims=True)
            gtab_ref[g] += ds
            scores.append(ds.astype(BF))
        dks = [dot_nn(ds, block_diagonal(part(w, g, 0), mask)) for (w, g), ds in zip(chains, scores)]
        dqs = [dot_tn(ds, part(w, g, 1)) for (w, g), ds in zip(chains, scores)]
        for (w, g), full, dk, dv in zip(chains, dqs, dks, dvs):
            dq = pick_diagonal(full) * scale
            out_rows = pl.ds(pl.multiple_of(base + w * WP, WP), WP)
            gqv_ref[g, 0:1] += jnp.sum(dq, 0, keepdims=True)
            gqv_ref[g, 1:2] += jnp.sum(dv, 0, keepdims=True)
            for n, value in enumerate((dq, dk, dv)):
                dq_ref[out_rows, (3 * g + n) * GL : (3 * g + n + 1) * GL] = value.astype(BF)
        return carry

    lax.fori_loop(0, NW // AT_ONCE, windows, 0)
    image_rows = pl.ds(base, ROWS)
    e = dot_nt(dq_ref[image_rows, :], wq_ref[...])
    e = dot_nn(gather_ref[...], e.astype(BF))
    if layer:
        x = x_ref[0].astype(F32)
    else:
        xs_ref[0:TOK, :] = x_ref[0, lax.axis_index("pipe")]
        x = xs_ref[...].astype(F32)
    normed, inverse = normalize(x)
    small_ref[:, 0:1] += by_shard(jnp.sum(e * normed, 0, keepdims=True))
    small_ref[:, 1:2] += by_shard(jnp.sum(e, 0, keepdims=True))
    gin = (gmid + norm_back(e, normed, inverse, gain_ref[...])).astype(BF)
    gin_ref[0] = gin
    out_ref[0] = gin[:TOK]

    @pl.when(i == last)
    def _():
        for call in planned(tasks, LATE):
            call()

        def chunk(n, carry):
            lanes = pl.ds(pl.multiple_of(n * D, D), D)
            value_ref[:, lanes] = dot_nn(fwt_ref[...], dq_ref[:, lanes]).astype(BF)
            return carry

        lax.fori_loop(0, 3, chunk, 0)
        value_ref[:, 3 * D :] = dot_nn(gms_ref[...].T, hos_ref[...]).astype(BF)
        core, dp = where_in_plane(rolled)
        for half, group_ref in enumerate((ga_ref, ga_away_ref)):
            for n, j in enumerate(PLACES):
                rows = pl.ds(pl.multiple_of((core ^ half) * 256 + (dp ^ j) * CHUNK, CHUNK), CHUNK)
                for g in range(4):
                    group_ref[n, g, :, : 3 * GL] = value_ref[rows, 3 * GL * g : 3 * GL * (g + 1)]
                    group_ref[n, g, :, 3 * GL :] = value_ref[rows, 3 * D + GL * g : 3 * D + GL * (g + 1)]

    step_end(tasks, 4)


def attn_bwd(layer, rolled, x, gmid, fw, qkv, p, ho, table, weights, tasks=(), collective_id=None):
    n = x.shape[0]
    return carried_call(
        functools.partial(attn_bwd_body, layer, rolled, weights, tasks),
        [weights, *tasks],
        collective_id,
        grid=(n,),
        in_specs=[
            per(x.shape[1:]), per((TP, D)), per((ROWS, D)), per((ROWS, 3 * D)), per((NW, 4, WP, GH * WP)), per((TP, D)),
            whole(table.shape),
        ],
        inputs=(x, gmid, fw, qkv, p, ho, table),
        out_specs=[
            per((TP, D)), per((TOK, D)), whole(PIECES.shape), whole(PIECES.shape), whole((4, 2, GL)), whole((4, WP, GH * WP)),
            whole((4, 2, GL)),
        ],
        out_shape=[
            jax.ShapeDtypeStruct((n, TP, D), BF),
            jax.ShapeDtypeStruct((n, TOK, D), BF),
            PIECES, PIECES,
            jax.ShapeDtypeStruct((4, 2, GL), F32),
            jax.ShapeDtypeStruct((4, WP, GH * WP), F32),
            jax.ShapeDtypeStruct((4, 2, GL), F32),
        ],
        scratch_shapes=[
            pltpu.VMEM((TP, D), BF), pltpu.VMEM((ROWS, D), BF), pltpu.VMEM((n * ROWS, 3 * D), BF), pltpu.VMEM((D, n * ROWS), BF),
            pltpu.VMEM((n * TP, D), BF), pltpu.VMEM((n * TP, D), BF), pltpu.VMEM((D, 4 * D), BF),
            pltpu.VMEM((ROWS, TP), BF), pltpu.VMEM((TP, ROWS), BF), pltpu.VMEM((GH * WP, GL), BF), pltpu.VMEM((1, D), F32),
        ],
        name="attn_bwd",
        cost=pl.CostEstimate(flops=n * 4 * 256 * 512 * 2600, bytes_accessed=n * 3 << 20, transcendentals=0),
    )


def plain_call(body, name, inputs, out_shape, scratch_shapes=(), grid=(), in_specs=None, out_specs=None, bytes_accessed=4 << 20):
    return pl.pallas_call(
        body,
        grid=grid,
        out_shape=out_shape,
        in_specs=in_specs or [pl.BlockSpec(memory_space=pltpu.VMEM)] * len(inputs),
        out_specs=out_specs or jax.tree.map(lambda _: pl.BlockSpec(memory_space=pltpu.VMEM), out_shape),
        scratch_shapes=list(scratch_shapes),
        name=name,
        compiler_params=pltpu.CompilerParams(vmem_limit_bytes=VMEM_LIMIT),
        cost_estimate=pl.CostEstimate(flops=bytes_accessed, bytes_accessed=bytes_accessed, transcendentals=0),
    )(*inputs)


def prepare_body(wqkv, wproj, gain, shift, qv, table, bproj, mgain, mshift, hb, ob, own_a_ref, lines_ref, rows_ref):
    own_a_ref[:, : 3 * GL] = dot_nn(wqkv[...], permutation(3 * GL, qkv_source, False)).astype(BF)
    own_a_ref[:, 3 * GL :] = wproj[...].T
    rows_ref[...] = jnp.zeros_like(rows_ref)
    for row, ref in ((GAIN, gain), (SHIFT_ROW, shift), (BPROJ, bproj), (MGAIN, mgain), (MSHIFT, mshift), (OB, ob)):
        rows_ref[row : row + 1, :] = ref[...].astype(F32)
    terms = dot_nn(jnp.broadcast_to(qv[...], (16, 2 * GL)), permutation(2 * GL, qv_source, False))
    hidden, places = hb[...].astype(F32), table[...].astype(F32)
    for n in range(2):
        rows_ref[QV + n : QV + n + 1, :] = terms[0:1, n * GL : (n + 1) * GL]
    for n in range(4):
        rows_ref[HB + n : HB + n + 1, :] = hidden[:, n * GL : (n + 1) * GL]
    rows_ref[TABLE : TABLE + 4, :] = places[:, :GL]
    rows_ref[TABLE + 4 : TABLE + 8, 0 : RELS - GL] = places[:, GL:]
    lines_ref[...] = rows_ref[...].astype(BF)


def prepare(wqkv, wproj, *small):
    return plain_call(
        prepare_body, "prepare", (wqkv, wproj, *small),
        [jax.ShapeDtypeStruct((D, D), BF), jax.ShapeDtypeStruct((LINES, GL), BF)], [pltpu.VMEM((LINES, GL), F32)],
    )


class Exchange(Part):
    def __init__(self, own, lines):
        shapes = [jax.ShapeDtypeStruct(part.shape, part.dtype) for part in own]
        shapes.append(jax.ShapeDtypeStruct((4, 2) + lines.shape, lines.dtype))
        super().__init__([*own, lines], shapes, sems(4) + sems(3) + [pltpu.SemaphoreType.DMA(())])

    def swap(self, n):
        core, _, _ = place_in_mesh()
        target = self.outs[n] if n < 3 else self.outs[3].at[0, core]
        return remote(self.ins[n], target, [sem.at[n] for sem in self.kept[:2]], "pipe", 1 - core)

    def keep(self):
        core, _, _ = place_in_mesh()
        return pltpu.make_async_copy(self.ins[3], self.outs[3].at[0, core], self.kept[4])

    def spread(self, k):
        _, _, shard = place_in_mesh()
        table = self.outs[3]
        return remote(table.at[0], table.at[k], [sem.at[k - 1] for sem in self.kept[2:4]], "tensor", lax.rem(shard + 4 - k, 4))


def gather_start(own, lines):
    exchange = Exchange(own, lines)
    near_a, near_h, far_a, far_h = Near(0, None, None), Near(0, None, None), Far(None), FarFirst(None)

    def body():
        for n, task in enumerate((near_a, near_h)):
            task.ins = [exchange.ins[n], exchange.outs[n]]
        far_a.ins, far_h.ins = [near_a.outs[0]], [near_h.outs[0]]
        greet()
        for n in (0, 3, 1, 2):
            exchange.swap(n).start()
        exchange.keep().start()
        exchange.swap(0).wait()
        near_a.start()
        exchange.keep().wait()
        exchange.swap(3).wait()
        for k in (1, 2, 3):
            exchange.spread(k).start()
        near_a.end()
        far_a.start()
        exchange.swap(1).wait()
        near_h.start()
        far_a.turn()
        far_a.rest()
        far_a.last()
        exchange.swap(2).wait()
        for k in (1, 2, 3):
            exchange.spread(k).wait()
        near_h.end()
        far_h.start()
        far_a.end()
        far_h.end()

    parts = [exchange, near_a, near_h, far_a, far_h]
    _, given = carried_call(
        body, parts, 0, grid=(), in_specs=[], inputs=(), out_specs=[], out_shape=[], scratch_shapes=[],
        name="gather_start", cost=pl.CostEstimate(flops=1 << 24, bytes_accessed=8 << 20, transcendentals=0),
    )
    others, given_a, given_h, far, first_h = given
    return others[:3], others[3], [given_a[0], *far], (given_h[0], first_h)


def onehot_of(rel_index):
    rel = jnp.pad(rel_index.T, ((0, WP - POS), (0, WP - POS)), constant_values=-1).reshape(-1)
    return (jnp.arange(2 * GL, dtype=jnp.int32)[:, None] == rel[None, :]).astype(BF)


def bias_tables(table, onehot):
    rows = table[:, :, TABLE : TABLE + 8].reshape(4, 2, 2, GH, GL).transpose(1, 0, 3, 2, 4).reshape(2 * H, 2 * GL)
    flat = jnp.dot(rows, onehot, preferred_element_type=F32)
    position = flat.reshape(2, 4, GH, WP, WP).transpose(0, 1, 3, 2, 4)
    shut = jnp.where(jnp.arange(WP) < POS, 0.0, SHUT).astype(F32)[:, None, None]
    return (position + shut).reshape(2, 4, WP, GH * WP)


def table_grad(gtab, rel_index):
    rel = jnp.pad(rel_index.T, ((0, WP - POS), (0, WP - POS)), constant_values=-1).reshape(-1)
    onehot = (rel[:, None] == jnp.arange(RELS, dtype=jnp.int32)[None, :]).astype(F32)
    flat = gtab.reshape(4, WP, GH, WP).transpose(0, 2, 1, 3).reshape(H, WP * WP)
    return jnp.dot(flat, onehot, precision=lax.Precision.HIGHEST).reshape(4, GH, RELS)


class Little(Part):
    def __init__(self, rows):
        self.rows = rows
        super().__init__(
            [],
            [jax.ShapeDtypeStruct((rows, GL), F32)],
            [pltpu.VMEM((2, 4, rows, GL), F32), pltpu.VMEM((4, rows, GL), F32), pltpu.VMEM((3, 4, rows, GL), F32),
             pltpu.VMEM((3, rows, GL), F32)]
            + sems() + sems(3) + sems(3) + [pltpu.SemaphoreType.DMA(())],
        )

    def pack(self, layers, tabs):
        _, _, shard = place_in_mesh()
        sums = self.kept[0]
        sums[...] = jnp.zeros_like(sums)
        for layer, (ghb, small_m, gqv, _, small_a) in enumerate(layers):
            for k in range(4):
                z = lax.rem(shard + k, 4)
                for row, source, n in (
                    (GAIN, small_a, 0), (SHIFT_ROW, small_a, 1), (OB, small_m, 0), (BPROJ, small_m, 1), (MGAIN, small_m, 2),
                    (MSHIFT, small_m, 3),
                ):
                    sums[layer, k, row : row + 1, :] = source[z, n : n + 1, :]
                sums[layer, k, QV : QV + 2, :] = gqv[k]
                sums[layer, k, HB : HB + 4, :] = ghb[k]
                rows = tabs[layer][GH * k : GH * (k + 1)]
                sums[layer, k, TABLE : TABLE + 4, :] = rows[:, 0:GL]
                sums[layer, k, TABLE + 4 : TABLE + 8, :] = rows[:, GL:]

    def over(self):
        core, _, _ = place_in_mesh()
        return remote(self.kept[0].at[1 - core], self.kept[1], self.kept[4:6], "pipe", 1 - core)

    def across(self, j):
        _, dp, _ = place_in_mesh()
        return remote(self.kept[1], self.kept[2].at[j - 1], [sem.at[j - 1] for sem in self.kept[6:8]], "dp", dp ^ j)

    def along(self, k):
        _, _, shard = place_in_mesh()
        return remote(
            self.kept[1].at[k], self.kept[3].at[k - 1], [sem.at[k - 1] for sem in self.kept[8:10]], "tensor", lax.rem(shard + k, 4)
        )

    def start(self):
        self.over().start()

    def second(self):
        core, _, _ = place_in_mesh()
        self.over().wait()
        self.kept[1][...] += self.kept[0][core]
        for j in (1, 2, 3):
            self.across(j).start()

    def third(self):
        for j in (1, 2, 3):
            self.across(j).wait()
        self.kept[1][...] += self.kept[2][0] + self.kept[2][1] + self.kept[2][2]
        for k in (1, 2, 3):
            self.along(k).start()

    def end(self):
        for k in (1, 2, 3):
            self.along(k).wait()
        self.kept[2][0, 0] = self.kept[1][0] + self.kept[3][0] + self.kept[3][1] + self.kept[3][2]
        copy = pltpu.make_async_copy(self.kept[2].at[0, 0], self.outs[0], self.kept[10])
        copy.start()
        copy.wait()


class Settle(Part):
    def __init__(self):
        super().__init__(
            [],
            [jax.ShapeDtypeStruct((3, D, D), BF)],
            [pltpu.VMEM((3, D, D), BF)] + sems(3) + [pltpu.SemaphoreType.DMA((3,)), pltpu.SemaphoreType.DMA((3,))],
        )

    def rows(self, core):
        return pl.ds(core * 256, 256)

    def send(self, source, n, core):
        return remote(source.at[self.rows(core)], self.outs[0].at[n, self.rows(core)], [sem.at[n] for sem in self.kept[1:3]], "pipe", 1 - core)

    def load(self, source, n, core):
        return pltpu.make_async_copy(source.at[self.rows(core)], self.kept[0].at[n, self.rows(core)], self.kept[3].at[n])

    def store(self, n, core):
        return pltpu.make_async_copy(self.kept[0].at[n, self.rows(core)], self.outs[0].at[n, self.rows(core)], self.kept[4].at[n])

    def start(self, matrices, layer, which):
        def action(core):
            for n in which:
                (self.load if core == layer else self.send)(matrices[n], n, core).start()

        by_core(action)

    def pass_on(self, matrices, layer, which):
        @pl.when(lax.axis_index("pipe") == layer)
        def _():
            for n in which:
                self.load(matrices[n], n, layer).wait()
                self.store(n, layer).start()

    def end(self, matrices):
        def action(core):
            for n in range(3):
                self.store(n, core).wait()
                self.send(matrices[1 - core][n], n, core).wait()

        by_core(action)


def table_sums(gtab_ref, onehot_ref, half_ref, pairs_ref, out_ref):
    for g in range(4):
        for n in range(2):
            half_ref[...] = gtab_ref[g, :, n * GL : (n + 1) * GL]
            even = half_ref[pl.ds(0, WP // 2, 2), :]
            odd = half_ref[pl.ds(1, WP // 2, 2), :]
            for m in range(2):
                lanes = slice(m * WP, (m + 1) * WP)
                pairs_ref[:, g * GH + 2 * n + m, :] = jnp.concatenate([even[:, lanes], odd[:, lanes]], 1)

    def add(n, total):
        pair = pairs_ref[n]
        high = pair.astype(BF)
        low = (pair - high.astype(F32)).astype(BF)
        places = onehot_ref[:, pl.ds(pl.multiple_of(n * GL, GL), GL)]
        return total + (dot_nt(high, places) + dot_nt(low, places))

    out_ref[...] = lax.fori_loop(0, WP // 2, add, jnp.zeros((H, 2 * GL), F32))


def reduce_end(attention0, turned0, totals_a1, shared1, grads_in, small, onehot):
    halves = ((0, 32), (32, 32))
    first = [ReduceFirst(attention0, rows=rows) for rows in halves]
    second = [ReduceSecond(size=32) for _ in halves]
    share = [Share(rows=halves[0])]
    share.append(Share(rows=halves[1], target=share[0]))
    onward_m = [ReduceOnward(given) for given in turned0]
    second_m, share_m = [ReduceSecond(), ReduceSecond()], [Share(), Share()]
    second_a1, share_a1, done_m1 = ReduceSecond(totals_a1), Share(), Part(shared1)
    settle, little, deliver, places = Settle(), Little(24), Deliver(grads_in), Stored(onehot)

    def body(*refs):
        layers, (tabs_ref, pairs_ref, half_ref) = (refs[:5], refs[5:10]), refs[10:]
        for n in range(2):
            second[n].ins, share[n].ins = [first[n].total], [second[n].kept[0]]
            second_m[n].ins, share_m[n].ins = [onward_m[n].kept[0]], [second_m[n].kept[0]]
        share_a1.ins = [second_a1.kept[0]]
        done = (
            [share[0].outs[0], share_m[0].outs[0], share_m[1].outs[0]],
            [share_a1.outs[0], done_m1.ins[0], done_m1.ins[1]],
        )

        def tab(layer):
            table_sums(layers[layer][3], places.kept[0], half_ref, pairs_ref, tabs_ref.at[layer])

        greet()
        for task in (*first, *onward_m):
            task.start()
        places.load()
        first[0].cores()
        first[1].cores()
        second_a1.start()
        settle.start(done[1], 1, (1, 2))
        deliver.start()
        places.wait()
        tab(1)
        for n in range(2):
            onward_m[n].close()
            second_m[n].start()
        first[0].turn()
        tab(0)
        little.pack(layers, tabs_ref)
        little.start()
        first[1].turn()
        second_a1.close()
        share_a1.start()
        settle.pass_on(done[1], 1, (1, 2))
        first[0].close()
        second[0].start()
        little.second()
        first[1].close()
        second[1].start()
        for n in range(2):
            second_m[n].close()
            share_m[n].start()
        share_a1.end()
        settle.start(done[1], 1, (0,))
        little.third()
        settle.pass_on(done[1], 1, (0,))
        for n in range(2):
            second[n].close()
            share[n].start()
        for n in range(2):
            share_m[n].end()
        settle.start(done[0], 0, (1, 2))
        little.end()
        deliver.end()
        settle.pass_on(done[0], 0, (1, 2))
        for n in range(2):
            share[n].end()
        settle.start(done[0], 0, (0,))
        settle.pass_on(done[0], 0, (0,))
        settle.end(done)

    parts = [*first, *second, *share, *onward_m, *second_m, *share_m, second_a1, share_a1, done_m1, settle, little, deliver, places]
    _, given = carried_call(
        body, parts, 7, grid=(), in_specs=[pl.BlockSpec(memory_space=pltpu.VMEM)] * 10, inputs=small, out_specs=[], out_shape=[],
        scratch_shapes=[pltpu.VMEM((2, H, 2 * GL), F32), pltpu.VMEM((WP // 2, H, GL), F32), pltpu.VMEM((WP, GL), F32)],
        name="reduce_end", cost=pl.CostEstimate(flops=1 << 24, bytes_accessed=8 << 20, transcendentals=0),
    )
    by_part = dict(zip(map(id, parts), given))
    return by_part[id(settle)][0], by_part[id(little)][0], by_part[id(deliver)][0]


def finish_body(
    matrix_ref, lines_ref, out0_ref, out1_ref, out_came_ref, gin0_ref, gin1_ref, gin_came_ref,
    block_out_ref, input_grad_ref, gqkv_ref, gproj_ref, ghw_ref, gow_ref, gain_ref, shift_ref, qv_ref, table_ref, bproj_ref,
    mgain_ref, mshift_ref, hb_ref, ob_ref,
):
    def images(core):
        for ref, own, came in (
            (block_out_ref, (out0_ref, out1_ref), out_came_ref), (input_grad_ref, (gin0_ref, gin1_ref), gin_came_ref)
        ):
            ref[0, 0, core] = own[core][0]
            ref[0, 0, 1 - core] = came[0]

    by_core(images)

    @pl.when(pl.program_id(0) == 0)
    def _():
        gqkv_ref[0] = dot_nn(matrix_ref[0, :, : 3 * GL], permutation(3 * GL, qkv_source, True))
        gproj_ref[0] = matrix_ref[0, :, 3 * GL :].T.astype(F32)
        lines = lines_ref[...]
        for row, ref in (
            (GAIN, gain_ref), (SHIFT_ROW, shift_ref), (BPROJ, bproj_ref), (MGAIN, mgain_ref), (MSHIFT, mshift_ref), (OB, ob_ref)
        ):
            ref[...] = lines[row : row + 1]
        qv_ref[...] = jnp.concatenate(
            [lines[QV + n : QV + n + 1, h * HD : (h + 1) * HD] for h in range(GH) for n in range(2)], 1
        )
        table_ref[0] = jnp.concatenate([lines[TABLE : TABLE + 4], lines[TABLE + 4 : TABLE + 8, : RELS - GL]], 1)
        hb_ref[...] = jnp.concatenate([lines[HB + n : HB + n + 1] for n in range(4)], 1)

    @pl.when(pl.program_id(0) == 1)
    def _():
        ghw_ref[0] = matrix_ref[1].astype(F32)
        gow_ref[0] = matrix_ref[2].T.astype(F32)


def finish(matrices, lines, out0, out1, out_came, gin0, gin1, gin_came):
    n = out0.shape[0]
    image = per((TOK, D))
    both = pl.BlockSpec((1, 1, 2, TOK, D), lambda i: (0, i, 0, 0, 0))
    shapes = [
        (1, D, 3 * GL), (1, GL, D), (1, D, D), (1, D, D), (1, GL), (1, GL), (1, 2 * GL), (1, GH, RELS), (1, GL), (1, GL), (1, GL),
        (1, D), (1, GL),
    ]
    return plain_call(
        finish_body, "finish", (matrices, lines, out0, out1, out_came, gin0, gin1, gin_came),
        [jax.ShapeDtypeStruct((1, n, 2, TOK, D), BF)] * 2 + [jax.ShapeDtypeStruct(shape, F32) for shape in shapes],
        grid=(n,),
        in_specs=[whole(matrices.shape), whole(lines.shape)] + [image] * 6,
        out_specs=[both, both] + [whole(shape) for shape in shapes],
    )


def layer_forward(layer, rolled, x, counts, table, bias, weights, tasks, ids):
    (fw, qkv, p, ho, mid), given = attn_fwd(layer, rolled, x, table, bias, weights[0](), tasks[0](), ids[0])
    mid = mid.reshape(-1, D)
    kept_a, given = given[0], given[1:]
    (second, act, slope, y, out), more = mlp_fwd(layer, rolled, counts, mid, table, weights[1](given), tasks[1](given), ids[1])
    return y, out, (x, fw, qkv, p, ho, mid, second, act, slope, kept_a, more[0]), given, more[1:]


def layer_backward(layer, rolled, cot, kept, counts, table, tasks, ids):
    x, fw, qkv, p, ho, mid, second, act, slope, kept_a, kept_m = kept
    if not layer:
        cot = cot.reshape(-1, TP, D)
    (ghw, ghw_away, gow, gow_away, ghb, gmid, small_m), given = mlp_bwd(
        layer, rolled, counts, cot, act, slope, second, mid, table, Stored(*kept_m), tasks[0](), ids[0]
    )
    big_m = ((ghw, ghw_away), (gow, gow_away))
    (gin, out, ga, ga_away, gqv, gtab, small_a), more = attn_bwd(
        layer, rolled, x, gmid.reshape(-1, TP, D), fw, qkv, p, ho, table, Stored(*kept_a), tasks[1](big_m, given), ids[1]
    )
    return gin, out, ((ga, ga_away), *big_m), (ghb, small_m, gqv, gtab, small_a), given, more


SMALL_ROWS = ((GAIN, 1), (SHIFT_ROW, 1), (QV, 2), (TABLE, 8), (BPROJ, 1), (MGAIN, 1), (MSHIFT, 1), (HB, 4), (OB, 1))


def on_lines(small_in):
    whole_of = [lax.all_gather(lax.all_gather(member[0], "tensor", axis=0, tiled=True), "pipe") for member in small_in]
    gain, shift, qv, table, bproj, mgain, mshift, hb, ob = whole_of

    def lines(member):
        return member.reshape(2, 4, -1, GL)

    qv = qv.reshape(2, 4, GH, 2, HD).transpose(0, 1, 3, 2, 4)
    table = jnp.pad(table, ((0, 0), (0, 0), (0, 2 * GL - RELS))).reshape(2, 4, GH, 2, GL).transpose(0, 1, 3, 2, 4)
    rows = jnp.concatenate([lines(part) for part in (gain, shift, qv, table, bproj, mgain, mshift, hb, ob)], 2)
    return jnp.pad(rows, ((0, 0), (0, 0), (0, LINES - rows.shape[2]), (0, 0))).transpose(1, 0, 2, 3)


def qkv_order(w):
    lead = w.shape[:-1]
    return jnp.swapaxes(w.reshape(*lead, GH, 3, HD), -3, -2).reshape(*lead, 3 * GL)


def general(core, images, cotangent, counts, rel_index, small_in, big_in):
    def both(member, axis):
        return lax.all_gather(lax.all_gather(member[0], "tensor", axis=axis, tiled=True), "pipe")

    table = on_lines(small_in)
    bias = bias_tables(table, onehot_of(rel_index))
    gathered = [both(member, axis) for member, axis in zip(big_in, (1, 0, 1, 0))]
    weights = []
    for l in range(2):
        wqkv, wproj, hw, ow = (pair[l] for pair in gathered)
        wqkv = qkv_order(wqkv.reshape(D, 4, 3 * GL).transpose(1, 0, 2))
        wa = jnp.concatenate([wqkv, wproj.reshape(4, GL, D).transpose(0, 2, 1)], 2)[None]
        wm = jnp.stack([hw.reshape(D, 4, -1).transpose(1, 0, 2), ow.reshape(4, -1, D)])
        weights.append((lambda *_, wa=wa: Weights(1, 0, whole=wa), lambda *_, wm=wm: Weights(2, 0, whole=wm)))
    none, back_none, ids = (lambda: [], lambda given: []), (lambda: [], lambda *_: []), (None, None)
    y0, out0, kept0, _, _ = layer_forward(0, False, images, counts, table, bias[0], weights[0], none, ids)
    _, out1, kept1, _, _ = layer_forward(1, False, y0, counts, table, bias[1], weights[1], none, ids)
    g1, gin1, big1, small1, _, _ = layer_backward(1, False, cotangent, kept1, counts, table, back_none, ids)
    _, gin0, big0, small0, _, _ = layer_backward(0, False, g1, kept0, counts, table, back_none, ids)
    first_core = core == 0

    def deliver(mine0, mine1):
        came = lax.ppermute(jnp.where(first_core, mine1, mine0), "pipe", [(0, 1), (1, 0)])
        mine = jnp.where(first_core, mine0, mine1)
        return jnp.stack([jnp.where(first_core, mine, came), jnp.where(first_core, came, mine)], 1)[None]

    def matrix_of(pair):
        parts = [part[jnp.array([PLACES.index(j) for j in range(4)])] for part in pair]
        return jnp.concatenate(parts).transpose(1, 0, 2, 3).reshape(4, D, D)

    def full(big):
        ga, ghw, gow = (matrix_of(pair) for pair in big)
        gqkv = jnp.swapaxes(ga[:, :, : 3 * GL].reshape(4, D, 3, GH, HD), 2, 3).reshape(4, D, 3 * GL)
        return (
            gqkv.transpose(1, 0, 2).reshape(D, 3 * D), ga[:, :, 3 * GL :].transpose(0, 2, 1).reshape(D, D),
            ghw.transpose(1, 0, 2).reshape(D, -1), gow.transpose(0, 2, 1).reshape(-1, D),
        )

    def reduced(pair, axis):
        mine = lax.psum_scatter(jnp.stack(pair), "pipe", scatter_dimension=0, tiled=False)
        mine = lax.psum_scatter(mine, "tensor", scatter_dimension=axis, tiled=True)
        return lax.psum(mine, "dp").astype(F32)[None]

    gqkv, gproj, ghw, gow = (reduced(pair, axis) for pair, axis in zip(zip(full(big0), full(big1)), (1, 0, 1, 0)))

    def vectors(terms):
        ghb, small_m, gqv, gtab, small_a = terms
        qv = jnp.swapaxes(gqv.reshape(4, 2, GH, HD), 1, 2).reshape(-1)
        tab = table_grad(gtab, rel_index).reshape(H, RELS)
        parts = (small_a[:, 0], small_a[:, 1], qv, tab, small_m[:, 1], small_m[:, 2], small_m[:, 3], ghb, small_m[:, 0])
        return jnp.concatenate([part.reshape(-1) for part in parts])

    totals = lax.psum(jnp.stack([vectors(small0), vectors(small1)]), ("pipe", "dp", "tensor"))
    mine = jnp.where(first_core, totals[0], totals[1])
    outs, at = [], 0
    for member in small_in:
        shape = member.shape[1:]
        whole_shape = (shape[0] * lax.axis_size("tensor"),) + tuple(shape[1:])
        size = math.prod(whole_shape)
        piece = mine[at : at + size].reshape(whole_shape)
        outs.append(lax.dynamic_slice_in_dim(piece, lax.axis_index("tensor") * shape[0], shape[0], 0)[None])
        at += size
    return deliver(out0, out1), deliver(gin0, gin1), (gqkv, gproj, ghw, gow), outs


def four_by_four(images, cotangent, counts, rel_index, small_in, big_in):
    own_a, lines = prepare(big_in[0][0], big_in[1][0], *[member[0] if member.ndim == 3 else member for member in small_in])
    own = (own_a, big_in[2][0], big_in[3][0])
    onehot = onehot_of(rel_index)
    other, table, pieces_a0, hidden0 = gather_start(own, lines)
    bias = bias_tables(table, onehot)

    def near(n, layer, **how):
        return Near(layer, own[n], other[n], **how)

    def weights(layer, which, pieces):
        return Weights(len(which), layer, own=[own[n] for n in which], other=[other[n] for n in which], pieces=pieces)

    def out_tasks(layer):
        near_o = near(2, layer, plan=((1, "finish"),))
        far_o = Far(None, source=near_o, deferred=True, plan=((1, "start"), (2, "turn"), (3, "rest"), (3, "last")))
        return [near_o, far_o]

    def weights_of_first(layer, pieces):
        return lambda: weights(layer, (0,), [pieces])

    y0, out0, kept0, given, more = layer_forward(
        0, True, images, counts, table, bias[0],
        (weights_of_first(0, pieces_a0),
         lambda given: weights(0, (1, 2), [gathered(*hidden0, given[1]), [given[2][0], *given[3]]])),
        (lambda: [FarSecond(hidden0[1], plan=((1, "last"),)), *out_tasks(0), near(0, 1, deferred=True, plan=((2, "start"),))],
         lambda given: [Far(given[4][0], plan=((1, "turn"), (3, "rest"), (3, "last"))), near(1, 1, deferred=True, plan=((1, "start"),))]),
        (1, 2),
    )
    pieces_a1, near_h1 = [given[4][0], *more[1]], more[2][0]
    _, out1, kept1, _, _ = layer_forward(
        1, True, y0, counts, table, bias[1],
        (weights_of_first(1, pieces_a1),
         lambda given: weights(1, (1, 2), [[near_h1, *given[1]], [given[2][0], *given[3]]])),
        (lambda: [Far(near_h1, plan=((1, "turn"), (2, "rest"), (2, "last"))), *out_tasks(1)], lambda given: []), (3, None),
    )

    def mlp_reduce(big_m):
        return [ReduceTurn(big_m[0], plan=((0, "cores"),)), ReduceTurn(big_m[1], plan=((1, "cores"),))]

    g1, gin1, big1, small1, given, more = layer_backward(
        1, True, cotangent, kept1, counts, table, (lambda: [Deliver([out0, out1])], lambda big_m, given: mlp_reduce(big_m)), (4, 5)
    )
    out_came, turned1 = given[1][0], more[1:3]

    def last_tasks(big_m, given):
        seconds = [ReduceSecond(given[2][0], plan=((1, "close"),)), ReduceSecond(given[3][0], plan=((LATE, "close"),))]
        shares = [Share(source=seconds[0], plan=((1, "start"),)), Share(source=seconds[1], plan=((LATE, "start"),))]
        return [*mlp_reduce(big_m), ReduceOnward(given[1]), *seconds, *shares]

    _, gin0, big0, small0, given, more = layer_backward(
        0, True, g1, kept0, counts, table,
        (
            lambda: [ReduceTurn(big1[0], plan=((0, "cores"),)), *[ReduceOnward(turned) for turned in turned1]],
            last_tasks,
        ),
        (6, 8),
    )
    turned0, totals_a1, shared1 = more[1:3], more[3][0], (more[6][0], more[7][0])
    matrices, lines, gin_came = reduce_end(big0[0], turned0, totals_a1, shared1, [gin0, gin1], [*small0, *small1], onehot)
    block_out, input_grad, gqkv, gproj, ghw, gow, *outs = finish(matrices, lines, out0, out1, out_came, gin0, gin1, gin_came)
    return block_out, input_grad, (gqkv, gproj, ghw, gow), outs


def local(
    images, cotangent, counts, rel_index, pre_attn_gain, pre_attn_bias, qkv_weight, qv_bias, bias_table, proj_weight, proj_bias,
    pre_mlp_gain, pre_mlp_bias, hidden_weight, hidden_bias, out_weight, out_bias,
):
    assert images.shape[1] == 2, images.shape
    small_in = (pre_attn_gain, pre_attn_bias, qv_bias, bias_table, proj_bias, pre_mlp_gain, pre_mlp_bias, hidden_bias, out_bias)
    big_in = (qkv_weight, proj_weight, hidden_weight, out_weight)
    if lax.axis_size("tensor") == 4 and lax.axis_size("dp") == 4:
        block_out, input_grad, big, small = four_by_four(images, cotangent, counts, rel_index, small_in, big_in)
    else:
        block_out, input_grad, big, small = general(
            lax.axis_index("pipe"), images, cotangent, counts, rel_index, small_in, big_in
        )
    gqkv, gproj, ghw, gow = big
    gain_g, shift_g, qv_g, table_g, bproj_g, mgain_g, mshift_g, hb_g, ob_g = small
    return (
        block_out, input_grad, gain_g, shift_g, gqkv, qv_g, table_g, gproj, bproj_g, mgain_g, mshift_g, ghw, hb_g, gow, ob_g,
    )


def solution(mesh):
    return jax.shard_map(
        local,
        mesh=mesh,
        in_specs=(
            P(None, ("dp", "tensor"), None, None),
            P(None, ("dp", "tensor"), None, None),
            P(None, "dp"),
            P(),
            P("pipe", "tensor"),
            P("pipe", "tensor"),
            P("pipe", None, "tensor"),
            P("pipe", "tensor"),
            P("pipe", "tensor", None),
            P("pipe", "tensor", None),
            P("pipe", "tensor"),
            P("pipe", "tensor"),
            P("pipe", "tensor"),
            P("pipe", None, "tensor"),
            P("pipe", "tensor"),
            P("pipe", "tensor", None),
            P("pipe", "tensor"),
        ),
        out_specs=(
            P("pipe", None, ("dp", "tensor"), None, None),
            P("pipe", None, ("dp", "tensor"), None, None),
            P("pipe", "tensor"),
            P("pipe", "tensor"),
            P("pipe", None, "tensor"),
            P("pipe", "tensor"),
            P("pipe", "tensor", None),
            P("pipe", "tensor", None),
            P("pipe", "tensor"),
            P("pipe", "tensor"),
            P("pipe", "tensor"),
            P("pipe", None, "tensor"),
            P("pipe", "tensor"),
            P("pipe", "tensor", None),
            P("pipe", "tensor"),
        ),
        check_vma=False,
    )
```

time: 815 us -> 265 us (0.33); the launches traced: 806 us -> 264 us
  waiting for transfers between devices: 422 us -> 0 us
  local copies, waits for them, and re-layouts: 137 us -> 13.1 us
  Pallas kernels: 145 us -> 247 us
  blocking collectives: 42.3 us -> 0 us
  other arithmetic: 33.8 us -> 2.5 us
  between operations: 16 us -> 0.84 us
    psum x2 -> x0, waiting for transfers between devices: 177 us -> none  [the longest x1 125 us: local(): lax.psum(jnp.stack([pack_small(little(little0)), pack_small(little(little...]
    reduce_scatter x7 -> x0, waiting for transfers between devices: 115 us -> none  [the longest x3 110 us: reduced(): mine = lax.psum_scatter(mine, 'tensor', scatter_dimension=axis, tiled=True)]
    pallas_call x8 -> x12, Pallas kernels: 145 us -> 247 us  [the longest x10 237 us: carried_call(): pl.pallas_call(whole_body, grid_spec=pltpu.PrefetchScalarGridSpec(num_sca...]
    all_gather x7 -> x0, waiting for transfers between devices: 89.4 us -> none  [the longest x3 82.2 us: both(): lax.all_gather(member[0], 'tensor', axis=axis, tiled=True)]
    unnamed x18 -> x0, waiting for transfers between devices: 40.3 us -> none
    unnamed x177 -> x16, local copies, waits for them, and re-layouts: 38.4 us -> 10 us
    transpose x8 -> x1, local copies, waits for them, and re-layouts: 26.6 us -> 0.01 us  [bias_tables(): table[:, :, TABLE:TABLE + 8].reshape(4, 2, 2, GH, GL)]
    all_gather x2 -> x0, blocking collectives: 24.6 us -> none  [the longest x1 22.8 us: both(): lax.all_gather(member[0], 'tensor', axis=axis, tiled=True)]
  transfers between devices with their start and end apart: 19 -> 0, of which waited for: 11 -> 0; matrix products, arithmetic and copies ran while one was open for 16% -> 0% of each run, Pallas kernels for 2% -> 0%
where the time goes in v2:
time: 265 us; the launch traced here: 264 us
  Pallas kernels  247 us (93%)
  local copies, waits for them, and re-layouts  13.1 us (5%)
    pallas_call x10, Pallas kernels, carried_call(): pl.pallas_call(whole_body, grid_spec=pltpu.PrefetchScalarGridSpec(num_sca...  237 us
    unnamed x16, local copies, waits for them, and re-layouts  10 us
    pallas_call x2, Pallas kernels, plain_call(): pl.pallas_call(body, grid=grid, out_shape=out_shape, in_specs=in_specs or...  9.43 us

profile of v2, /device:TPU:0, one launch (start us, length us, event | category | flops | bytes accessed | tf_op | source)
XLA Modules:
  0.0 264.3 jit_solution(961199395204605266)
XLA Ops:
  0.7 0.0 copy-start.3
  0.7 2.4 prepare.1
  3.0 31.0 %gather_start.1 = (bf16[512,512]{1,0:T(8,128)(2,1)}, bf16[512,512]{1,0:T(8,128)(2,1)}, bf16[512,512]{1,0:T(8,128)(2,1)}, bf16[4,2,32,128]{3,2,1,0:T(8,128)(2,1)}...) custom-call(bf16[512,512]{1,0:T(8,128)(2,1)} %get-tuple-element.155., ...), custom_call_target="tpu_custom_call" | custom-call | flops 16777216 | bytes 8388608 | tf_op jit(solution)/shard_map/gather_start/pallas_call | solution.py:647
  34.0 0.8 slice.11
  34.8 0.0 copy-done.3
  34.8 0.1 copy.55
  34.9 0.1 eq.31
  35.0 0.7 iota_compare_fusion.1
  35.8 0.0 copy-start.1
  35.8 1.1 fusion.1
  36.9 0.1 fusion.3
  36.9 1.0 squeeze.26.refs_2_
  38.0 0.0 copy-done.1
  38.0 1.4 copy.44.refs_0_
  39.4 0.0 copy-start.4
  39.4 24.2 %attn_fwd.2 = (bf16[4,256,512]{2,1,0:T(8,128)(2,1)}, bf16[4,256,1536]{2,1,0:T(8,128)(2,1)}, bf16[4,4,4,64,256]{4,3,2,1,0:T(8,128)(2,1)}, bf16[4,208,512]{2,1,0:T...) custom-call(bf16[4,2,196,512]{3,2,1,0:T(8,128)(2,1)} %copy.44.refs_0, ...), custom_call_target="tpu_custom_call" | custom-call | flops 2726297600 | bytes 8388608 | tf_op jit(solution)/shard_map/attn_fwd/pallas_call | solution.py:647
  63.6 0.0 copy-done.4
  63.6 0.7 copy.49.refs_0_
  64.3 17.2 %mlp_fwd.2 = (bf16[832,512]{1,0:T(8,128)(2,1)}, bf16[4,832,512]{2,1,0:T(8,128)(2,1)}, bf16[4,832,512]{2,1,0:T(8,128)(2,1)}, bf16[4,208,512]{2,1,0:T(8,128)(2,1)}...) custom-call(s32[4,1]{1,0:T(4,128)} %copy.49.refs_0_, ...), custom_call_target="tpu_custom_call" | custom-call | flops 3489660928 | bytes 12582912 | tf_op jit(solution)/shard_map/mlp_fwd/pallas_call | solution.py:647
  81.5 1.0 squeeze.27.refs_2_
  82.5 23.0 %attn_fwd.3 = (bf16[4,256,512]{2,1,0:T(8,128)(2,1)}, bf16[4,256,1536]{2,1,0:T(8,128)(2,1)}, bf16[4,4,4,64,256]{4,3,2,1,0:T(8,128)(2,1)}, bf16[4,208,512]{2,1,0:T...) custom-call(bf16[4,208,512]{2,1,0:T(8,128)(2,1)} %get-tuple-element., ...), custom_call_target="tpu_custom_call" | custom-call | flops 2726297600 | bytes 8388608 | tf_op jit(solution)/shard_map/attn_fwd/pallas_call | solution.py:647
  105.5 0.0 copy-start.2
  105.5 11.1 %mlp_fwd.3 = (bf16[832,512]{1,0:T(8,128)(2,1)}, bf16[4,832,512]{2,1,0:T(8,128)(2,1)}, bf16[4,832,512]{2,1,0:T(8,128)(2,1)}, bf16[4,208,512]{2,1,0:T(8,128)(2,1)}...) custom-call(s32[4,1]{1,0:T(4,128)} %copy.49.refs_0_, f32[832,512]{1,0:T(8,128)} %bitcast.41, ...), custom_call_target="tpu_custom_call" | custom-call | flops 3489660928 | bytes 12582912 | tf_op jit(solution)/shard_map/mlp_fwd/pallas_call | solution.py:647
  116.6 0.0 copy-done.2
  116.6 1.5 copy.48.refs_1_
  118.1 17.8 %mlp_bwd.2 = (bf16[4,4,64,512]{3,2,1,0:T(8,128)(2,1)}, bf16[4,4,64,512]{3,2,1,0:T(8,128)(2,1)}, bf16[4,4,64,512]{3,2,1,0:T(8,128)(2,1)}, bf16[4,4,64,512]{3,2,1,...) custom-call(s32[4,1]{1,0:T(4,128)} %copy.49.refs_0_, ...), custom_call_target="tpu_custom_call" | custom-call | flops 6979321856 | bytes 16777216 | tf_op jit(solution)/shard_map/mlp_bwd/pallas_call | solution.py:647
  135.9 23.3 %attn_bwd.2 = (bf16[4,208,512]{2,1,0:T(8,128)(2,1)}, bf16[4,196,512]{2,1,0:T(8,128)(2,1)}, bf16[4,4,64,512]{3,2,1,0:T(8,128)(2,1)}, bf16[4,4,64,512]{3,2,1,0:T(8...) custom-call(bf16[4,208,512]{2,1,0:T(8,128)(2,1)} %get-tuple-element., ...), custom_call_target="tpu_custom_call" | custom-call | flops 5452595200 | bytes 12582912 | tf_op jit(solution)/shard_map/attn_bwd/pallas_call | solution.py:647
  159.2 21.8 %mlp_bwd.3 = (bf16[4,4,64,512]{3,2,1,0:T(8,128)(2,1)}, bf16[4,4,64,512]{3,2,1,0:T(8,128)(2,1)}, bf16[4,4,64,512]{3,2,1,0:T(8,128)(2,1)}, bf16[4,4,64,512]{3,2,1,...) custom-call(s32[4,1]{1,0:T(4,128)} %copy.49.refs_0_, ...), custom_call_target="tpu_custom_call" | custom-call | flops 6979321856 | bytes 16777216 | tf_op jit(solution)/shard_map/mlp_bwd/pallas_call | solution.py:647
  181.0 28.4 %attn_bwd.3 = (bf16[4,208,512]{2,1,0:T(8,128)(2,1)}, bf16[4,196,512]{2,1,0:T(8,128)(2,1)}, bf16[4,4,64,512]{3,2,1,0:T(8,128)(2,1)}, bf16[4,4,64,512]{3,2,1,0:T(8...) custom-call(bf16[4,2,196,512]{3,2,1,0:T(8,128)(2,1)} %copy.44.refs_0, ...), custom_call_target="tpu_custom_call" | custom-call | flops 5452595200 | bytes 12582912 | tf_op jit(solution)/shard_map/attn_bwd/pallas_call | solution.py:647
  209.5 1.8 fusion.refs_23_
  211.2 39.6 %reduce_end.1 = (bf16[4,32,512]{2,1,0:T(8,128)(2,1)}, bf16[4,32,512]{2,1,0:T(8,128)(2,1)}, bf16[32,512]{1,0:T(8,128)(2,1)}, bf16[32,512]{1,0:T(8,128)(2,1)}, bf1...) custom-call(f32[4,4,128]{2,1,0:T(4,128)} %get-tuple-element.240.refs, ...), custom_call_target="tpu_custom_call" | custom-call | flops 16777216 | bytes 8388608 | tf_op jit(solution)/shard_map/reduce_end/pallas_call | solution.py:647
  250.9 7.1 %finish.1 = (bf16[1,4,2,196,512]{4,3,2,1,0:T(8,128)(2,1)}, bf16[1,4,2,196,512]{4,3,2,1,0:T(8,128)(2,1)}, f32[1,512,384]{2,1,0:T(8,128)}, f32[1,128,512]{2,1,0:T(...) custom-call(bf16[3,512,512]{2,1,0:T(8,128)(2,1)} %get-tuple-element., ...), custom_call_target="tpu_custom_call" | custom-call | flops 4194304 | bytes 4194304 | tf_op jit(solution)/shard_map/finish/pallas_call | solution.py:1245
  257.9 0.0 copy-start
  258.0 3.9 %copy.51 = bf16[1,4,2,196,512]{4,2,3,1,0:T(2,128)(2,1)} copy(bf16[1,4,2,196,512]{4,3,2,1,0:T(8,128)(2,1)} %get-tuple-element.310) | data formatting | bytes 3211264
  261.9 0.0 copy-done
  261.9 2.4 copy.52
  (4 shorter events, 0.0 us)
Async XLA Ops:
  0.7 34.2 %copy-start.3 = (s32[49,49]{1,0:T(8,128)S(1)}, s32[49,49]{1,0:T(8,128)}, u32[]{:S(2)}) copy-start(s32[49,49]{1,0:T(8,128)} %param.20) | copy-start | bytes 28816
  35.8 2.2 copy-start.1
  39.4 24.2 %copy-start.4 = (s32[4,1]{0,1:T(1,128)S(1)}, s32[4,1]{0,1:T(1,128)}, u32[]{:S(2)}) copy-start(s32[4,1]{0,1:T(1,128)} %param.19) | copy-start | bytes 52
  105.5 11.1 %copy-start.2 = (bf16[4,2,196,512]{3,1,2,0:T(2,128)(2,1)S(1)}, bf16[4,2,196,512]{3,1,2,0:T(2,128)(2,1)}, u32[]{:S(2)}) copy-start(bf16[4,2,196,512]{3,1,2,0:T(2,128)(2,1)} %param.18) | copy-start | bytes 4816900
  257.9 4.0 %copy-start = (bf16[1,4,2,196,512]{4,3,2,1,0:T(8,128)(2,1)S(1)}, bf16[1,4,2,196,512]{4,3,2,1,0:T(8,128)(2,1)}, u32[]{:S(2)}) copy-start(bf16[1,4,2,196,512]{4,3,2,1,0:T(8,128)(2,1)} %get-tuple-element.311) | copy-start | bytes 4816900

commit v3 on v2

--- a/solution.py
+++ b/solution.py
@@ -118,6 +118,9 @@
     plan = ()
     deferred = False
 
+    def flush(self):
+        pass
+
     def __init__(self, inputs=(), outputs=(), scratch=()):
         self.inputs, self.outputs, self.scratch = list(inputs), list(outputs), list(scratch)
 
@@ -166,6 +169,10 @@
                     self.shard(core == self.layer, b).start()
 
             by_core(shards)
+        if self.count == 1:
+            self.load_rest()
+
+    def load_rest(self):
         for copy in self.rest():
             copy.start()
 
@@ -290,70 +297,6 @@
     def end(self):
         for j in range(4):
             self.over(j).wait()
-
-
-class FarFirst(Part):
-    def __init__(self, near, plan=(), source=None, deferred=False):
-        self.plan, self.source, self.deferred = plan, source, deferred
-        shape = jax.ShapeDtypeStruct((3, CHUNK, D), BF)
-        super().__init__([] if near is None else [near], [shape] * 5, sems(2) + sems(3))
-
-    def across(self, j):
-        _, dp, _ = place_in_mesh()
-        return remote(self.ins[0], self.outs[j - 1], [sem.at[j - 1] for sem in self.kept[:2]], "dp", dp ^ j)
-
-    def over(self, j):
-        core, _, _ = place_in_mesh()
-        source = self.ins[0] if j == 0 else self.outs[j - 1]
-        return remote(source, self.outs[2 + j], [sem.at[j] for sem in self.kept[2:]], "pipe", 1 - core)
-
-    def start(self):
-        for j in (1, 2):
-            self.across(j).start()
-        self.over(0).start()
-
-    def end(self):
-        for j in (1, 2):
-            self.across(j).wait()
-            self.over(j).start()
-        for j in range(3):
-            self.over(j).wait()
-
-
-class FarSecond(Part):
-    def __init__(self, first, plan=()):
-        self.plan = plan
-        shape = jax.ShapeDtypeStruct((3, CHUNK, D), BF)
-        super().__init__(first[:2], [shape] * 2, sems(2) + sems())
-
-    def onward(self, j):
-        _, dp, _ = place_in_mesh()
-        rows = pl.ds((j - 1) * 32, 32)
-        return remote(
-            self.ins[j - 1].at[:, rows], self.outs[0].at[:, rows], [sem.at[j - 1] for sem in self.kept[:2]], "dp", dp ^ (3 - j)
-        )
-
-    def over(self):
-        core, _, _ = place_in_mesh()
-        return remote(self.outs[0], self.outs[1], self.kept[2:], "pipe", 1 - core)
-
-    def start(self):
-        for j in (1, 2):
-            self.onward(j).start()
-
-    def last(self):
-        for j in (1, 2):
-            self.onward(j).wait()
-        self.over().start()
-
-    def end(self):
-        if not any(what == "last" for _, what in self.plan):
-            self.last()
-        self.over().wait()
-
-
-def gathered(near, first, second):
-    return [near, *first[:2], second[0], *first[2:], second[1]]
 
 
 class ReduceFirst(Part):
@@ -399,7 +342,7 @@
         self.load().wait()
 
         def add(place, k):
-            self.mine[place, k] = (self.mine[place, k].astype(F32) + self.came[place, k].astype(F32)).astype(BF)
+            self.mine[place, k] += self.came[place, k]
 
         def sent(n, carry):
             add(n // 2, n % 2)
@@ -421,8 +364,8 @@
             self.across(j).wait()
 
         def add(n, carry):
-            self.mine[2, n] = (self.mine[2, n].astype(F32) + self.first[0, 1, n].astype(F32)).astype(BF)
-            self.mine[0, n + 2] = (self.mine[0, n + 2].astype(F32) + self.first[1, 0, n].astype(F32)).astype(BF)
+            self.mine[2, n] += self.first[0, 1, n]
+            self.mine[0, n + 2] += self.first[1, 0, n]
             return carry
 
         lax.fori_loop(0, 2, add, 0)
@@ -442,11 +385,15 @@
 
         lax.fori_loop(0, 2, add, 0)
 
+    def out(self):
+        return pltpu.make_async_copy(self.total, self.outs[0], self.kept[12])
+
     def end(self):
         self.close()
-        copy = pltpu.make_async_copy(self.total, self.outs[0], self.kept[12])
-        copy.start()
-        copy.wait()
+        self.out().start()
+
+    def flush(self):
+        self.out().wait()
 
 
 class ReduceTurn(ReduceFirst):
@@ -460,23 +407,26 @@
             self.across(j).wait()
 
         def add(n, carry):
-            self.mine[2, n] = (self.mine[2, n].astype(F32) + self.first[0, 1, n].astype(F32)).astype(BF)
-            self.mine[0, n + 2] = (self.mine[0, n + 2].astype(F32) + self.first[1, 0, n].astype(F32)).astype(BF)
+            self.mine[2, n] += self.first[0, 1, n]
+            self.mine[0, n + 2] += self.first[1, 0, n]
             for j in (1, 2):
-                k = n + 2 * j - 2
-                self.mine[3, k] = (self.mine[3, k].astype(F32) + self.first[j - 1, j - 1, n].astype(F32)).astype(BF)
+                self.mine[3, n + 2 * j - 2] += self.first[j - 1, j - 1, n]
             return carry
 
         lax.fori_loop(0, 2, add, 0)
+        for copy in self.copies():
+            copy.start()
+
+    def copies(self):
         sem = self.kept[13]
-        copies = [
+        return [
             pltpu.make_async_copy(self.mine.at[2, pl.ds(0, 2)], self.outs[0].at[0], sem.at[0]),
             pltpu.make_async_copy(self.mine.at[0, pl.ds(2, 2)], self.outs[0].at[1], sem.at[1]),
             pltpu.make_async_copy(self.mine.at[3], self.outs[1], sem.at[2]),
         ]
-        for copy in copies:
-            copy.start()
-        for copy in copies:
+
+    def flush(self):
+        for copy in self.copies():
             copy.wait()
 
 
@@ -509,22 +459,26 @@
 
         def add(n, carry):
             for j in (1, 2):
-                k = n + 2 * j - 2
-                total[k] = (total[k].astype(F32) + self.kept[1][j - 1, n].astype(F32)).astype(BF)
+                total[n + 2 * j - 2] += self.kept[1][j - 1, n]
             return carry
 
         lax.fori_loop(0, 2, add, 0)
 
+    def out(self):
+        return pltpu.make_async_copy(self.kept[0], self.outs[0], self.kept[5])
+
     def end(self):
-        self.close()
-        copy = pltpu.make_async_copy(self.kept[0], self.outs[0], self.kept[5])
-        copy.start()
-        copy.wait()
+        if not any(what == "close" for _, what in self.plan):
+            self.close()
+        self.out().start()
+
+    def flush(self):
+        self.out().wait()
 
 
 class ReduceSecond(Part):
-    def __init__(self, totals=None, size=CHUNK, plan=()):
-        self.plan = plan
+    def __init__(self, totals=None, size=CHUNK, plan=(), source=None, deferred=False):
+        self.plan, self.after, self.deferred = plan, source, deferred
         line = pltpu.VMEM((size, D), BF)
         super().__init__(
             [totals] if totals is not None else [],
@@ -542,6 +496,8 @@
         )
 
     def start(self):
+        if self.after is not None:
+            self.ins = [self.after.kept[0]]
         for k in (2, 1, 3):
             self.along(k).start()
         self.own().start()
@@ -558,9 +514,13 @@
     def end(self):
         if not any(what == "close" for _, what in self.plan):
             self.close()
-        copy = pltpu.make_async_copy(self.kept[0], self.outs[0], self.kept[5])
-        copy.start()
-        copy.wait()
+        self.out().start()
+
+    def out(self):
+        return pltpu.make_async_copy(self.kept[0], self.outs[0], self.kept[5])
+
+    def flush(self):
+        self.out().wait()
 
 
 class Share(Part):
@@ -616,6 +576,63 @@
 
     def end(self):
         self.send(0).wait()
+
+
+class Weave(Part):
+    def __init__(self, of_layers, came=None, plan=()):
+        self.plan = plan
+        count = of_layers[0].shape[0]
+        images = pltpu.VMEM((count, TOK, D), BF)
+        self.count = count
+        super().__init__(
+            [*of_layers] + ([] if came is None else [came]), [jax.ShapeDtypeStruct((count, TOK, 2, D), BF)],
+            [images, images, pltpu.VMEM((count, TOK, 2, D), BF)] + sems()
+            + [pltpu.SemaphoreType.DMA(()), pltpu.SemaphoreType.DMA(()), pltpu.SemaphoreType.DMA((count,))],
+        )
+
+    def send(self, core):
+        return remote(self.ins[1 - core], self.kept[1], self.kept[3:5], "pipe", 1 - core)
+
+    def own(self, core):
+        return pltpu.make_async_copy(self.ins[core], self.kept[0], self.kept[5])
+
+    def came(self):
+        return pltpu.make_async_copy(self.ins[2], self.kept[1], self.kept[6])
+
+    def store(self, m):
+        return pltpu.make_async_copy(self.kept[2].at[m], self.outs[0].at[m], self.kept[7].at[m])
+
+    def start(self):
+        by_core(lambda core: self.own(core).start())
+        if len(self.ins) > 2:
+            self.came().start()
+        else:
+            by_core(lambda core: self.send(core).start())
+
+    def wait(self):
+        self.own(0).wait()
+        (self.came() if len(self.ins) > 2 else self.send(0)).wait()
+
+    def weave(self, first, last):
+        first_core = lax.axis_index("pipe") == 0
+
+        def image(m, carry):
+            mine, theirs = self.kept[0][m], self.kept[1][m]
+            pair = [jnp.where(first_core, mine, theirs), jnp.where(first_core, theirs, mine)]
+            self.kept[2][m] = jnp.stack(pair, axis=1)
+            return carry
+
+        lax.fori_loop(first, last, image, 0)
+        for m in range(first, last):
+            self.store(m).start()
+
+    def all(self):
+        self.wait()
+        self.weave(0, self.count)
+
+    def end(self):
+        for m in range(self.count):
+            self.store(m).wait()
 
 
 def carried_call(body, parts, collective_id, *, grid, in_specs, inputs, out_specs, out_shape, scratch_shapes, name, cost):
@@ -677,6 +694,9 @@
                 if not task.deferred:
                     task.start()
 
+    if isinstance(weights, Weights) and weights.count > 1:
+        pl.when(pl.program_id(0) == 0)(weights.load_rest)
+
 
 def planned(tasks, point):
     return [getattr(task, what) for task in tasks for at, what in task.plan if at == point]
@@ -686,7 +706,7 @@
     for step in range(steps):
         calls = planned(tasks, step)
         if step == steps - 1:
-            calls += [task.end for task in tasks]
+            calls += [task.end for task in tasks] + [task.flush for task in tasks]
         if calls:
 
             @pl.when(pl.program_id(0) == step)
@@ -778,7 +798,7 @@
 
 def attn_fwd_body(
     layer, rolled, weights, keep, tasks, x_ref, table_ref, bias_ref, fw_ref, qkv_ref, p_ref, ho_ref, mid_ref,
-    xs_ref, how_ref, wq_ref, wpt_ref, vec_ref, shift_ref, spread_ref, gather_ref, mask_ref, region_ref,
+    how_ref, wq_ref, wpt_ref, vec_ref, shift_ref, spread_ref, gather_ref, mask_ref, region_ref,
 ):
     begin(weights, tasks)
     wa_ref = weights.kept[0].at[0]
@@ -801,14 +821,8 @@
         if layer:
             for w in range(NW):
                 region_ref[w] = region_mask(w)
-        else:
-            xs_ref[...] = jnp.zeros_like(xs_ref)
-
-    if layer:
-        x = x_ref[0].astype(F32)
-    else:
-        xs_ref[0:TOK, :] = x_ref[0, lax.axis_index("pipe")]
-        x = xs_ref[...].astype(F32)
+
+    x = x_ref[0].astype(F32)
     normed, _ = normalize(x)
     first = (normed * vec_ref[0:1, :] + vec_ref[1:2, :]).astype(BF)
     fw = dot_nn(spread_ref[...], first).astype(BF)
@@ -840,7 +854,7 @@
         scores = [dot_nt(part(w, g, 1), block_diagonal(part(w, g, 0), mask_ref[...])) for w, g in chains]
         probs = []
         for (w, g), st in zip(chains, scores):
-            st = st + bias_ref[g]
+            st = st + bias_ref[0, g]
             if layer:
                 st = st + region_ref[w]
             e = jnp.exp(st - jnp.max(st, 0, keepdims=True))
@@ -871,7 +885,9 @@
         [keep, weights, *tasks],
         collective_id,
         grid=(n,),
-        in_specs=[per(x.shape[1:]), whole(table.shape), whole((4, WP, GH * WP))],
+        in_specs=[
+            per(x.shape[1:]), whole(table.shape), pl.BlockSpec((1, 4, WP, GH * WP), lambda i: (layer, 0, 0, 0)),
+        ],
         inputs=(x, table, bias),
         out_specs=[per((ROWS, D)), per((ROWS, 3 * D)), per((NW, 4, WP, GH * WP)), per((TP, D)), per((TP, D))],
         out_shape=[
@@ -882,7 +898,7 @@
             jax.ShapeDtypeStruct((n, TP, D), F32),
         ],
         scratch_shapes=[
-            pltpu.VMEM((TP, D), BF), pltpu.VMEM((ROWS, D), BF), pltpu.VMEM((D, 3 * D), BF), pltpu.VMEM((D, D), BF), pltpu.VMEM((8, D), F32),
+            pltpu.VMEM((ROWS, D), BF), pltpu.VMEM((D, 3 * D), BF), pltpu.VMEM((D, D), BF), pltpu.VMEM((8, D), F32),
             pltpu.VMEM((8, 3 * D), F32), pltpu.VMEM((ROWS, TP), BF), pltpu.VMEM((TP, ROWS), BF), pltpu.VMEM((GH * WP, GL), BF),
             pltpu.VMEM((NW, WP, GH * WP), F32),
         ],
@@ -899,7 +915,7 @@
 
 def alive_of(counts_ref, m):
     slot = lax.axis_index("tensor") * 2 + lax.axis_index("pipe")
-    return (slot < counts_ref[m, 0]).astype(F32)
+    return (slot < counts_ref[0, m]).astype(F32)
 
 
 def live_rows(counts_ref, m):
@@ -1015,13 +1031,8 @@
         total = jnp.zeros((1, D), F32)
         for m in range(rows_total // TP):
             rows = slice(m * TP, (m + 1) * TP)
-            if layer:
-                gy_ref[rows, :] = jnp.zeros((TP, D), BF)
-                gy = g_ref[m, lax.axis_index("pipe")].astype(F32) * alive_of(counts_ref, m)
-                gy_ref[m * TP : m * TP + TOK, :] = gy.astype(BF)
-            else:
-                gy = g_ref[m].astype(F32) * live_rows(counts_ref, m)
-                gy_ref[rows, :] = gy.astype(BF)
+            gy = g_ref[m].astype(F32) * live_rows(counts_ref, m)
+            gy_ref[rows, :] = gy.astype(BF)
             total += jnp.sum(gy, 0, keepdims=True)
         small_ref[:, 0:1] = by_shard(total)
         gyt_ref[...] = gy_ref[...].T
@@ -1102,7 +1113,7 @@
 def attn_bwd_body(
     layer, rolled, weights, tasks, x_ref, gmid_ref, fw_ref, qkv_ref, p_ref, ho_ref, table_ref,
     gin_ref, out_ref, ga_ref, ga_away_ref, gqv_ref, gtab_ref, small_ref,
-    xs_ref, gw_ref, dq_ref, fwt_ref, hos_ref, gms_ref, value_ref, spread_ref, gather_ref, mask_ref, gain_ref,
+    gw_ref, dq_ref, fwt_ref, hos_ref, gms_ref, value_ref, spread_ref, gather_ref, mask_ref, gain_ref,
 ):
     i = pl.program_id(0)
     last = pl.num_programs(0) - 1
@@ -1118,8 +1129,6 @@
         gather_ref[...] = gather_map(layer * SHIFT)
         mask_ref[...] = head_mask()
         gain_ref[...] = along_model(table_ref, layer, GAIN, rolled)
-        if not layer:
-            xs_ref[...] = jnp.zeros_like(xs_ref)
 
     gmid = gmid_ref[0]
     gmb = gmid.astype(BF)
@@ -1172,12 +1181,7 @@
     image_rows = pl.ds(base, ROWS)
     e = dot_nt(dq_ref[image_rows, :], wq_ref[...])
     e = dot_nn(gather_ref[...], e.astype(BF))
-    if layer:
-        x = x_ref[0].astype(F32)
-    else:
-        xs_ref[0:TOK, :] = x_ref[0, lax.axis_index("pipe")]
-        x = xs_ref[...].astype(F32)
-    normed, inverse = normalize(x)
+    normed, inverse = normalize(x_ref[0].astype(F32))
     small_ref[:, 0:1] += by_shard(jnp.sum(e * normed, 0, keepdims=True))
     small_ref[:, 1:2] += by_shard(jnp.sum(e, 0, keepdims=True))
     gin = (gmid + norm_back(e, normed, inverse, gain_ref[...])).astype(BF)
@@ -1232,7 +1236,7 @@
             jax.ShapeDtypeStruct((4, 2, GL), F32),
         ],
         scratch_shapes=[
-            pltpu.VMEM((TP, D), BF), pltpu.VMEM((ROWS, D), BF), pltpu.VMEM((n * ROWS, 3 * D), BF), pltpu.VMEM((D, n * ROWS), BF),
+            pltpu.VMEM((ROWS, D), BF), pltpu.VMEM((n * ROWS, 3 * D), BF), pltpu.VMEM((D, n * ROWS), BF),
             pltpu.VMEM((n * TP, D), BF), pltpu.VMEM((n * TP, D), BF), pltpu.VMEM((D, 4 * D), BF),
             pltpu.VMEM((ROWS, TP), BF), pltpu.VMEM((TP, ROWS), BF), pltpu.VMEM((GH * WP, GL), BF), pltpu.VMEM((1, D), F32),
         ],
@@ -1255,7 +1259,7 @@
     )(*inputs)
 
 
-def prepare_body(wqkv, wproj, gain, shift, qv, table, bproj, mgain, mshift, hb, ob, own_a_ref, lines_ref, rows_ref):
+def prepare_body(turned, wqkv, wproj, gain, shift, qv, table, bproj, mgain, mshift, hb, ob, own_a_ref, lines_ref, index_ref, rows_ref, keys_ref):
     own_a_ref[:, : 3 * GL] = dot_nn(wqkv[...], permutation(3 * GL, qkv_source, False)).astype(BF)
     own_a_ref[:, 3 * GL :] = wproj[...].T
     rows_ref[...] = jnp.zeros_like(rows_ref)
@@ -1270,12 +1274,20 @@
     rows_ref[TABLE : TABLE + 4, :] = places[:, :GL]
     rows_ref[TABLE + 4 : TABLE + 8, 0 : RELS - GL] = places[:, GL:]
     lines_ref[...] = rows_ref[...].astype(BF)
-
-
-def prepare(wqkv, wproj, *small):
+    keys_ref[...] = jnp.full((WP, GL), -1, jnp.int32)
+    keys_ref[0:POS, 0:POS] = turned[...]
+    pair = [keys_ref[pl.ds(odd, WP // 2, 2), :][:, :WP] for odd in range(2)]
+    index_ref[...] = jnp.concatenate(pair, 1)
+
+
+def prepare(turned, wqkv, wproj, *small):
     return plain_call(
-        prepare_body, "prepare", (wqkv, wproj, *small),
-        [jax.ShapeDtypeStruct((D, D), BF), jax.ShapeDtypeStruct((LINES, GL), BF)], [pltpu.VMEM((LINES, GL), F32)],
+        prepare_body, "prepare", (turned, wqkv, wproj, *small),
+        [
+            jax.ShapeDtypeStruct((D, D), BF), jax.ShapeDtypeStruct((LINES, GL), BF),
+            jax.ShapeDtypeStruct((WP // 2, GL), jnp.int32),
+        ],
+        [pltpu.VMEM((LINES, GL), F32), pltpu.VMEM((WP, GL), jnp.int32)],
     )
 
 
@@ -1300,55 +1312,152 @@
         return remote(table.at[0], table.at[k], [sem.at[k - 1] for sem in self.kept[2:4]], "tensor", lax.rem(shard + 4 - k, 4))
 
 
-def gather_start(own, lines):
+def gather_start(own, lines, index, view):
     exchange = Exchange(own, lines)
-    near_a, near_h, far_a, far_h = Near(0, None, None), Near(0, None, None), Far(None), FarFirst(None)
+    near_a, near_h, near_o, far_a, bias = Near(0, None, None), Near(0, None, None), Near(0, None, None), Far(None), Bias(index)
+    pick = Own(view)
 
     def body():
-        for n, task in enumerate((near_a, near_h)):
+        for n, task in enumerate((near_a, near_h, near_o)):
             task.ins = [exchange.ins[n], exchange.outs[n]]
-        far_a.ins, far_h.ins = [near_a.outs[0]], [near_h.outs[0]]
+        far_a.ins = [near_a.outs[0]]
         greet()
         for n in (0, 3, 1, 2):
             exchange.swap(n).start()
         exchange.keep().start()
+        pick.start()
         exchange.swap(0).wait()
         near_a.start()
         exchange.keep().wait()
         exchange.swap(3).wait()
         for k in (1, 2, 3):
             exchange.spread(k).start()
+        pick.pick()
         near_a.end()
         far_a.start()
         exchange.swap(1).wait()
         near_h.start()
+        for k in (1, 2, 3):
+            exchange.spread(k).wait()
+        bias.build(exchange.outs[3])
         far_a.turn()
+        exchange.swap(2).wait()
+        near_o.start()
         far_a.rest()
         far_a.last()
-        exchange.swap(2).wait()
-        for k in (1, 2, 3):
-            exchange.spread(k).wait()
+        far_a.end()
+        bias.end()
+        pick.end()
         near_h.end()
-        far_h.start()
-        far_a.end()
-        far_h.end()
-
-    parts = [exchange, near_a, near_h, far_a, far_h]
+        near_o.end()
+
+    parts = [exchange, near_a, near_h, near_o, far_a, bias, pick]
     _, given = carried_call(
         body, parts, 0, grid=(), in_specs=[], inputs=(), out_specs=[], out_shape=[], scratch_shapes=[],
         name="gather_start", cost=pl.CostEstimate(flops=1 << 24, bytes_accessed=8 << 20, transcendentals=0),
     )
-    others, given_a, given_h, far, first_h = given
-    return others[:3], others[3], [given_a[0], *far], (given_h[0], first_h)
-
-
-def onehot_of(rel_index):
-    rel = jnp.pad(rel_index.T, ((0, WP - POS), (0, WP - POS)), constant_values=-1).reshape(-1)
-    return (jnp.arange(2 * GL, dtype=jnp.int32)[:, None] == rel[None, :]).astype(BF)
-
-
-def bias_tables(table, onehot):
+    others, given_a, given_h, given_o, far, *rest = given
+    return others[:3], others[3], [given_a[0], *far], given_h[0], given_o[0], *[part[0] for part in rest]
+
+
+def turned_index(rel_index):
+    return jnp.pad(rel_index.T, ((0, WP - POS), (0, WP - POS)), constant_values=-1)
+
+
+def places_of(pairs):
+    return (iota((2 * GL, pairs.shape[1]), 0) == pairs).astype(F32).astype(BF)
+
+
+class Own(Part):
+    def __init__(self, view, plan=()):
+        count = view.shape[0]
+        self.count, self.plan = count, plan
+        super().__init__(
+            [view], [jax.ShapeDtypeStruct((count, TP, D), BF)],
+            [pltpu.VMEM(view.shape, BF), pltpu.VMEM((count, TP, D), BF), pltpu.SemaphoreType.DMA((2,))],
+        )
+
+    def load(self):
+        return pltpu.make_async_copy(self.ins[0], self.kept[0], self.kept[2].at[0])
+
+    def out(self):
+        return pltpu.make_async_copy(self.kept[1], self.outs[0], self.kept[2].at[1])
+
+    def start(self):
+        self.load().start()
+
+    def pick(self):
+        self.load().wait()
+        first_core = lax.axis_index("pipe") == 0
+
+        def image(m, carry):
+            both = self.kept[0][m]
+            self.kept[1][m] = jnp.zeros((TP, D), BF)
+            self.kept[1][m, 0:TOK, :] = jnp.where(first_core, both[:, 0, :], both[:, 1, :])
+            return carry
+
+        lax.fori_loop(0, self.count, image, 0)
+        self.out().start()
+
+    def end(self):
+        self.out().wait()
+
+
+class Bias(Part):
+    def __init__(self, index):
+        super().__init__(
+            [index], [jax.ShapeDtypeStruct((2, 4, WP, GH * WP), F32)],
+            [pltpu.VMEM((4, 2, LINES, GL), BF), pltpu.VMEM((WP // 2, GL), jnp.int32), pltpu.VMEM((2 * H, 2 * GL), F32),
+             pltpu.VMEM((WP // 2, 2 * H, GL), F32), pltpu.VMEM((WP, GL), F32), pltpu.VMEM((2, 4, WP, GH * WP), F32),
+             pltpu.SemaphoreType.DMA((3,))],
+        )
+
+    def loads(self, table):
+        return [pltpu.make_async_copy(table, self.kept[0], self.kept[6].at[0]), self.index()]
+
+    def index(self):
+        return pltpu.make_async_copy(self.ins[0], self.kept[1], self.kept[6].at[1])
+
+    def out(self):
+        return pltpu.make_async_copy(self.kept[5], self.outs[0], self.kept[6].at[2])
+
+    def build(self, table):
+        lines, index, rows, pairs, half, whole_ref, _ = self.kept
+        for copy in self.loads(table):
+            copy.start()
+        for copy in self.loads(table):
+            copy.wait()
+        for l in range(2):
+            for k in range(4):
+                values = lines[k, l].astype(F32)
+                at = l * H + k * GH
+                rows[at : at + GH, :GL] = values[TABLE : TABLE + GH]
+                rows[at : at + GH, GL:] = values[TABLE + GH : TABLE + 2 * GH]
+        tables = rows[...].astype(BF)
+
+        def product(n, carry):
+            pairs[n] = dot_nn(tables, places_of(index[pl.ds(n, 1), :]))
+            return carry
+
+        lax.fori_loop(0, WP // 2, product, 0)
+        shut = jnp.where(iota((WP, GL), 0) < POS, 0.0, SHUT).astype(F32)
+        for l in range(2):
+            for g in range(4):
+                for n in range(2):
+                    heads = [pairs[:, l * H + g * GH + 2 * n + m, :] for m in range(2)]
+                    for odd in range(2):
+                        lanes = slice(odd * WP, (odd + 1) * WP)
+                        half[pl.ds(odd, WP // 2, 2), :] = jnp.concatenate([head[:, lanes] for head in heads], 1)
+                    whole_ref[l, g, :, n * GL : (n + 1) * GL] = half[...] + shut
+        self.out().start()
+
+    def end(self):
+        self.out().wait()
+
+
+def bias_tables(table, rel_index):
     rows = table[:, :, TABLE : TABLE + 8].reshape(4, 2, 2, GH, GL).transpose(1, 0, 3, 2, 4).reshape(2 * H, 2 * GL)
+    onehot = (jnp.arange(2 * GL, dtype=jnp.int32)[:, None] == turned_index(rel_index).reshape(1, -1)).astype(BF)
     flat = jnp.dot(rows, onehot, preferred_element_type=F32)
     position = flat.reshape(2, 4, GH, WP, WP).transpose(0, 1, 3, 2, 4)
     shut = jnp.where(jnp.arange(WP) < POS, 0.0, SHUT).astype(F32)[:, None, None]
@@ -1474,7 +1583,7 @@
         by_core(action)
 
 
-def table_sums(gtab_ref, onehot_ref, half_ref, pairs_ref, out_ref):
+def table_sums(gtab_ref, index_ref, half_ref, pairs_ref, out_ref):
     for g in range(4):
         for n in range(2):
             half_ref[...] = gtab_ref[g, :, n * GL : (n + 1) * GL]
@@ -1488,29 +1597,29 @@
         pair = pairs_ref[n]
         high = pair.astype(BF)
         low = (pair - high.astype(F32)).astype(BF)
-        places = onehot_ref[:, pl.ds(pl.multiple_of(n * GL, GL), GL)]
+        places = places_of(index_ref[pl.ds(n, 1), :])
         return total + (dot_nt(high, places) + dot_nt(low, places))
 
     out_ref[...] = lax.fori_loop(0, WP // 2, add, jnp.zeros((H, 2 * GL), F32))
 
 
-def reduce_end(attention0, turned0, totals_a1, shared1, grads_in, small, onehot):
+def reduce_end(attention0, totals_h0, turned_o0, piece_a1, shared1, grads_in, small, index):
     halves = ((0, 32), (32, 32))
     first = [ReduceFirst(attention0, rows=rows) for rows in halves]
     second = [ReduceSecond(size=32) for _ in halves]
     share = [Share(rows=halves[0])]
     share.append(Share(rows=halves[1], target=share[0]))
-    onward_m = [ReduceOnward(given) for given in turned0]
-    second_m, share_m = [ReduceSecond(), ReduceSecond()], [Share(), Share()]
-    second_a1, share_a1, done_m1 = ReduceSecond(totals_a1), Share(), Part(shared1)
-    settle, little, deliver, places = Settle(), Little(24), Deliver(grads_in), Stored(onehot)
+    onward_o = ReduceOnward(turned_o0)
+    second_m, share_m = [ReduceSecond(totals_h0), ReduceSecond()], [Share(), Share()]
+    share_a1, done_m1 = Share(piece_a1), Part(shared1)
+    settle, little, places = Settle(), Little(24), Stored(index)
+    input_grad = Weave(grads_in)
 
     def body(*refs):
         layers, (tabs_ref, pairs_ref, half_ref) = (refs[:5], refs[5:10]), refs[10:]
         for n in range(2):
-            second[n].ins, share[n].ins = [first[n].total], [second[n].kept[0]]
-            second_m[n].ins, share_m[n].ins = [onward_m[n].kept[0]], [second_m[n].kept[0]]
-        share_a1.ins = [second_a1.kept[0]]
+            second[n].ins, share[n].ins, share_m[n].ins = [first[n].total], [second[n].kept[0]], [second_m[n].kept[0]]
+        second_m[1].ins = [onward_o.kept[0]]
         done = (
             [share[0].outs[0], share_m[0].outs[0], share_m[1].outs[0]],
             [share_a1.outs[0], done_m1.ins[0], done_m1.ins[1]],
@@ -1520,25 +1629,24 @@
             table_sums(layers[layer][3], places.kept[0], half_ref, pairs_ref, tabs_ref.at[layer])
 
         greet()
-        for task in (*first, *onward_m):
+        for task in (*first, onward_o, second_m[0]):
             task.start()
         places.load()
         first[0].cores()
         first[1].cores()
-        second_a1.start()
         settle.start(done[1], 1, (1, 2))
-        deliver.start()
+        input_grad.start()
         places.wait()
         tab(1)
-        for n in range(2):
-            onward_m[n].close()
-            second_m[n].start()
+        onward_o.close()
+        second_m[1].start()
+        second_m[0].close()
+        share_m[0].start()
         first[0].turn()
+        first[1].turn()
         tab(0)
         little.pack(layers, tabs_ref)
         little.start()
-        first[1].turn()
-        second_a1.close()
         share_a1.start()
         settle.pass_on(done[1], 1, (1, 2))
         first[0].close()
@@ -1546,88 +1654,68 @@
         little.second()
         first[1].close()
         second[1].start()
-        for n in range(2):
-            second_m[n].close()
-            share_m[n].start()
+        second_m[1].close()
+        share_m[1].start()
+        share_m[0].end()
         share_a1.end()
         settle.start(done[1], 1, (0,))
+        settle.start(done[0], 0, (1,))
         little.third()
-        settle.pass_on(done[1], 1, (0,))
+        input_grad.wait()
+        input_grad.weave(0, 2)
         for n in range(2):
             second[n].close()
             share[n].start()
-        for n in range(2):
-            share_m[n].end()
-        settle.start(done[0], 0, (1, 2))
+        settle.pass_on(done[1], 1, (0,))
+        settle.pass_on(done[0], 0, (1,))
+        share_m[1].end()
+        settle.start(done[0], 0, (2,))
         little.end()
-        deliver.end()
-        settle.pass_on(done[0], 0, (1, 2))
+        input_grad.weave(2, 4)
+        settle.pass_on(done[0], 0, (2,))
         for n in range(2):
             share[n].end()
         settle.start(done[0], 0, (0,))
         settle.pass_on(done[0], 0, (0,))
+        input_grad.end()
         settle.end(done)
 
-    parts = [*first, *second, *share, *onward_m, *second_m, *share_m, second_a1, share_a1, done_m1, settle, little, deliver, places]
+    parts = [
+        *first, *second, *share, onward_o, *second_m, *share_m, share_a1, done_m1, settle, little, input_grad, places
+    ]
     _, given = carried_call(
         body, parts, 7, grid=(), in_specs=[pl.BlockSpec(memory_space=pltpu.VMEM)] * 10, inputs=small, out_specs=[], out_shape=[],
         scratch_shapes=[pltpu.VMEM((2, H, 2 * GL), F32), pltpu.VMEM((WP // 2, H, GL), F32), pltpu.VMEM((WP, GL), F32)],
         name="reduce_end", cost=pl.CostEstimate(flops=1 << 24, bytes_accessed=8 << 20, transcendentals=0),
     )
     by_part = dict(zip(map(id, parts), given))
-    return by_part[id(settle)][0], by_part[id(little)][0], by_part[id(deliver)][0]
+    return by_part[id(settle)][0], by_part[id(little)][0], by_part[id(input_grad)][0]
 
 
 def finish_body(
-    matrix_ref, lines_ref, out0_ref, out1_ref, out_came_ref, gin0_ref, gin1_ref, gin_came_ref,
-    block_out_ref, input_grad_ref, gqkv_ref, gproj_ref, ghw_ref, gow_ref, gain_ref, shift_ref, qv_ref, table_ref, bproj_ref,
-    mgain_ref, mshift_ref, hb_ref, ob_ref,
+    matrix_ref, lines_ref, gqkv_ref, gproj_ref, ghw_ref, gow_ref, gain_ref, shift_ref, qv_ref, table_ref, bproj_ref, mgain_ref,
+    mshift_ref, hb_ref, ob_ref,
 ):
-    def images(core):
-        for ref, own, came in (
-            (block_out_ref, (out0_ref, out1_ref), out_came_ref), (input_grad_ref, (gin0_ref, gin1_ref), gin_came_ref)
-        ):
-            ref[0, 0, core] = own[core][0]
-            ref[0, 0, 1 - core] = came[0]
-
-    by_core(images)
-
-    @pl.when(pl.program_id(0) == 0)
-    def _():
-        gqkv_ref[0] = dot_nn(matrix_ref[0, :, : 3 * GL], permutation(3 * GL, qkv_source, True))
-        gproj_ref[0] = matrix_ref[0, :, 3 * GL :].T.astype(F32)
-        lines = lines_ref[...]
-        for row, ref in (
-            (GAIN, gain_ref), (SHIFT_ROW, shift_ref), (BPROJ, bproj_ref), (MGAIN, mgain_ref), (MSHIFT, mshift_ref), (OB, ob_ref)
-        ):
-            ref[...] = lines[row : row + 1]
-        qv_ref[...] = jnp.concatenate(
-            [lines[QV + n : QV + n + 1, h * HD : (h + 1) * HD] for h in range(GH) for n in range(2)], 1
-        )
-        table_ref[0] = jnp.concatenate([lines[TABLE : TABLE + 4], lines[TABLE + 4 : TABLE + 8, : RELS - GL]], 1)
-        hb_ref[...] = jnp.concatenate([lines[HB + n : HB + n + 1] for n in range(4)], 1)
-
-    @pl.when(pl.program_id(0) == 1)
-    def _():
-        ghw_ref[0] = matrix_ref[1].astype(F32)
-        gow_ref[0] = matrix_ref[2].T.astype(F32)
-
-
-def finish(matrices, lines, out0, out1, out_came, gin0, gin1, gin_came):
-    n = out0.shape[0]
-    image = per((TOK, D))
-    both = pl.BlockSpec((1, 1, 2, TOK, D), lambda i: (0, i, 0, 0, 0))
+    gqkv_ref[0] = dot_nn(matrix_ref[0, :, : 3 * GL], permutation(3 * GL, qkv_source, True))
+    gproj_ref[0] = matrix_ref[0, :, 3 * GL :].T.astype(F32)
+    ghw_ref[0] = matrix_ref[1].astype(F32)
+    gow_ref[0] = matrix_ref[2].T.astype(F32)
+    lines = lines_ref[...]
+    for row, ref in (
+        (GAIN, gain_ref), (SHIFT_ROW, shift_ref), (BPROJ, bproj_ref), (MGAIN, mgain_ref), (MSHIFT, mshift_ref), (OB, ob_ref)
+    ):
+        ref[...] = lines[row : row + 1]
+    qv_ref[...] = jnp.concatenate([lines[QV + n : QV + n + 1, h * HD : (h + 1) * HD] for h in range(GH) for n in range(2)], 1)
+    table_ref[0] = jnp.concatenate([lines[TABLE : TABLE + 4], lines[TABLE + 4 : TABLE + 8, : RELS - GL]], 1)
+    hb_ref[...] = jnp.concatenate([lines[HB + n : HB + n + 1] for n in range(4)], 1)
+
+
+def finish(matrices, lines):
     shapes = [
         (1, D, 3 * GL), (1, GL, D), (1, D, D), (1, D, D), (1, GL), (1, GL), (1, 2 * GL), (1, GH, RELS), (1, GL), (1, GL), (1, GL),
         (1, D), (1, GL),
     ]
-    return plain_call(
-        finish_body, "finish", (matrices, lines, out0, out1, out_came, gin0, gin1, gin_came),
-        [jax.ShapeDtypeStruct((1, n, 2, TOK, D), BF)] * 2 + [jax.ShapeDtypeStruct(shape, F32) for shape in shapes],
-        grid=(n,),
-        in_specs=[whole(matrices.shape), whole(lines.shape)] + [image] * 6,
-        out_specs=[both, both] + [whole(shape) for shape in shapes],
-    )
+    return plain_call(finish_body, "finish", (matrices, lines), [jax.ShapeDtypeStruct(shape, F32) for shape in shapes])
 
 
 def layer_forward(layer, rolled, x, counts, table, bias, weights, tasks, ids):
@@ -1640,8 +1728,6 @@
 
 def layer_backward(layer, rolled, cot, kept, counts, table, tasks, ids):
     x, fw, qkv, p, ho, mid, second, act, slope, kept_a, kept_m = kept
-    if not layer:
-        cot = cot.reshape(-1, TP, D)
     (ghw, ghw_away, gow, gow_away, ghb, gmid, small_m), given = mlp_bwd(
         layer, rolled, counts, cot, act, slope, second, mid, table, Stored(*kept_m), tasks[0](), ids[0]
     )
@@ -1678,7 +1764,7 @@
         return lax.all_gather(lax.all_gather(member[0], "tensor", axis=axis, tiled=True), "pipe")
 
     table = on_lines(small_in)
-    bias = bias_tables(table, onehot_of(rel_index))
+    bias = bias_tables(table, rel_index)
     gathered = [both(member, axis) for member, axis in zip(big_in, (1, 0, 1, 0))]
     weights = []
     for l in range(2):
@@ -1688,8 +1774,11 @@
         wm = jnp.stack([hw.reshape(D, 4, -1).transpose(1, 0, 2), ow.reshape(4, -1, D)])
         weights.append((lambda *_, wa=wa: Weights(1, 0, whole=wa), lambda *_, wm=wm: Weights(2, 0, whole=wm)))
     none, back_none, ids = (lambda: [], lambda given: []), (lambda: [], lambda *_: []), (None, None)
-    y0, out0, kept0, _, _ = layer_forward(0, False, images, counts, table, bias[0], weights[0], none, ids)
-    _, out1, kept1, _, _ = layer_forward(1, False, y0, counts, table, bias[1], weights[1], none, ids)
+    images, cotangent = (
+        jnp.pad(lax.dynamic_index_in_dim(array, core, 1, False), ((0, 0), (0, TP - TOK), (0, 0))) for array in (images, cotangent)
+    )
+    y0, out0, kept0, _, _ = layer_forward(0, False, images, counts, table, bias, weights[0], none, ids)
+    _, out1, kept1, _, _ = layer_forward(1, False, y0, counts, table, bias, weights[1], none, ids)
     g1, gin1, big1, small1, _, _ = layer_backward(1, False, cotangent, kept1, counts, table, back_none, ids)
     _, gin0, big0, small0, _, _ = layer_backward(0, False, g1, kept0, counts, table, back_none, ids)
     first_core = core == 0
@@ -1739,11 +1828,10 @@
 
 
 def four_by_four(images, cotangent, counts, rel_index, small_in, big_in):
-    own_a, lines = prepare(big_in[0][0], big_in[1][0], *[member[0] if member.ndim == 3 else member for member in small_in])
+    own_a, lines, index = prepare(rel_index.T, big_in[0][0], big_in[1][0], *[member[0] if member.ndim == 3 else member for member in small_in])
     own = (own_a, big_in[2][0], big_in[3][0])
-    onehot = onehot_of(rel_index)
-    other, table, pieces_a0, hidden0 = gather_start(own, lines)
-    bias = bias_tables(table, onehot)
+    other, table, pieces_a0, near_h0, near_o0, bias, x0 = gather_start(own, lines, index, jnp.swapaxes(images, 1, 2))
+    pick_cot = Own(jnp.swapaxes(cotangent, 1, 2), plan=((2, "pick"),))
 
     def near(n, layer, **how):
         return Near(layer, own[n], other[n], **how)
@@ -1751,42 +1839,46 @@
     def weights(layer, which, pieces):
         return Weights(len(which), layer, own=[own[n] for n in which], other=[other[n] for n in which], pieces=pieces)
 
-    def out_tasks(layer):
-        near_o = near(2, layer, plan=((1, "finish"),))
-        far_o = Far(None, source=near_o, deferred=True, plan=((1, "start"), (2, "turn"), (3, "rest"), (3, "last")))
-        return [near_o, far_o]
-
-    def weights_of_first(layer, pieces):
-        return lambda: weights(layer, (0,), [pieces])
+    def mlp_tasks(near_h, near_o):
+        return [Far(near_h, plan=((1, "turn"), (2, "rest"), (3, "last"))), Far(near_o, plan=((2, "turn"), (3, "rest"), (3, "last")))]
+
+    def forward_weights(layer, pieces, near_h, near_o):
+        return (
+            lambda: weights(layer, (0,), [pieces]),
+            lambda given: weights(layer, (1, 2), [[near_h, *given[1]], [near_o, *given[2]]]),
+        )
 
     y0, out0, kept0, given, more = layer_forward(
-        0, True, images, counts, table, bias[0],
-        (weights_of_first(0, pieces_a0),
-         lambda given: weights(0, (1, 2), [gathered(*hidden0, given[1]), [given[2][0], *given[3]]])),
-        (lambda: [FarSecond(hidden0[1], plan=((1, "last"),)), *out_tasks(0), near(0, 1, deferred=True, plan=((2, "start"),))],
-         lambda given: [Far(given[4][0], plan=((1, "turn"), (3, "rest"), (3, "last"))), near(1, 1, deferred=True, plan=((1, "start"),))]),
+        0, True, x0, counts, table, bias, forward_weights(0, pieces_a0, near_h0, near_o0),
+        (lambda: [*mlp_tasks(near_h0, near_o0), near(0, 1), near(1, 1, deferred=True, plan=((1, "start"),))],
+         lambda given: [Far(given[3][0], plan=((1, "turn"), (2, "rest"), (3, "last"))), near(2, 1)]),
         (1, 2),
     )
-    pieces_a1, near_h1 = [given[4][0], *more[1]], more[2][0]
-    _, out1, kept1, _, _ = layer_forward(
-        1, True, y0, counts, table, bias[1],
-        (weights_of_first(1, pieces_a1),
-         lambda given: weights(1, (1, 2), [[near_h1, *given[1]], [given[2][0], *given[3]]])),
-        (lambda: [Far(near_h1, plan=((1, "turn"), (2, "rest"), (2, "last"))), *out_tasks(1)], lambda given: []), (3, None),
+    pieces_a1, near_h1, near_o1 = [given[3][0], *more[1]], given[4][0], more[2][0]
+    _, out1, kept1, given, _ = layer_forward(
+        1, True, y0, counts, table, bias, forward_weights(1, pieces_a1, near_h1, near_o1),
+        (lambda: [*mlp_tasks(near_h1, near_o1), pick_cot], lambda given: []), (3, None),
     )
+    cot = given[3][0]
 
     def mlp_reduce(big_m):
         return [ReduceTurn(big_m[0], plan=((0, "cores"),)), ReduceTurn(big_m[1], plan=((1, "cores"),))]
 
     g1, gin1, big1, small1, given, more = layer_backward(
-        1, True, cotangent, kept1, counts, table, (lambda: [Deliver([out0, out1])], lambda big_m, given: mlp_reduce(big_m)), (4, 5)
+        1, True, cot, kept1, counts, table, (lambda: [Deliver([out0, out1])], lambda big_m, given: mlp_reduce(big_m)), (4, 5)
     )
     out_came, turned1 = given[1][0], more[1:3]
 
     def last_tasks(big_m, given):
-        seconds = [ReduceSecond(given[2][0], plan=((1, "close"),)), ReduceSecond(given[3][0], plan=((LATE, "close"),))]
-        shares = [Share(source=seconds[0], plan=((1, "start"),)), Share(source=seconds[1], plan=((LATE, "start"),))]
-        return [*mlp_reduce(big_m), ReduceOnward(given[1]), *seconds, *shares]
+        onward = ReduceOnward(given[1], plan=((1, "close"),))
+        second_h = ReduceSecond(given[2][0], plan=((1, "close"),))
+        second_o = ReduceSecond(given[3][0], deferred=True, plan=((1, "start"), (LATE, "close")))
+        second_a = ReduceSecond(source=onward, deferred=True, plan=((2, "start"),))
+        shares = [Share(source=second_h, plan=((1, "start"),)), Share(source=second_o, plan=((LATE, "start"),))]
+        return [
+            ReduceFirst(big_m[0], plan=((0, "cores"), (LATE, "turn"))), ReduceTurn(big_m[1], plan=((1, "cores"),)), onward, second_h,
+            *shares[:1], second_o, second_a, *shares[1:], Weave([out0, out1], out_came, plan=((3, "all"),)),
+        ]
 
     _, gin0, big0, small0, given, more = layer_backward(
         0, True, g1, kept0, counts, table,
@@ -1796,10 +1888,13 @@
         ),
         (6, 8),
     )
-    turned0, totals_a1, shared1 = more[1:3], more[3][0], (more[6][0], more[7][0])
-    matrices, lines, gin_came = reduce_end(big0[0], turned0, totals_a1, shared1, [gin0, gin1], [*small0, *small1], onehot)
-    block_out, input_grad, gqkv, gproj, ghw, gow, *outs = finish(matrices, lines, out0, out1, out_came, gin0, gin1, gin_came)
-    return block_out, input_grad, (gqkv, gproj, ghw, gow), outs
+    totals_h0, turned_o0, piece_a1, shared1 = more[1][0], more[2], more[7][0], (more[5][0], more[8][0])
+    block_out = more[9][0]
+    matrices, lines, input_grad = reduce_end(
+        big0[0], totals_h0, turned_o0, piece_a1, shared1, [gin0, gin1], [*small0, *small1], index
+    )
+    gqkv, gproj, ghw, gow, *outs = finish(matrices, lines)
+    return jnp.swapaxes(block_out, 1, 2)[None], jnp.swapaxes(input_grad, 1, 2)[None], (gqkv, gproj, ghw, gow), outs
 
 
 def local(
@@ -1807,6 +1902,7 @@
     pre_mlp_gain, pre_mlp_bias, hidden_weight, hidden_bias, out_weight, out_bias,
 ):
     assert images.shape[1] == 2, images.shape
+    counts = counts.T
     small_in = (pre_attn_gain, pre_attn_bias, qv_bias, bias_table, proj_bias, pre_mlp_gain, pre_mlp_bias, hidden_bias, out_bias)
     big_in = (qkv_weight, proj_weight, hidden_weight, out_weight)
     if lax.axis_size("tensor") == 4 and lax.axis_size("dp") == 4:

time: 265 us -> 240 us (0.906)
  Pallas kernels: 247 us -> 235 us
  local copies, waits for them, and re-layouts: 13.1 us -> 4.58 us
    pallas_call x10, Pallas kernels: 237 us -> 229 us  [carried_call(): pl.pallas_call(whole_body, grid_spec=pltpu.PrefetchScalarGridSpec(num_sca...]
    unnamed x16 -> x7, local copies, waits for them, and re-layouts: 10 us -> 4.58 us
    pallas_call x2, Pallas kernels: 9.43 us -> 5.9 us  [plain_call(): pl.pallas_call(body, grid=grid, out_shape=out_shape, in_specs=in_specs or...]
where the time goes in v3:
time: 240 us
  Pallas kernels  235 us (98%)
  local copies, waits for them, and re-layouts  4.58 us (2%)
    pallas_call x10, Pallas kernels, carried_call(): pl.pallas_call(whole_body, grid_spec=pltpu.PrefetchScalarGridSpec(num_sca...  229 us
    pallas_call x2, Pallas kernels, plain_call(): pl.pallas_call(body, grid=grid, out_shape=out_shape, in_specs=in_specs or...  5.9 us

profile of v3, /device:TPU:0, one launch (start us, length us, event | category | flops | bytes accessed | tf_op | source)
XLA Modules:
  0.0 239.9 jit_solution(15630022227456875719)
XLA Ops:
  0.6 1.4 copy.32
  2.1 2.3 prepare.1
  4.4 29.4 %gather_start.1 = (bf16[512,512]{1,0:T(8,128)(2,1)}, bf16[512,512]{1,0:T(8,128)(2,1)}, bf16[512,512]{1,0:T(8,128)(2,1)}, bf16[4,2,32,128]{3,2,1,0:T(8,128)(2,1)}...) custom-call(bf16[512,512]{1,0:T(8,128)(2,1)} %get-tuple-element.157., ...), custom_call_target="tpu_custom_call" | custom-call | flops 16777216 | bytes 8388608 | tf_op jit(solution)/shard_map/gather_start/pallas_call | solution.py:664
  33.8 23.0 %attn_fwd.2 = (bf16[4,256,512]{2,1,0:T(8,128)(2,1)}, bf16[4,256,1536]{2,1,0:T(8,128)(2,1)}, bf16[4,4,4,64,256]{4,3,2,1,0:T(8,128)(2,1)}, bf16[4,208,512]{2,1,0:T...) custom-call(bf16[4,208,512]{2,1,0:T(8,128)(2,1)} %get-tuple-element., ...), custom_call_target="tpu_custom_call" | custom-call | flops 2726297600 | bytes 8388608 | tf_op jit(solution)/shard_map/attn_fwd/pallas_call | solution.py:664
  56.8 15.9 %mlp_fwd.2 = (bf16[832,512]{1,0:T(8,128)(2,1)}, bf16[4,832,512]{2,1,0:T(8,128)(2,1)}, bf16[4,832,512]{2,1,0:T(8,128)(2,1)}, bf16[4,208,512]{2,1,0:T(8,128)(2,1)}...) custom-call(s32[1,4]{1,0:T(1,128)} %bitcast.35, ...), custom_call_target="tpu_custom_call" | custom-call | flops 3489660928 | bytes 12582912 | tf_op jit(solution)/shard_map/mlp_fwd/pallas_call | solution.py:664
  72.7 21.6 %attn_fwd.3 = (bf16[4,256,512]{2,1,0:T(8,128)(2,1)}, bf16[4,256,1536]{2,1,0:T(8,128)(2,1)}, bf16[4,4,4,64,256]{4,3,2,1,0:T(8,128)(2,1)}, bf16[4,208,512]{2,1,0:T...) custom-call(bf16[4,208,512]{2,1,0:T(8,128)(2,1)} %get-tuple-element., ...), custom_call_target="tpu_custom_call" | custom-call | flops 2726297600 | bytes 8388608 | tf_op jit(solution)/shard_map/attn_fwd/pallas_call | solution.py:664
  94.4 10.9 %mlp_fwd.3 = (bf16[832,512]{1,0:T(8,128)(2,1)}, bf16[4,832,512]{2,1,0:T(8,128)(2,1)}, bf16[4,832,512]{2,1,0:T(8,128)(2,1)}, bf16[4,208,512]{2,1,0:T(8,128)(2,1)}...) custom-call(s32[1,4]{1,0:T(1,128)} %bitcast.36, f32[832,512]{1,0:T(8,128)} %bitcast.41, ...), custom_call_target="tpu_custom_call" | custom-call | flops 3489660928 | bytes 12582912 | tf_op jit(solution)/shard_map/mlp_fwd/pallas_call | solution.py:664
  105.3 17.1 %mlp_bwd.2 = (bf16[4,4,64,512]{3,2,1,0:T(8,128)(2,1)}, bf16[4,4,64,512]{3,2,1,0:T(8,128)(2,1)}, bf16[4,4,64,512]{3,2,1,0:T(8,128)(2,1)}, bf16[4,4,64,512]{3,2,1,...) custom-call(s32[1,4]{1,0:T(1,128)} %bitcast.37, ...), custom_call_target="tpu_custom_call" | custom-call | flops 6979321856 | bytes 16777216 | tf_op jit(solution)/shard_map/mlp_bwd/pallas_call | solution.py:664
  122.4 23.3 %attn_bwd.2 = (bf16[4,208,512]{2,1,0:T(8,128)(2,1)}, bf16[4,196,512]{2,1,0:T(8,128)(2,1)}, bf16[4,4,64,512]{3,2,1,0:T(8,128)(2,1)}, bf16[4,4,64,512]{3,2,1,0:T(8...) custom-call(bf16[4,208,512]{2,1,0:T(8,128)(2,1)} %get-tuple-element., ...), custom_call_target="tpu_custom_call" | custom-call | flops 5452595200 | bytes 12582912 | tf_op jit(solution)/shard_map/attn_bwd/pallas_call | solution.py:664
  145.7 19.7 %mlp_bwd.3 = (bf16[4,4,64,512]{3,2,1,0:T(8,128)(2,1)}, bf16[4,4,64,512]{3,2,1,0:T(8,128)(2,1)}, bf16[4,4,64,512]{3,2,1,0:T(8,128)(2,1)}, bf16[4,4,64,512]{3,2,1,...) custom-call(s32[1,4]{1,0:T(1,128)} %bitcast.38, ...), custom_call_target="tpu_custom_call" | custom-call | flops 6979321856 | bytes 16777216 | tf_op jit(solution)/shard_map/mlp_bwd/pallas_call | solution.py:664
  165.4 31.3 %attn_bwd.3 = (bf16[4,208,512]{2,1,0:T(8,128)(2,1)}, bf16[4,196,512]{2,1,0:T(8,128)(2,1)}, bf16[4,4,64,512]{3,2,1,0:T(8,128)(2,1)}, bf16[4,4,64,512]{3,2,1,0:T(8...) custom-call(bf16[4,208,512]{2,1,0:T(8,128)(2,1)} %get-tuple-element., ...), custom_call_target="tpu_custom_call" | custom-call | flops 5452595200 | bytes 12582912 | tf_op jit(solution)/shard_map/attn_bwd/pallas_call | solution.py:664
  196.8 36.4 %reduce_end.1 = (bf16[4,32,512]{2,1,0:T(8,128)(2,1)}, bf16[4,32,512]{2,1,0:T(8,128)(2,1)}, bf16[32,512]{1,0:T(8,128)(2,1)}, bf16[32,512]{1,0:T(8,128)(2,1)}, bf1...) custom-call(f32[4,4,128]{2,1,0:T(4,128)} %get-tuple-element.263.refs, ...), custom_call_target="tpu_custom_call" | custom-call | flops 16777216 | bytes 8388608 | tf_op jit(solution)/shard_map/reduce_end/pallas_call | solution.py:664
  233.2 0.0 copy-start
  233.2 3.6 %finish.1 = (f32[1,512,384]{2,1,0:T(8,128)}, f32[1,128,512]{2,1,0:T(8,128)}, f32[1,512,512]{2,1,0:T(8,128)}, f32[1,512,512]{2,1,0:T(8,128)}, f32[1,128]{1,0:T(1,...) custom-call(bf16[3,512,512]{2,1,0:T(8,128)(2,1)} %get-tuple-element., ...), custom_call_target="tpu_custom_call" | custom-call | flops 4194304 | bytes 4194304 | tf_op jit(solution)/shard_map/finish/pallas_call | solution.py:1249
  236.8 0.0 copy-start.1
  236.8 0.0 copy-done
  236.8 1.2 copy.35
  238.0 0.8 copy-done.1
  238.8 1.2 copy.36
Async XLA Ops:
  233.2 3.6 %copy-start = (bf16[4,196,2,512]{3,2,1,0:T(2,128)(2,1)S(1)}, bf16[4,196,2,512]{3,2,1,0:T(2,128)(2,1)}, u32[]{:S(2)}) copy-start(bf16[4,196,2,512]{3,2,1,0:T(2,128)(2,1)} %get-tuple-element.262) | copy-start | bytes 4816900
  236.8 2.0 copy-start.1

commit v4 on v3

--- a/solution.py
+++ b/solution.py
@@ -524,19 +524,24 @@
 
 
 class Share(Part):
-    def __init__(self, piece=None, rows=(0, CHUNK), target=None, source=None, plan=()):
+    def __init__(self, piece=None, rows=(0, CHUNK), target=None, source=None, plan=(), in_vmem=False):
         self.start_row, self.size = rows
         self.target, self.after, self.plan, self.deferred = target, source, plan, source is not None
         super().__init__(
             [piece] if piece is not None else [],
-            [jax.ShapeDtypeStruct((D, D), BF)] if target is None else [],
-            [pltpu.VMEM((self.size, D), BF)] + sems(3) + [pltpu.SemaphoreType.DMA(()), pltpu.SemaphoreType.DMA(())],
+            [jax.ShapeDtypeStruct((D, D), BF)] if target is None and not in_vmem else [],
+            [pltpu.VMEM((self.size, D), BF)] + sems(3) + [pltpu.SemaphoreType.DMA(()), pltpu.SemaphoreType.DMA(())]
+            + ([pltpu.VMEM((D, D), BF)] if in_vmem else []),
         )
+        self.in_vmem = in_vmem
+
+    def whole(self):
+        return self.kept[5] if self.in_vmem else self.outs[0]
 
     def place(self):
         core, dp, _ = place_in_mesh()
         start = pl.multiple_of(core * 256 + dp * CHUNK, CHUNK) + self.start_row
-        out = self.outs[0] if self.target is None else self.target.outs[0]
+        out = (self.target or self).whole()
         return out.at[pl.ds(pl.multiple_of(start, self.size), self.size), :]
 
     def across(self, j):
@@ -561,6 +566,8 @@
         self.keep().start()
         for j in (1, 2, 3):
             self.across(j).wait()
+
+    def flush(self):
         self.keep().wait()
 
 
@@ -1259,7 +1266,7 @@
     )(*inputs)
 
 
-def prepare_body(turned, wqkv, wproj, gain, shift, qv, table, bproj, mgain, mshift, hb, ob, own_a_ref, lines_ref, index_ref, rows_ref, keys_ref):
+def prepare_body(index, wqkv, wproj, gain, shift, qv, table, bproj, mgain, mshift, hb, ob, own_a_ref, lines_ref, index_ref, rows_ref, keys_ref):
     own_a_ref[:, : 3 * GL] = dot_nn(wqkv[...], permutation(3 * GL, qkv_source, False)).astype(BF)
     own_a_ref[:, 3 * GL :] = wproj[...].T
     rows_ref[...] = jnp.zeros_like(rows_ref)
@@ -1274,20 +1281,21 @@
     rows_ref[TABLE : TABLE + 4, :] = places[:, :GL]
     rows_ref[TABLE + 4 : TABLE + 8, 0 : RELS - GL] = places[:, GL:]
     lines_ref[...] = rows_ref[...].astype(BF)
-    keys_ref[...] = jnp.full((WP, GL), -1, jnp.int32)
-    keys_ref[0:POS, 0:POS] = turned[...]
+    keys_ref[...] = jnp.full((GL, GL), -1.0, F32)
+    keys_ref[0:POS, 0:POS] = index[...].astype(F32)
+    keys_ref[...] = keys_ref[...].T
     pair = [keys_ref[pl.ds(odd, WP // 2, 2), :][:, :WP] for odd in range(2)]
-    index_ref[...] = jnp.concatenate(pair, 1)
-
-
-def prepare(turned, wqkv, wproj, *small):
+    index_ref[...] = jnp.concatenate(pair, 1).astype(jnp.int32)
+
+
+def prepare(rel_index, wqkv, wproj, *small):
     return plain_call(
-        prepare_body, "prepare", (turned, wqkv, wproj, *small),
+        prepare_body, "prepare", (rel_index, wqkv, wproj, *small),
         [
             jax.ShapeDtypeStruct((D, D), BF), jax.ShapeDtypeStruct((LINES, GL), BF),
             jax.ShapeDtypeStruct((WP // 2, GL), jnp.int32),
         ],
-        [pltpu.VMEM((LINES, GL), F32), pltpu.VMEM((WP, GL), jnp.int32)],
+        [pltpu.VMEM((LINES, GL), F32), pltpu.VMEM((GL, GL), F32)],
     )
 
 
@@ -1477,7 +1485,7 @@
         super().__init__(
             [],
             [jax.ShapeDtypeStruct((rows, GL), F32)],
-            [pltpu.VMEM((2, 4, rows, GL), F32), pltpu.VMEM((4, rows, GL), F32), pltpu.VMEM((3, 4, rows, GL), F32),
+            [pltpu.VMEM((2, 4, rows, GL), F32), pltpu.VMEM((4, rows, GL), F32), pltpu.VMEM((4, rows, GL), F32),
              pltpu.VMEM((3, rows, GL), F32)]
             + sems() + sems(3) + sems(3) + [pltpu.SemaphoreType.DMA(())],
         )
@@ -1506,7 +1514,7 @@
 
     def across(self, j):
         _, dp, _ = place_in_mesh()
-        return remote(self.kept[1], self.kept[2].at[j - 1], [sem.at[j - 1] for sem in self.kept[6:8]], "dp", dp ^ j)
+        return remote(self.kept[2].at[0], self.kept[2].at[j], [sem.at[j - 1] for sem in self.kept[6:8]], "dp", dp ^ j)
 
     def along(self, k):
         _, _, shard = place_in_mesh()
@@ -1521,23 +1529,28 @@
         core, _, _ = place_in_mesh()
         self.over().wait()
         self.kept[1][...] += self.kept[0][core]
+        for k in (1, 2, 3):
+            self.along(k).start()
+
+    def third(self):
+        for k in (1, 2, 3):
+            self.along(k).wait()
+        self.kept[2][0] = self.kept[1][0] + self.kept[3][0] + self.kept[3][1] + self.kept[3][2]
         for j in (1, 2, 3):
             self.across(j).start()
 
-    def third(self):
+    def fourth(self):
         for j in (1, 2, 3):
             self.across(j).wait()
-        self.kept[1][...] += self.kept[2][0] + self.kept[2][1] + self.kept[2][2]
-        for k in (1, 2, 3):
-            self.along(k).start()
+        total = self.kept[2]
+        self.kept[1][0] = total[0] + total[1] + total[2] + total[3]
+        self.out().start()
+
+    def out(self):
+        return pltpu.make_async_copy(self.kept[1].at[0], self.outs[0], self.kept[10])
 
     def end(self):
-        for k in (1, 2, 3):
-            self.along(k).wait()
-        self.kept[2][0, 0] = self.kept[1][0] + self.kept[3][0] + self.kept[3][1] + self.kept[3][2]
-        copy = pltpu.make_async_copy(self.kept[2].at[0, 0], self.outs[0], self.kept[10])
-        copy.start()
-        copy.wait()
+        self.out().wait()
 
 
 class Settle(Part):
@@ -1564,6 +1577,16 @@
         def action(core):
             for n in which:
                 (self.load if core == layer else self.send)(matrices[n], n, core).start()
+
+        by_core(action)
+
+    def straight(self, matrix, n, layer):
+        def action(core):
+            if core == layer:
+                rows = self.rows(core)
+                pltpu.make_async_copy(matrix.at[rows], self.outs[0].at[n, rows], self.kept[4].at[n]).start()
+            else:
+                self.send(matrix, n, core).start()
 
         by_core(action)
 
@@ -1607,7 +1630,7 @@
     halves = ((0, 32), (32, 32))
     first = [ReduceFirst(attention0, rows=rows) for rows in halves]
     second = [ReduceSecond(size=32) for _ in halves]
-    share = [Share(rows=halves[0])]
+    share = [Share(rows=halves[0], in_vmem=True)]
     share.append(Share(rows=halves[1], target=share[0]))
     onward_o = ReduceOnward(turned_o0)
     second_m, share_m = [ReduceSecond(totals_h0), ReduceSecond()], [Share(), Share()]
@@ -1621,7 +1644,7 @@
             second[n].ins, share[n].ins, share_m[n].ins = [first[n].total], [second[n].kept[0]], [second_m[n].kept[0]]
         second_m[1].ins = [onward_o.kept[0]]
         done = (
-            [share[0].outs[0], share_m[0].outs[0], share_m[1].outs[0]],
+            [share[0].whole(), share_m[0].outs[0], share_m[1].outs[0]],
             [share_a1.outs[0], done_m1.ins[0], done_m1.ins[1]],
         )
 
@@ -1632,51 +1655,55 @@
         for task in (*first, onward_o, second_m[0]):
             task.start()
         places.load()
+        places.wait()
+        tab(1)
         first[0].cores()
         first[1].cores()
         settle.start(done[1], 1, (1, 2))
         input_grad.start()
-        places.wait()
-        tab(1)
+        tab(0)
+        little.pack(layers, tabs_ref)
+        little.start()
         onward_o.close()
         second_m[1].start()
         second_m[0].close()
         share_m[0].start()
         first[0].turn()
+        little.second()
         first[1].turn()
-        tab(0)
-        little.pack(layers, tabs_ref)
-        little.start()
         share_a1.start()
         settle.pass_on(done[1], 1, (1, 2))
         first[0].close()
         second[0].start()
-        little.second()
         first[1].close()
         second[1].start()
+        little.third()
         second_m[1].close()
         share_m[1].start()
-        share_m[0].end()
-        share_a1.end()
+        input_grad.wait()
+        input_grad.weave(0, 2)
+        for task in (share_m[0], share_a1):
+            task.end()
+            task.flush()
         settle.start(done[1], 1, (0,))
         settle.start(done[0], 0, (1,))
-        little.third()
-        input_grad.wait()
-        input_grad.weave(0, 2)
         for n in range(2):
             second[n].close()
             share[n].start()
+        input_grad.weave(2, 4)
+        little.fourth()
         settle.pass_on(done[1], 1, (0,))
         settle.pass_on(done[0], 0, (1,))
         share_m[1].end()
+        share_m[1].flush()
         settle.start(done[0], 0, (2,))
+        settle.pass_on(done[0], 0, (2,))
+        for task in share:
+            task.end()
+        for task in share:
+            task.flush()
+        settle.straight(done[0][0], 0, 0)
         little.end()
-        input_grad.weave(2, 4)
-        settle.pass_on(done[0], 0, (2,))
-        for n in range(2):
-            share[n].end()
-        settle.start(done[0], 0, (0,))
-        settle.pass_on(done[0], 0, (0,))
         input_grad.end()
         settle.end(done)
 
@@ -1828,7 +1855,7 @@
 
 
 def four_by_four(images, cotangent, counts, rel_index, small_in, big_in):
-    own_a, lines, index = prepare(rel_index.T, big_in[0][0], big_in[1][0], *[member[0] if member.ndim == 3 else member for member in small_in])
+    own_a, lines, index = prepare(rel_index, big_in[0][0], big_in[1][0], *[member[0] if member.ndim == 3 else member for member in small_in])
     own = (own_a, big_in[2][0], big_in[3][0])
     other, table, pieces_a0, near_h0, near_o0, bias, x0 = gather_start(own, lines, index, jnp.swapaxes(images, 1, 2))
     pick_cot = Own(jnp.swapaxes(cotangent, 1, 2), plan=((2, "pick"),))
@@ -1872,9 +1899,9 @@
     def last_tasks(big_m, given):
         onward = ReduceOnward(given[1], plan=((1, "close"),))
         second_h = ReduceSecond(given[2][0], plan=((1, "close"),))
-        second_o = ReduceSecond(given[3][0], deferred=True, plan=((1, "start"), (LATE, "close")))
+        second_o = ReduceSecond(given[3][0], deferred=True, plan=((1, "start"), (3, "close")))
         second_a = ReduceSecond(source=onward, deferred=True, plan=((2, "start"),))
-        shares = [Share(source=second_h, plan=((1, "start"),)), Share(source=second_o, plan=((LATE, "start"),))]
+        shares = [Share(source=second_h, plan=((1, "start"),)), Share(source=second_o, plan=((3, "start"),))]
         return [
             ReduceFirst(big_m[0], plan=((0, "cores"), (LATE, "turn"))), ReduceTurn(big_m[1], plan=((1, "cores"),)), onward, second_h,
             *shares[:1], second_o, second_a, *shares[1:], Weave([out0, out1], out_came, plan=((3, "all"),)),

time: 240 us -> 236 us (0.983)
  Pallas kernels: 235 us -> 231 us
    pallas_call x10, Pallas kernels: 229 us -> 225 us  [carried_call(): pl.pallas_call(whole_body, grid_spec=pltpu.PrefetchScalarGridSpec(num_sca...]
where the time goes in v4:
time: 236 us; the launch traced here: 235 us
  Pallas kernels  231 us (98%)
  local copies, waits for them, and re-layouts  3.14 us (1%)
    pallas_call x10, Pallas kernels, carried_call(): pl.pallas_call(whole_body, grid_spec=pltpu.PrefetchScalarGridSpec(num_sca...  225 us
    pallas_call x2, Pallas kernels, plain_call(): pl.pallas_call(body, grid=grid, out_shape=out_shape, in_specs=in_specs or...  5.9 us

profile of v4, /device:TPU:0, one launch (start us, length us, event | category | flops | bytes accessed | tf_op | source)
XLA Modules:
  0.0 235.2 jit_solution(17158643378108251616)
XLA Ops:
  0.7 2.3 prepare.1
  3.0 29.4 %gather_start.1 = (bf16[512,512]{1,0:T(8,128)(2,1)}, bf16[512,512]{1,0:T(8,128)(2,1)}, bf16[512,512]{1,0:T(8,128)(2,1)}, bf16[4,2,32,128]{3,2,1,0:T(8,128)(2,1)}...) custom-call(bf16[512,512]{1,0:T(8,128)(2,1)} %get-tuple-element.157., ...), custom_call_target="tpu_custom_call" | custom-call | flops 16777216 | bytes 8388608 | tf_op jit(solution)/shard_map/gather_start/pallas_call | solution.py:671
  32.4 23.0 %attn_fwd.2 = (bf16[4,256,512]{2,1,0:T(8,128)(2,1)}, bf16[4,256,1536]{2,1,0:T(8,128)(2,1)}, bf16[4,4,4,64,256]{4,3,2,1,0:T(8,128)(2,1)}, bf16[4,208,512]{2,1,0:T...) custom-call(bf16[4,208,512]{2,1,0:T(8,128)(2,1)} %get-tuple-element., ...), custom_call_target="tpu_custom_call" | custom-call | flops 2726297600 | bytes 8388608 | tf_op jit(solution)/shard_map/attn_fwd/pallas_call | solution.py:671
  55.4 15.9 %mlp_fwd.2 = (bf16[832,512]{1,0:T(8,128)(2,1)}, bf16[4,832,512]{2,1,0:T(8,128)(2,1)}, bf16[4,832,512]{2,1,0:T(8,128)(2,1)}, bf16[4,208,512]{2,1,0:T(8,128)(2,1)}...) custom-call(s32[1,4]{1,0:T(1,128)} %bitcast.33, ...), custom_call_target="tpu_custom_call" | custom-call | flops 3489660928 | bytes 12582912 | tf_op jit(solution)/shard_map/mlp_fwd/pallas_call | solution.py:671
  71.3 21.7 %attn_fwd.3 = (bf16[4,256,512]{2,1,0:T(8,128)(2,1)}, bf16[4,256,1536]{2,1,0:T(8,128)(2,1)}, bf16[4,4,4,64,256]{4,3,2,1,0:T(8,128)(2,1)}, bf16[4,208,512]{2,1,0:T...) custom-call(bf16[4,208,512]{2,1,0:T(8,128)(2,1)} %get-tuple-element., ...), custom_call_target="tpu_custom_call" | custom-call | flops 2726297600 | bytes 8388608 | tf_op jit(solution)/shard_map/attn_fwd/pallas_call | solution.py:671
  93.0 10.9 %mlp_fwd.3 = (bf16[832,512]{1,0:T(8,128)(2,1)}, bf16[4,832,512]{2,1,0:T(8,128)(2,1)}, bf16[4,832,512]{2,1,0:T(8,128)(2,1)}, bf16[4,208,512]{2,1,0:T(8,128)(2,1)}...) custom-call(s32[1,4]{1,0:T(1,128)} %bitcast.34, f32[832,512]{1,0:T(8,128)} %bitcast.39, ...), custom_call_target="tpu_custom_call" | custom-call | flops 3489660928 | bytes 12582912 | tf_op jit(solution)/shard_map/mlp_fwd/pallas_call | solution.py:671
  103.9 17.1 %mlp_bwd.2 = (bf16[4,4,64,512]{3,2,1,0:T(8,128)(2,1)}, bf16[4,4,64,512]{3,2,1,0:T(8,128)(2,1)}, bf16[4,4,64,512]{3,2,1,0:T(8,128)(2,1)}, bf16[4,4,64,512]{3,2,1,...) custom-call(s32[1,4]{1,0:T(1,128)} %bitcast.35, ...), custom_call_target="tpu_custom_call" | custom-call | flops 6979321856 | bytes 16777216 | tf_op jit(solution)/shard_map/mlp_bwd/pallas_call | solution.py:671
  121.0 23.2 %attn_bwd.2 = (bf16[4,208,512]{2,1,0:T(8,128)(2,1)}, bf16[4,196,512]{2,1,0:T(8,128)(2,1)}, bf16[4,4,64,512]{3,2,1,0:T(8,128)(2,1)}, bf16[4,4,64,512]{3,2,1,0:T(8...) custom-call(bf16[4,208,512]{2,1,0:T(8,128)(2,1)} %get-tuple-element., ...), custom_call_target="tpu_custom_call" | custom-call | flops 5452595200 | bytes 12582912 | tf_op jit(solution)/shard_map/attn_bwd/pallas_call | solution.py:671
  144.2 19.8 %mlp_bwd.3 = (bf16[4,4,64,512]{3,2,1,0:T(8,128)(2,1)}, bf16[4,4,64,512]{3,2,1,0:T(8,128)(2,1)}, bf16[4,4,64,512]{3,2,1,0:T(8,128)(2,1)}, bf16[4,4,64,512]{3,2,1,...) custom-call(s32[1,4]{1,0:T(1,128)} %bitcast.36, ...), custom_call_target="tpu_custom_call" | custom-call | flops 6979321856 | bytes 16777216 | tf_op jit(solution)/shard_map/mlp_bwd/pallas_call | solution.py:671
  164.0 31.1 %attn_bwd.3 = (bf16[4,208,512]{2,1,0:T(8,128)(2,1)}, bf16[4,196,512]{2,1,0:T(8,128)(2,1)}, bf16[4,4,64,512]{3,2,1,0:T(8,128)(2,1)}, bf16[4,4,64,512]{3,2,1,0:T(8...) custom-call(bf16[4,208,512]{2,1,0:T(8,128)(2,1)} %get-tuple-element., ...), custom_call_target="tpu_custom_call" | custom-call | flops 5452595200 | bytes 12582912 | tf_op jit(solution)/shard_map/attn_bwd/pallas_call | solution.py:671
  195.1 33.4 %reduce_end.1 = (bf16[4,32,512]{2,1,0:T(8,128)(2,1)}, bf16[4,32,512]{2,1,0:T(8,128)(2,1)}, bf16[32,512]{1,0:T(8,128)(2,1)}, bf16[32,512]{1,0:T(8,128)(2,1)}, bf1...) custom-call(f32[4,4,128]{2,1,0:T(4,128)} %get-tuple-element.263.refs, ...), custom_call_target="tpu_custom_call" | custom-call | flops 16777216 | bytes 8388608 | tf_op jit(solution)/shard_map/reduce_end/pallas_call | solution.py:671
  228.5 0.0 copy-start
  228.5 3.6 %finish.1 = (f32[1,512,384]{2,1,0:T(8,128)}, f32[1,128,512]{2,1,0:T(8,128)}, f32[1,512,512]{2,1,0:T(8,128)}, f32[1,512,512]{2,1,0:T(8,128)}, f32[1,128]{1,0:T(1,...) custom-call(bf16[3,512,512]{2,1,0:T(8,128)(2,1)} %get-tuple-element., ...), custom_call_target="tpu_custom_call" | custom-call | flops 4194304 | bytes 4194304 | tf_op jit(solution)/shard_map/finish/pallas_call | solution.py:1256
  232.1 0.0 copy-start.1
  232.1 0.0 copy-done
  232.1 1.2 copy.34
  233.3 0.8 copy-done.1
  234.1 1.2 copy.35
Async XLA Ops:
  228.5 3.6 %copy-start = (bf16[4,196,2,512]{3,2,1,0:T(2,128)(2,1)S(1)}, bf16[4,196,2,512]{3,2,1,0:T(2,128)(2,1)}, u32[]{:S(2)}) copy-start(bf16[4,196,2,512]{3,2,1,0:T(2,128)(2,1)} %get-tuple-element.262) | copy-start | bytes 4816900
  232.1 2.0 copy-start.1

commit v5 on v4

--- a/solution.py
+++ b/solution.py
@@ -1626,7 +1626,7 @@
     out_ref[...] = lax.fori_loop(0, WP // 2, add, jnp.zeros((H, 2 * GL), F32))
 
 
-def reduce_end(attention0, totals_h0, turned_o0, piece_a1, shared1, grads_in, small, index):
+def reduce_end(attention0, totals_h0, turned_o0, pieces1, shared_h1, grads_in, small, index):
     halves = ((0, 32), (32, 32))
     first = [ReduceFirst(attention0, rows=rows) for rows in halves]
     second = [ReduceSecond(size=32) for _ in halves]
@@ -1634,7 +1634,7 @@
     share.append(Share(rows=halves[1], target=share[0]))
     onward_o = ReduceOnward(turned_o0)
     second_m, share_m = [ReduceSecond(totals_h0), ReduceSecond()], [Share(), Share()]
-    share_a1, done_m1 = Share(piece_a1), Part(shared1)
+    share_a1, share_o1, done_h1 = Share(pieces1[0]), Share(pieces1[1]), Part([shared_h1])
     settle, little, places = Settle(), Little(24), Stored(index)
     input_grad = Weave(grads_in)
 
@@ -1645,7 +1645,7 @@
         second_m[1].ins = [onward_o.kept[0]]
         done = (
             [share[0].whole(), share_m[0].outs[0], share_m[1].outs[0]],
-            [share_a1.outs[0], done_m1.ins[0], done_m1.ins[1]],
+            [share_a1.outs[0], done_h1.ins[0], share_o1.outs[0]],
         )
 
         def tab(layer):
@@ -1659,7 +1659,8 @@
         tab(1)
         first[0].cores()
         first[1].cores()
-        settle.start(done[1], 1, (1, 2))
+        share_o1.start()
+        settle.start(done[1], 1, (1,))
         input_grad.start()
         tab(0)
         little.pack(layers, tabs_ref)
@@ -1672,7 +1673,7 @@
         little.second()
         first[1].turn()
         share_a1.start()
-        settle.pass_on(done[1], 1, (1, 2))
+        settle.pass_on(done[1], 1, (1,))
         first[0].close()
         second[0].start()
         first[1].close()
@@ -1682,17 +1683,17 @@
         share_m[1].start()
         input_grad.wait()
         input_grad.weave(0, 2)
-        for task in (share_m[0], share_a1):
+        for task in (share_m[0], share_a1, share_o1):
             task.end()
             task.flush()
-        settle.start(done[1], 1, (0,))
+        settle.start(done[1], 1, (0, 2))
         settle.start(done[0], 0, (1,))
         for n in range(2):
             second[n].close()
             share[n].start()
         input_grad.weave(2, 4)
         little.fourth()
-        settle.pass_on(done[1], 1, (0,))
+        settle.pass_on(done[1], 1, (0, 2))
         settle.pass_on(done[0], 0, (1,))
         share_m[1].end()
         share_m[1].flush()
@@ -1708,7 +1709,7 @@
         settle.end(done)
 
     parts = [
-        *first, *second, *share, onward_o, *second_m, *share_m, share_a1, done_m1, settle, little, input_grad, places
+        *first, *second, *share, onward_o, *second_m, *share_m, share_a1, share_o1, done_h1, settle, little, input_grad, places
     ]
     _, given = carried_call(
         body, parts, 7, grid=(), in_specs=[pl.BlockSpec(memory_space=pltpu.VMEM)] * 10, inputs=small, out_specs=[], out_shape=[],
@@ -1899,12 +1900,12 @@
     def last_tasks(big_m, given):
         onward = ReduceOnward(given[1], plan=((1, "close"),))
         second_h = ReduceSecond(given[2][0], plan=((1, "close"),))
-        second_o = ReduceSecond(given[3][0], deferred=True, plan=((1, "start"), (3, "close")))
+        second_o = ReduceSecond(given[3][0], deferred=True, plan=((1, "start"),))
         second_a = ReduceSecond(source=onward, deferred=True, plan=((2, "start"),))
-        shares = [Share(source=second_h, plan=((1, "start"),)), Share(source=second_o, plan=((3, "start"),))]
+        share_h = Share(source=second_h, plan=((1, "start"),))
         return [
             ReduceFirst(big_m[0], plan=((0, "cores"), (LATE, "turn"))), ReduceTurn(big_m[1], plan=((1, "cores"),)), onward, second_h,
-            *shares[:1], second_o, second_a, *shares[1:], Weave([out0, out1], out_came, plan=((3, "all"),)),
+            share_h, second_o, second_a, Weave([out0, out1], out_came, plan=((3, "all"),)),
         ]
 
     _, gin0, big0, small0, given, more = layer_backward(
@@ -1915,10 +1916,10 @@
         ),
         (6, 8),
     )
-    totals_h0, turned_o0, piece_a1, shared1 = more[1][0], more[2], more[7][0], (more[5][0], more[8][0])
-    block_out = more[9][0]
+    totals_h0, turned_o0, pieces1, shared_h1 = more[1][0], more[2], (more[7][0], more[6][0]), more[5][0]
+    block_out = more[8][0]
     matrices, lines, input_grad = reduce_end(
-        big0[0], totals_h0, turned_o0, piece_a1, shared1, [gin0, gin1], [*small0, *small1], index
+        big0[0], totals_h0, turned_o0, pieces1, shared_h1, [gin0, gin1], [*small0, *small1], index
     )
     gqkv, gproj, ghw, gow, *outs = finish(matrices, lines)
     return jnp.swapaxes(block_out, 1, 2)[None], jnp.swapaxes(input_grad, 1, 2)[None], (gqkv, gproj, ghw, gow), outs

time: 236 us -> 238 us (level)
  Pallas kernels: 231 us -> 234 us
    pallas_call x10, Pallas kernels: 225 us -> 228 us  [carried_call(): pl.pallas_call(whole_body, grid_spec=pltpu.PrefetchScalarGridSpec(num_sca...]
where the time goes in v5:
time: 238 us
  Pallas kernels  234 us (98%)
  local copies, waits for them, and re-layouts  3.14 us (1%)
    pallas_call x10, Pallas kernels, carried_call(): pl.pallas_call(whole_body, grid_spec=pltpu.PrefetchScalarGridSpec(num_sca...  228 us
    pallas_call x2, Pallas kernels, plain_call(): pl.pallas_call(body, grid=grid, out_shape=out_shape, in_specs=in_specs or...  5.9 us

profile of v5, /device:TPU:0, one launch (start us, length us, event | category | flops | bytes accessed | tf_op | source)
XLA Modules:
  0.0 237.8 jit_solution(279618825441386217)
XLA Ops:
  0.7 2.3 prepare.1
  3.0 29.4 %gather_start.1 = (bf16[512,512]{1,0:T(8,128)(2,1)}, bf16[512,512]{1,0:T(8,128)(2,1)}, bf16[512,512]{1,0:T(8,128)(2,1)}, bf16[4,2,32,128]{3,2,1,0:T(8,128)(2,1)}...) custom-call(bf16[512,512]{1,0:T(8,128)(2,1)} %get-tuple-element.157., ...), custom_call_target="tpu_custom_call" | custom-call | flops 16777216 | bytes 8388608 | tf_op jit(solution)/shard_map/gather_start/pallas_call | solution.py:671
  32.4 23.0 %attn_fwd.2 = (bf16[4,256,512]{2,1,0:T(8,128)(2,1)}, bf16[4,256,1536]{2,1,0:T(8,128)(2,1)}, bf16[4,4,4,64,256]{4,3,2,1,0:T(8,128)(2,1)}, bf16[4,208,512]{2,1,0:T...) custom-call(bf16[4,208,512]{2,1,0:T(8,128)(2,1)} %get-tuple-element., ...), custom_call_target="tpu_custom_call" | custom-call | flops 2726297600 | bytes 8388608 | tf_op jit(solution)/shard_map/attn_fwd/pallas_call | solution.py:671
  55.4 15.9 %mlp_fwd.2 = (bf16[832,512]{1,0:T(8,128)(2,1)}, bf16[4,832,512]{2,1,0:T(8,128)(2,1)}, bf16[4,832,512]{2,1,0:T(8,128)(2,1)}, bf16[4,208,512]{2,1,0:T(8,128)(2,1)}...) custom-call(s32[1,4]{1,0:T(1,128)} %bitcast.33, ...), custom_call_target="tpu_custom_call" | custom-call | flops 3489660928 | bytes 12582912 | tf_op jit(solution)/shard_map/mlp_fwd/pallas_call | solution.py:671
  71.3 21.7 %attn_fwd.3 = (bf16[4,256,512]{2,1,0:T(8,128)(2,1)}, bf16[4,256,1536]{2,1,0:T(8,128)(2,1)}, bf16[4,4,4,64,256]{4,3,2,1,0:T(8,128)(2,1)}, bf16[4,208,512]{2,1,0:T...) custom-call(bf16[4,208,512]{2,1,0:T(8,128)(2,1)} %get-tuple-element., ...), custom_call_target="tpu_custom_call" | custom-call | flops 2726297600 | bytes 8388608 | tf_op jit(solution)/shard_map/attn_fwd/pallas_call | solution.py:671
  93.0 10.9 %mlp_fwd.3 = (bf16[832,512]{1,0:T(8,128)(2,1)}, bf16[4,832,512]{2,1,0:T(8,128)(2,1)}, bf16[4,832,512]{2,1,0:T(8,128)(2,1)}, bf16[4,208,512]{2,1,0:T(8,128)(2,1)}...) custom-call(s32[1,4]{1,0:T(1,128)} %bitcast.34, f32[832,512]{1,0:T(8,128)} %bitcast.39, ...), custom_call_target="tpu_custom_call" | custom-call | flops 3489660928 | bytes 12582912 | tf_op jit(solution)/shard_map/mlp_fwd/pallas_call | solution.py:671
  103.9 17.1 %mlp_bwd.2 = (bf16[4,4,64,512]{3,2,1,0:T(8,128)(2,1)}, bf16[4,4,64,512]{3,2,1,0:T(8,128)(2,1)}, bf16[4,4,64,512]{3,2,1,0:T(8,128)(2,1)}, bf16[4,4,64,512]{3,2,1,...) custom-call(s32[1,4]{1,0:T(1,128)} %bitcast.35, ...), custom_call_target="tpu_custom_call" | custom-call | flops 6979321856 | bytes 16777216 | tf_op jit(solution)/shard_map/mlp_bwd/pallas_call | solution.py:671
  121.0 23.2 %attn_bwd.2 = (bf16[4,208,512]{2,1,0:T(8,128)(2,1)}, bf16[4,196,512]{2,1,0:T(8,128)(2,1)}, bf16[4,4,64,512]{3,2,1,0:T(8,128)(2,1)}, bf16[4,4,64,512]{3,2,1,0:T(8...) custom-call(bf16[4,208,512]{2,1,0:T(8,128)(2,1)} %get-tuple-element., ...), custom_call_target="tpu_custom_call" | custom-call | flops 5452595200 | bytes 12582912 | tf_op jit(solution)/shard_map/attn_bwd/pallas_call | solution.py:671
  144.2 19.8 %mlp_bwd.3 = (bf16[4,4,64,512]{3,2,1,0:T(8,128)(2,1)}, bf16[4,4,64,512]{3,2,1,0:T(8,128)(2,1)}, bf16[4,4,64,512]{3,2,1,0:T(8,128)(2,1)}, bf16[4,4,64,512]{3,2,1,...) custom-call(s32[1,4]{1,0:T(1,128)} %bitcast.36, ...), custom_call_target="tpu_custom_call" | custom-call | flops 6979321856 | bytes 16777216 | tf_op jit(solution)/shard_map/mlp_bwd/pallas_call | solution.py:671
  164.0 29.2 %attn_bwd.3 = (bf16[4,208,512]{2,1,0:T(8,128)(2,1)}, bf16[4,196,512]{2,1,0:T(8,128)(2,1)}, bf16[4,4,64,512]{3,2,1,0:T(8,128)(2,1)}, bf16[4,4,64,512]{3,2,1,0:T(8...) custom-call(bf16[4,208,512]{2,1,0:T(8,128)(2,1)} %get-tuple-element., ...), custom_call_target="tpu_custom_call" | custom-call | flops 5452595200 | bytes 12582912 | tf_op jit(solution)/shard_map/attn_bwd/pallas_call | solution.py:671
  193.3 37.8 %reduce_end.1 = (bf16[4,32,512]{2,1,0:T(8,128)(2,1)}, bf16[4,32,512]{2,1,0:T(8,128)(2,1)}, bf16[32,512]{1,0:T(8,128)(2,1)}, bf16[32,512]{1,0:T(8,128)(2,1)}, bf1...) custom-call(f32[4,4,128]{2,1,0:T(4,128)} %get-tuple-element.263.refs, ...), custom_call_target="tpu_custom_call" | custom-call | flops 16777216 | bytes 8388608 | tf_op jit(solution)/shard_map/reduce_end/pallas_call | solution.py:671
  231.1 0.0 copy-start
  231.1 3.6 %finish.1 = (f32[1,512,384]{2,1,0:T(8,128)}, f32[1,128,512]{2,1,0:T(8,128)}, f32[1,512,512]{2,1,0:T(8,128)}, f32[1,512,512]{2,1,0:T(8,128)}, f32[1,128]{1,0:T(1,...) custom-call(bf16[3,512,512]{2,1,0:T(8,128)(2,1)} %get-tuple-element., ...), custom_call_target="tpu_custom_call" | custom-call | flops 4194304 | bytes 4194304 | tf_op jit(solution)/shard_map/finish/pallas_call | solution.py:1256
  234.6 0.0 copy-start.1
  234.6 0.0 copy-done
  234.7 1.2 copy.34
  235.8 0.8 copy-done.1
  236.6 1.2 copy.35
Async XLA Ops:
  231.1 3.6 %copy-start = (bf16[4,196,2,512]{3,2,1,0:T(2,128)(2,1)S(1)}, bf16[4,196,2,512]{3,2,1,0:T(2,128)(2,1)}, u32[]{:S(2)}) copy-start(bf16[4,196,2,512]{3,2,1,0:T(2,128)(2,1)} %get-tuple-element.262) | copy-start | bytes 4816900
  234.6 2.0 copy-start.1
